TPU v7x, 32 devices: a whole 2x2x4 slice. The times are simulated.
32 devices in a mesh: gx: 4 (over z), gy: 2 (over x), gz: 4 (over y, core).
Axes of the slice: x: 2, y: 2, z: 4, core: 2. Of those that a mesh axis runs over, the one named last changes fastest.
Arguments:
- start_potential: float32 [64, 256, 512], P('gx', 'gy', 'gz'), may hold values from -0.9 to 2.1
- permittivity: float32 [64, 256, 512], P('gx', 'gy', 'gz'), may hold values from 1 to 8
- screening: float32 [64, 256, 512], P('gx', 'gy', 'gz'), may hold values from 0.05 to 2
- source: float32 [64, 256, 512], P('gx', 'gy', 'gz'), may hold values from -12 to 12
Outputs:
- potential: float32 [64, 256, 512], P('gx', 'gy', 'gz')
- residual_rms: float32 [3], replicated
- induced_charge: float32 [3], replicated
All inputs are finite; a program needn't handle non-finite values.
Results may differ from a plain program's by a relative error of at most 0.0003.
Values sent between devices are 32-bit elements; how exact they have to be, the bound alone decides.
No kernel may reach another device: no remote copies, remote signals or barrier semaphores. Data moves between devices by JAX's collectives and lax.ppermute only.
A program may use at most 64 MiB of HBM per device.

v0:
```python
import jax
import jax.numpy as jnp
from jax import lax
from jax.sharding import PartitionSpec as P

ITERS = 3


def padded_2(array, sides, width):
    for axis, dim in sides:
        size, length = (lax.axis_size(axis), array.shape[dim])
        up = [(i, (i + 1) % size) for i in range(size - 1)]
        down = [(j, i) for i, j in up]
        last = lax.slice_in_dim(array, length - width, length, axis=dim)
        initial = lax.slice_in_dim(array, 0, width, axis=dim)
        before = lax.ppermute(last, axis, up)
        after = lax.ppermute(initial, axis, down)
        array = jnp.concatenate([before, array, after], axis=dim)
    return array


def harmonic(left, right):
    total = left + right
    return 2.0 * left * right / jnp.where(total > 0, total, 1.0)


def neighbours(block):
    return [
        block[2:, 1:-1, 1:-1],
        block[:-2, 1:-1, 1:-1],
        block[1:-1, 2:, 1:-1],
        block[1:-1, :-2, 1:-1],
        block[1:-1, 1:-1, 2:],
        block[1:-1, 1:-1, :-2],
    ]


def relax(padded, weights_pad, screening, source):
    center = padded[1:-1, 1:-1, 1:-1]
    middle = weights_pad[1:-1, 1:-1, 1:-1]
    flux = jnp.zeros_like(center)
    diagonal = jnp.zeros_like(center)
    for near, other in zip(neighbours(padded), neighbours(weights_pad)):
        weight = harmonic(middle, other)
        flux = flux + weight * (center - near)
        diagonal = diagonal + weight
    induced = screening * jnp.sinh(center)
    residual = source - flux - induced
    diagonal = diagonal + screening * jnp.cosh(center)
    return (center, residual, jnp.where(diagonal > 0, diagonal, 1.0), induced)


def statistics(own_residual, own_induced, cells, charge_terms):
    squares = jnp.sum(own_residual * own_residual)
    square_sum, charge_sum = lax.psum((squares, jnp.sum(own_induced)), ("gx", "gy", "gz"))
    charge_terms.append(charge_sum / cells)
    return jnp.sqrt(square_sum / cells + 1e-06)


def body(start_potential, permittivity, screening, source):
    shape = start_potential.shape
    cells = (
        shape[0]
        * shape[1]
        * shape[2]
        * lax.axis_size("gx")
        * lax.axis_size("gy")
        * lax.axis_size("gz")
    )
    norms = []
    charge_terms = []
    weights_pad = padded_2(permittivity, (("gx", 0), ("gy", 1), ("gz", 2)), 1)
    potential = start_potential
    for iteration in range(ITERS):
        padded = padded_2(potential, (("gx", 0), ("gy", 1), ("gz", 2)), 1)
        center, residual, diagonal, induced = relax(padded, weights_pad, screening, source)
        rms = statistics(residual, induced, cells, charge_terms)
        norms.append(rms)
        potential = center + 1.0 / (1.0 + rms) * residual / diagonal
    charges = jnp.stack(charge_terms)
    return (potential, jnp.stack(norms), charges)


def solution(mesh):
    placed = (P("gx", "gy", "gz"), P("gx", "gy", "gz"), P("gx", "gy", "gz"), P("gx", "gy", "gz"))
    return jax.shard_map(
        body, mesh=mesh, in_specs=placed, out_specs=(P("gx", "gy", "gz"), P(), P()), check_vma=False
    )
```

profile of v0, /device:TPU:0, one launch (start us, length us, event | category | flops | bytes accessed | tf_op | source)
XLA Modules:
  0.0 297.7 jit_solution(15585116569991222834)
XLA Ops:
  2.8 5.6 %collective-permute-start.2 = (f32[1,128,128]{2,0,1:T(1,128)S(1)}, f32[1,128,128]{2,0,1:T(1,128)S(1)}, u32[]{:S(2)}, u32[]{:S(2)}) collective-permute-start(f32[1,128,128]{2,0,1:T(1,128)S(1)} %bitcast.12), channel_id=1, source_target_pairs={{0,8},{8,16},{16,24},{1,9},{9,17},{17,25},{2,10},{10,18},{18,26},{... | collective-permute-start | bytes 196616 | tf_op jit(solution)/shard_map/ppermute | solution.py:16
  10.6 4.7 %collective-permute-start.3 = (f32[1,128,128]{2,0,1:T(1,128)S(1)}, f32[1,128,128]{2,0,1:T(1,128)S(1)}, u32[]{:S(2)}, u32[]{:S(2)}) collective-permute-start(f32[1,128,128]{2,0,1:T(1,128)S(1)} %bitcast.10), channel_id=1, source_target_pairs={{0,8},{8,16},{16,24},{1,9},{9,17},{17,25},{2,10},{10,18},{18,26},{... | collective-permute-start | bytes 196616 | tf_op jit(solution)/shard_map/ppermute | solution.py:16
  15.3 4.7 %fusion.88 = (f32[]{:T(128)}, f32[16,128,128]{2,0,1:T(8,128)}, f32[16,128,128]{2,0,1:T(8,128)S(1)}) fusion(f32[16,128,128]{2,1,0:T(8,128)} %param.4, f32[16,128,128]{2,1,0:T(8,128)} %param.6), kind=kLoop, calls=%fused_computation.203 | loop fusion | flops 3145727 | bytes 4194308 | tf_op jit(solution)/shard_map/reduce_sum | solution.py:55
  22.0 4.5 %collective-permute-start.6 = (f32[18,1,128]{2,0,1:T(8,128)S(1)}, f32[18,1,128]{2,0,1:T(8,128)S(1)}, u32[]{:S(2)}, u32[]{:S(2)}) collective-permute-start(f32[18,1,128]{2,0,1:T(8,128)S(1)} %get-tuple-element.44), channel_id=1, source_target_pairs={{0,4},{1,5},{2,6},{3,7},{8,12},{9,13},{10,14},{11,15},{16,20},{17,... | collective-permute-start | bytes 27656 | tf_op jit(solution)/shard_map/ppermute | solution.py:16
  31.6 2.4 copy.168
  34.0 2.4 copy.162
  37.6 3.0 %collective-permute-start.10 = (f32[18,130,1]{1,0,2:T(8,128)S(1)}, f32[18,130,1]{1,0,2:T(8,128)S(1)}, u32[]{:S(2)}, u32[]{:S(2)}) collective-permute-start(f32[18,130,1]{1,0,2:T(8,128)S(1)} %copy.168), channel_id=1, source_target_pairs={{0,1},{1,2},{2,3},{4,5},{5,6},{6,7},{8,9},{9,10},{10,11},{12,13},{... | collective-permute-start | bytes 28088 | tf_op jit(solution)/shard_map/ppermute | solution.py:16
  43.1 2.4 copy.165
  46.8 2.4 copy.171
  49.1 4.1 %collective-permute-start.11 = (f32[18,130,1]{1,0,2:T(8,128)S(1)}, f32[18,130,1]{1,0,2:T(8,128)S(1)}, u32[]{:S(2)}, u32[]{:S(2)}) collective-permute-start(f32[18,130,1]{1,0,2:T(8,128)S(1)} %copy.171), channel_id=1, source_target_pairs={{0,1},{1,2},{2,3},{4,5},{5,6},{6,7},{8,9},{9,10},{10,11},{12,13},{... | collective-permute-start | bytes 28088 | tf_op jit(solution)/shard_map/ppermute | solution.py:16
  61.7 9.7 %multiply_reduce_fusion.2 = (f32[]{:T(128)}, f32[16,128,128]{2,0,1:T(8,128)}, f32[16,128,128]{2,0,1:T(8,128)}, f32[16,128,128]{2,0,1:T(8,128)}) fusion(f32[16,128,128]{2,0,1:T(8,128)} %get-tuple-element.19, f32[16,128,128]{2,0,1:T(8,128)S(1)} %get-tuple-element.55, f32[18,1,128]{2,0,1:T(8,128)S(1)} %collective-permute-done.5, ...), kind=kLoop, calls=%fused_computation.183 | loop fusion | flops 23068672 | bytes 7676484 | tf_op jit(solution)/shard_map/reduce_sum | solution.py:54
  71.4 42.1 %psum.42 = f32[]{:T(128)} all-reduce(f32[]{:T(128)} %get-tuple-element.27), channel_id=1, replica_groups=mesh['gx'=4,'gy'=2,'gz'=4] {'gx','gy','gz'}, use_global_device_ids=true, to_apply=%region_1.2 | all-reduce | flops 1 | bytes 8 | tf_op jit(solution)/shard_map/psum | solution.py:55
  114.3 5.9 %fusion.16 = (f32[16,128,128]{2,0,1:T(8,128)S(1)}, f32[16,128,128]{2,0,1:T(8,128)}) fusion(f32[16,128,128]{2,0,1:T(8,128)} %get-tuple-element.28, f32[16,128,128]{2,1,0:T(8,128)S(1)} %copy-done, f32[]{:T(128)S(6)} %div.73, f32[16,128,128]{2,1,0:T(8,128)} %param.4, f32[16,128,128]{2,0,1:T(8,128)} %get-tuple-element.30, f32[16,128,128]{2,0,1:T(8,128)} %get-tuple-element.29, ...), kind=kLoop, calls=%fused_computation.32 | loop fusion | flops 11534336 | bytes 8538116 | tf_op jit(solution)/shard_map/add | solution.py:79
  124.3 4.3 %collective-permute-done.12 = f32[1,128,128]{2,0,1:T(1,128)S(1)} collective-permute-done((f32[1,128,128]{2,0,1:T(1,128)S(1)}, f32[1,128,128]{2,0,1:T(1,128)S(1)}, u32[]{:S(2)}, u32[]{:S(2)}) %collective-permute-start.12) | collective-permute-done | bytes 65568 | tf_op jit(solution)/shard_map/ppermute | solution.py:17
  128.6 4.2 %collective-permute-start.15 = (f32[18,1,128]{2,0,1:T(8,128)S(1)}, f32[18,1,128]{2,0,1:T(8,128)S(1)}, u32[]{:S(2)}, u32[]{:S(2)}) collective-permute-start(f32[18,1,128]{2,0,1:T(8,128)S(1)} %get-tuple-element.41), channel_id=1, source_target_pairs={{0,4},{1,5},{2,6},{3,7},{8,12},{9,13},{10,14},{11,15},{16,20},{17,... | collective-permute-start | bytes 27656 | tf_op jit(solution)/shard_map/ppermute | solution.py:16
  134.2 4.2 %collective-permute-done.14 = f32[18,1,128]{2,0,1:T(8,128)S(1)} collective-permute-done((f32[18,1,128]{2,0,1:T(8,128)S(1)}, f32[18,1,128]{2,0,1:T(8,128)S(1)}, u32[]{:S(2)}, u32[]{:S(2)}) %collective-permute-start.14) | collective-permute-done | bytes 9248 | tf_op jit(solution)/shard_map/ppermute | solution.py:17
  140.8 2.4 copy.182
  144.5 2.4 copy.184
  146.8 3.0 %collective-permute-start.17 = (f32[18,130,1]{1,0,2:T(8,128)S(1)}, f32[18,130,1]{1,0,2:T(8,128)S(1)}, u32[]{:S(2)}, u32[]{:S(2)}) collective-permute-start(f32[18,130,1]{1,0,2:T(8,128)S(1)} %copy.184), channel_id=1, source_target_pairs={{0,1},{1,2},{2,3},{4,5},{5,6},{6,7},{8,9},{9,10},{10,11},{12,13},{... | collective-permute-start | bytes 28088 | tf_op jit(solution)/shard_map/ppermute | solution.py:16
  154.1 8.9 %multiply_reduce_fusion.1 = (f32[]{:T(128)}, f32[16,128,128]{2,0,1:T(8,128)}) fusion(f32[16,128,128]{2,0,1:T(8,128)S(1)} %get-tuple-element.25, f32[16,128,128]{2,1,0:T(8,128)S(1)} %copy-done, f32[16,128,128]{2,0,1:T(8,128)} %get-tuple-element.30, f32[18,1,128]{2,0,1:T(8,128)S(1)} %collective-permute-done.14, ...), kind=kLoop, calls=%fused_computation.178 | loop fusion | flops 20709376 | bytes 7657764 | tf_op jit(solution)/shard_map/reduce_sum | solution.py:54
  163.0 39.6 %psum.43 = f32[]{:T(128)} all-reduce(f32[]{:T(128)} %get-tuple-element.23), channel_id=1, replica_groups=mesh['gx'=4,'gy'=2,'gz'=4] {'gx','gy','gz'}, use_global_device_ids=true, to_apply=%region_3.4 | all-reduce | flops 1 | bytes 8 | tf_op jit(solution)/shard_map/psum | solution.py:55
  203.3 4.5 %fusion.87 = (f32[]{:T(128)}, f32[]{:T(128)}, f32[16,128,128]{2,0,1:T(8,128)S(1)}) fusion(f32[16,128,128]{2,0,1:T(8,128)S(1)} %get-tuple-element.25, f32[16,128,128]{2,1,0:T(8,128)S(1)} %copy-done, f32[16,128,128]{2,0,1:T(8,128)} %get-tuple-element.26, f32[16,128,128]{2,0,1:T(8,128)} %get-tuple-element.24, f32[]{:T(128)S(6)} %div.76), kind=kLoop, calls=%fused_computation.202 | loop fusion | flops 8388606 | bytes 5242892 | tf_op jit(solution)/shard_map/reduce_sum | solution.py:55
  207.9 2.2 collective-permute-start.19
  212.0 4.3 %collective-permute-done.18 = f32[1,128,128]{2,0,1:T(1,128)S(1)} collective-permute-done((f32[1,128,128]{2,0,1:T(1,128)S(1)}, f32[1,128,128]{2,0,1:T(1,128)S(1)}, u32[]{:S(2)}, u32[]{:S(2)}) %collective-permute-start.18) | collective-permute-done | bytes 65568 | tf_op jit(solution)/shard_map/ppermute | solution.py:17
  216.3 4.2 %collective-permute-start.21 = (f32[18,1,128]{2,0,1:T(8,128)S(1)}, f32[18,1,128]{2,0,1:T(8,128)S(1)}, u32[]{:S(2)}, u32[]{:S(2)}) collective-permute-start(f32[18,1,128]{2,0,1:T(8,128)S(1)} %get-tuple-element.39), channel_id=1, source_target_pairs={{0,4},{1,5},{2,6},{3,7},{8,12},{9,13},{10,14},{11,15},{16,20},{17,... | collective-permute-start | bytes 27656 | tf_op jit(solution)/shard_map/ppermute | solution.py:16
  222.0 4.1 %collective-permute-done.20 = f32[18,1,128]{2,0,1:T(8,128)S(1)} collective-permute-done((f32[18,1,128]{2,0,1:T(8,128)S(1)}, f32[18,1,128]{2,0,1:T(8,128)S(1)}, u32[]{:S(2)}, u32[]{:S(2)}) %collective-permute-start.20) | collective-permute-done | bytes 9248 | tf_op jit(solution)/shard_map/ppermute | solution.py:17
  228.5 2.4 copy.189
  232.1 2.4 copy.191
  234.5 3.2 %collective-permute-start.23 = (f32[18,130,1]{1,0,2:T(8,128)S(1)}, f32[18,130,1]{1,0,2:T(8,128)S(1)}, u32[]{:S(2)}, u32[]{:S(2)}) collective-permute-start(f32[18,130,1]{1,0,2:T(8,128)S(1)} %copy.191), channel_id=1, source_target_pairs={{0,1},{1,2},{2,3},{4,5},{5,6},{6,7},{8,9},{9,10},{10,11},{12,13},{... | collective-permute-start | bytes 28088 | tf_op jit(solution)/shard_map/ppermute | solution.py:16
  241.9 8.9 %multiply_reduce_fusion = (f32[]{:T(128)}, f32[16,128,128]{2,0,1:T(8,128)}) fusion(f32[16,128,128]{2,0,1:T(8,128)S(1)} %copy-done.2, f32[16,128,128]{2,1,0:T(8,128)S(1)} %copy-done, f32[16,128,128]{2,0,1:T(8,128)} %get-tuple-element.30, f32[18,1,128]{2,0,1:T(8,128)S(1)} %collective-permute-done.20, f32[1,128,128]{2,0,1:T(1,128)S(1)} %collective-permute-done.18, ...), kind=kLoop, calls=%fused_computation.174 | loop fusion | flops 20709376 | bytes 7657764 | tf_op jit(solution)/shard_map/reduce_sum | solution.py:54
  250.8 39.9 %all-reduce = (f32[]{:T(128)}, f32[]{:T(128)}, f32[]{:T(128)}, f32[]{:T(128)}) all-reduce(f32[]{:T(128)} %get-tuple-element.21, f32[]{:T(128)} %get-tuple-element.13, f32[]{:T(128)} %get-tuple-element.12, f32[]{:T(128)} %get-tuple-element.18), channel_id=1, replica_groups=mesh['gx'=4,'gy'=2,'gz'=4] {'gx','gy','gz'}, use_global_device_ids=true, to_apply=%region_5.6 | all-reduce | flops 4 | bytes 32 | tf_op jit(solution)/shard_map/psum | solution.py:55
  293.3 2.5 fusion.20
  (69 shorter events, 51.4 us)
Async XLA Ops:
  1.5 19.1 %collective-permute-start = (f32[1,128,128]{2,0,1:T(1,128)S(1)}, f32[1,128,128]{2,0,1:T(1,128)S(1)}, u32[]{:S(2)}, u32[]{:S(2)}) collective-permute-start(f32[1,128,128]{2,0,1:T(1,128)S(1)} %bitcast.13), channel_id=1, source_target_pairs={{8,0},{16,8},{24,16},{9,1},{17,9},{25,17},{10,2},{18,10},{26,18},{... | collective-permute-start | bytes 196616 | tf_op jit(solution)/shard_map/ppermute | solution.py:17
  2.8 17.9 %collective-permute-start.2 = (f32[1,128,128]{2,0,1:T(1,128)S(1)}, f32[1,128,128]{2,0,1:T(1,128)S(1)}, u32[]{:S(2)}, u32[]{:S(2)}) collective-permute-start(f32[1,128,128]{2,0,1:T(1,128)S(1)} %bitcast.12), channel_id=1, source_target_pairs={{0,8},{8,16},{16,24},{1,9},{9,17},{17,25},{2,10},{10,18},{18,26},{... | collective-permute-start | bytes 196616 | tf_op jit(solution)/shard_map/ppermute | solution.py:16
  9.3 17.3 %collective-permute-start.1 = (f32[1,128,128]{2,0,1:T(1,128)S(1)}, f32[1,128,128]{2,0,1:T(1,128)S(1)}, u32[]{:S(2)}, u32[]{:S(2)}) collective-permute-start(f32[1,128,128]{2,0,1:T(1,128)S(1)} %bitcast.11), channel_id=1, source_target_pairs={{8,0},{16,8},{24,16},{9,1},{17,9},{25,17},{10,2},{18,10},{26,18},{... | collective-permute-start | bytes 196616 | tf_op jit(solution)/shard_map/ppermute | solution.py:17
  10.6 9.4 %copy-start.3 = (f32[16,128,128]{2,1,0:T(8,128)S(1)}, f32[16,128,128]{2,1,0:T(8,128)}, u32[]{:S(2)}) copy-start(f32[16,128,128]{2,1,0:T(8,128)} %param.5) | copy-start | bytes 3145732
  10.6 16.0 %collective-permute-start.3 = (f32[1,128,128]{2,0,1:T(1,128)S(1)}, f32[1,128,128]{2,0,1:T(1,128)S(1)}, u32[]{:S(2)}, u32[]{:S(2)}) collective-permute-start(f32[1,128,128]{2,0,1:T(1,128)S(1)} %bitcast.10), channel_id=1, source_target_pairs={{0,8},{8,16},{16,24},{1,9},{9,17},{17,25},{2,10},{10,18},{18,26},{... | collective-permute-start | bytes 196616 | tf_op jit(solution)/shard_map/ppermute | solution.py:16
  20.7 8.5 %collective-permute-start.4 = (f32[18,1,128]{2,0,1:T(8,128)S(1)}, f32[18,1,128]{2,0,1:T(8,128)S(1)}, u32[]{:S(2)}, u32[]{:S(2)}) collective-permute-start(f32[18,1,128]{2,0,1:T(8,128)S(1)} %get-tuple-element.43), channel_id=1, source_target_pairs={{4,0},{5,1},{6,2},{7,3},{12,8},{13,9},{14,10},{15,11},{20,16},{21,... | collective-permute-start | bytes 27656 | tf_op jit(solution)/shard_map/ppermute | solution.py:17
  22.0 7.2 %collective-permute-start.6 = (f32[18,1,128]{2,0,1:T(8,128)S(1)}, f32[18,1,128]{2,0,1:T(8,128)S(1)}, u32[]{:S(2)}, u32[]{:S(2)}) collective-permute-start(f32[18,1,128]{2,0,1:T(8,128)S(1)} %get-tuple-element.44), channel_id=1, source_target_pairs={{0,4},{1,5},{2,6},{3,7},{8,12},{9,13},{10,14},{11,15},{16,20},{17,... | collective-permute-start | bytes 27656 | tf_op jit(solution)/shard_map/ppermute | solution.py:16
  26.6 14.1 %collective-permute-start.7 = (f32[18,1,128]{2,0,1:T(8,128)S(1)}, f32[18,1,128]{2,0,1:T(8,128)S(1)}, u32[]{:S(2)}, u32[]{:S(2)}) collective-permute-start(f32[18,1,128]{2,0,1:T(8,128)S(1)} %get-tuple-element.45), channel_id=1, source_target_pairs={{0,4},{1,5},{2,6},{3,7},{8,12},{9,13},{10,14},{11,15},{16,20},{17,... | collective-permute-start | bytes 27656 | tf_op jit(solution)/shard_map/ppermute | solution.py:16
  27.9 12.8 %collective-permute-start.5 = (f32[18,1,128]{2,0,1:T(8,128)S(1)}, f32[18,1,128]{2,0,1:T(8,128)S(1)}, u32[]{:S(2)}, u32[]{:S(2)}) collective-permute-start(f32[18,1,128]{2,0,1:T(8,128)S(1)} %get-tuple-element.46), channel_id=1, source_target_pairs={{4,0},{5,1},{6,2},{7,3},{12,8},{13,9},{14,10},{15,11},{20,16},{21,... | collective-permute-start | bytes 27656 | tf_op jit(solution)/shard_map/ppermute | solution.py:17
  36.3 19.1 %collective-permute-start.8 = (f32[18,130,1]{1,0,2:T(8,128)S(1)}, f32[18,130,1]{1,0,2:T(8,128)S(1)}, u32[]{:S(2)}, u32[]{:S(2)}) collective-permute-start(f32[18,130,1]{1,0,2:T(8,128)S(1)} %copy.162), channel_id=1, source_target_pairs={{1,0},{2,1},{3,2},{5,4},{6,5},{7,6},{9,8},{10,9},{11,10},{13,12},{... | collective-permute-start | bytes 28088 | tf_op jit(solution)/shard_map/ppermute | solution.py:17
  37.6 15.6 %collective-permute-start.10 = (f32[18,130,1]{1,0,2:T(8,128)S(1)}, f32[18,130,1]{1,0,2:T(8,128)S(1)}, u32[]{:S(2)}, u32[]{:S(2)}) collective-permute-start(f32[18,130,1]{1,0,2:T(8,128)S(1)} %copy.168), channel_id=1, source_target_pairs={{0,1},{1,2},{2,3},{4,5},{5,6},{6,7},{8,9},{9,10},{10,11},{12,13},{... | collective-permute-start | bytes 28088 | tf_op jit(solution)/shard_map/ppermute | solution.py:16
  45.5 12.1 %collective-permute-start.9 = (f32[18,130,1]{1,0,2:T(8,128)S(1)}, f32[18,130,1]{1,0,2:T(8,128)S(1)}, u32[]{:S(2)}, u32[]{:S(2)}) collective-permute-start(f32[18,130,1]{1,0,2:T(8,128)S(1)} %copy.165), channel_id=1, source_target_pairs={{1,0},{2,1},{3,2},{5,4},{6,5},{7,6},{9,8},{10,9},{11,10},{13,12},{... | collective-permute-start | bytes 28088 | tf_op jit(solution)/shard_map/ppermute | solution.py:17
  49.1 10.5 %collective-permute-start.11 = (f32[18,130,1]{1,0,2:T(8,128)S(1)}, f32[18,130,1]{1,0,2:T(8,128)S(1)}, u32[]{:S(2)}, u32[]{:S(2)}) collective-permute-start(f32[18,130,1]{1,0,2:T(8,128)S(1)} %copy.171), channel_id=1, source_target_pairs={{0,1},{1,2},{2,3},{4,5},{5,6},{6,7},{8,9},{9,10},{10,11},{12,13},{... | collective-permute-start | bytes 28088 | tf_op jit(solution)/shard_map/ppermute | solution.py:16
  61.7 52.6 %copy-start = (f32[16,128,128]{2,1,0:T(8,128)S(1)}, f32[16,128,128]{2,1,0:T(8,128)}, u32[]{:S(2)}) copy-start(f32[16,128,128]{2,1,0:T(8,128)} %param.6) | copy-start | bytes 3145732
  120.3 4.0 %collective-permute-start.13 = (f32[1,128,128]{2,0,1:T(1,128)S(1)}, f32[1,128,128]{2,0,1:T(1,128)S(1)}, u32[]{:S(2)}, u32[]{:S(2)}) collective-permute-start(f32[1,128,128]{2,0,1:T(1,128)S(1)} %get-tuple-element.49), channel_id=1, source_target_pairs={{0,8},{8,16},{16,24},{1,9},{9,17},{17,25},{2,10},{10,18},{18,26},{... | collective-permute-start | bytes 196616 | tf_op jit(solution)/shard_map/ppermute | solution.py:16
  122.4 6.2 %collective-permute-start.12 = (f32[1,128,128]{2,0,1:T(1,128)S(1)}, f32[1,128,128]{2,0,1:T(1,128)S(1)}, u32[]{:S(2)}, u32[]{:S(2)}) collective-permute-start(f32[1,128,128]{2,0,1:T(1,128)S(1)} %get-tuple-element.50), channel_id=1, source_target_pairs={{8,0},{16,8},{24,16},{9,1},{17,9},{25,17},{10,2},{18,10},{26,18},{... | collective-permute-start | bytes 196616 | tf_op jit(solution)/shard_map/ppermute | solution.py:17
  128.6 5.6 %collective-permute-start.15 = (f32[18,1,128]{2,0,1:T(8,128)S(1)}, f32[18,1,128]{2,0,1:T(8,128)S(1)}, u32[]{:S(2)}, u32[]{:S(2)}) collective-permute-start(f32[18,1,128]{2,0,1:T(8,128)S(1)} %get-tuple-element.41), channel_id=1, source_target_pairs={{0,4},{1,5},{2,6},{3,7},{8,12},{9,13},{10,14},{11,15},{16,20},{17,... | collective-permute-start | bytes 27656 | tf_op jit(solution)/shard_map/ppermute | solution.py:16
  132.8 5.6 %collective-permute-start.14 = (f32[18,1,128]{2,0,1:T(8,128)S(1)}, f32[18,1,128]{2,0,1:T(8,128)S(1)}, u32[]{:S(2)}, u32[]{:S(2)}) collective-permute-start(f32[18,1,128]{2,0,1:T(8,128)S(1)} %get-tuple-element.42), channel_id=1, source_target_pairs={{4,0},{5,1},{6,2},{7,3},{12,8},{13,9},{14,10},{15,11},{20,16},{21,... | collective-permute-start | bytes 27656 | tf_op jit(solution)/shard_map/ppermute | solution.py:17
  143.2 6.7 %collective-permute-start.16 = (f32[18,130,1]{1,0,2:T(8,128)S(1)}, f32[18,130,1]{1,0,2:T(8,128)S(1)}, u32[]{:S(2)}, u32[]{:S(2)}) collective-permute-start(f32[18,130,1]{1,0,2:T(8,128)S(1)} %copy.182), channel_id=1, source_target_pairs={{1,0},{2,1},{3,2},{5,4},{6,5},{7,6},{9,8},{10,9},{11,10},{13,12},{... | collective-permute-start | bytes 28088 | tf_op jit(solution)/shard_map/ppermute | solution.py:17
  146.8 5.1 %collective-permute-start.17 = (f32[18,130,1]{1,0,2:T(8,128)S(1)}, f32[18,130,1]{1,0,2:T(8,128)S(1)}, u32[]{:S(2)}, u32[]{:S(2)}) collective-permute-start(f32[18,130,1]{1,0,2:T(8,128)S(1)} %copy.184), channel_id=1, source_target_pairs={{0,1},{1,2},{2,3},{4,5},{5,6},{6,7},{8,9},{9,10},{10,11},{12,13},{... | collective-permute-start | bytes 28088 | tf_op jit(solution)/shard_map/ppermute | solution.py:16
  207.8 18.3 %copy-start.1 = (f32[16,128,128]{2,0,1:T(8,128)}, f32[16,128,128]{2,0,1:T(8,128)S(1)}, u32[]{:S(2)}) copy-start(f32[16,128,128]{2,0,1:T(8,128)S(1)} %get-tuple-element.20) | copy-start | bytes 3145732
  207.9 4.1 %collective-permute-start.19 = (f32[1,128,128]{2,0,1:T(1,128)S(1)}, f32[1,128,128]{2,0,1:T(1,128)S(1)}, u32[]{:S(2)}, u32[]{:S(2)}) collective-permute-start(f32[1,128,128]{2,0,1:T(1,128)S(1)} %get-tuple-element.47), channel_id=1, source_target_pairs={{0,8},{8,16},{16,24},{1,9},{9,17},{17,25},{2,10},{10,18},{18,26},{... | collective-permute-start | bytes 196616 | tf_op jit(solution)/shard_map/ppermute | solution.py:16
  210.1 6.2 %collective-permute-start.18 = (f32[1,128,128]{2,0,1:T(1,128)S(1)}, f32[1,128,128]{2,0,1:T(1,128)S(1)}, u32[]{:S(2)}, u32[]{:S(2)}) collective-permute-start(f32[1,128,128]{2,0,1:T(1,128)S(1)} %get-tuple-element.48), channel_id=1, source_target_pairs={{8,0},{16,8},{24,16},{9,1},{17,9},{25,17},{10,2},{18,10},{26,18},{... | collective-permute-start | bytes 196616 | tf_op jit(solution)/shard_map/ppermute | solution.py:17
  216.3 5.7 %collective-permute-start.21 = (f32[18,1,128]{2,0,1:T(8,128)S(1)}, f32[18,1,128]{2,0,1:T(8,128)S(1)}, u32[]{:S(2)}, u32[]{:S(2)}) collective-permute-start(f32[18,1,128]{2,0,1:T(8,128)S(1)} %get-tuple-element.39), channel_id=1, source_target_pairs={{0,4},{1,5},{2,6},{3,7},{8,12},{9,13},{10,14},{11,15},{16,20},{17,... | collective-permute-start | bytes 27656 | tf_op jit(solution)/shard_map/ppermute | solution.py:16
  220.5 5.6 %collective-permute-start.20 = (f32[18,1,128]{2,0,1:T(8,128)S(1)}, f32[18,1,128]{2,0,1:T(8,128)S(1)}, u32[]{:S(2)}, u32[]{:S(2)}) collective-permute-start(f32[18,1,128]{2,0,1:T(8,128)S(1)} %get-tuple-element.40), channel_id=1, source_target_pairs={{4,0},{5,1},{6,2},{7,3},{12,8},{13,9},{14,10},{15,11},{20,16},{21,... | collective-permute-start | bytes 27656 | tf_op jit(solution)/shard_map/ppermute | solution.py:17
  230.8 6.8 %collective-permute-start.22 = (f32[18,130,1]{1,0,2:T(8,128)S(1)}, f32[18,130,1]{1,0,2:T(8,128)S(1)}, u32[]{:S(2)}, u32[]{:S(2)}) collective-permute-start(f32[18,130,1]{1,0,2:T(8,128)S(1)} %copy.189), channel_id=1, source_target_pairs={{1,0},{2,1},{3,2},{5,4},{6,5},{7,6},{9,8},{10,9},{11,10},{13,12},{... | collective-permute-start | bytes 28088 | tf_op jit(solution)/shard_map/ppermute | solution.py:17
  234.5 7.4 %copy-start.2 = (f32[16,128,128]{2,0,1:T(8,128)S(1)}, f32[16,128,128]{2,0,1:T(8,128)}, u32[]{:S(2)}) copy-start(f32[16,128,128]{2,0,1:T(8,128)} %copy-done.1) | copy-start | bytes 3145732
  234.5 5.3 %collective-permute-start.23 = (f32[18,130,1]{1,0,2:T(8,128)S(1)}, f32[18,130,1]{1,0,2:T(8,128)S(1)}, u32[]{:S(2)}, u32[]{:S(2)}) collective-permute-start(f32[18,130,1]{1,0,2:T(8,128)S(1)} %copy.191), channel_id=1, source_target_pairs={{0,1},{1,2},{2,3},{4,5},{5,6},{6,7},{8,9},{9,10},{10,11},{12,13},{... | collective-permute-start | bytes 28088 | tf_op jit(solution)/shard_map/ppermute | solution.py:16
where the time goes:
time: 299 us; the launch traced here: 298 us
  blocking collectives  122 us (41%)
  starting transfers between devices  57.9 us (19%)
  local copies, waits for them, and re-layouts  48.2 us (16%)
  other arithmetic  46.6 us (16%)
  waiting for transfers between devices  18.1 us (6%)
  between operations  5.17 us (2%)
    psum x3, blocking collectives, statistics(): lax.psum((squares, jnp.sum(own_induced)), ('gx', 'gy', 'gz'))  122 us
    ppermute x12, starting transfers between devices, padded_2(): before = lax.ppermute(last, axis, up)  42.2 us
    reduce_sum x3, other arithmetic, statistics(): squares = jnp.sum(own_residual * own_residual)  27.5 us
    ppermute x12, waiting for transfers between devices, padded_2(): after = lax.ppermute(initial, axis, down)  16.8 us
    slice x7, local copies, waits for them, and re-layouts, padded_2(): initial = lax.slice_in_dim(array, 0, width, axis=dim)  15.9 us
    ppermute x12, starting transfers between devices, padded_2(): after = lax.ppermute(initial, axis, down)  15.7 us
    slice x9, local copies, waits for them, and re-layouts, padded_2(): last = lax.slice_in_dim(array, length - width, length, axis=dim)  13.5 us
    reduce_sum x2, other arithmetic, statistics(): jnp.sum(own_induced)  9.21 us
  transfers between devices with their start and end apart: 24, of which 7 were waited for; matrix products, arithmetic and copies ran while one was open for 12% of the time, Pallas kernels for 0%

commit v1 on v0

v1 whole, which is shorter than its diff:
```python
import functools
import jax
import jax.numpy as jnp
from jax import lax
from jax.experimental import pallas as pl
from jax.experimental.pallas import tpu as pltpu
from jax.sharding import PartitionSpec as P

ITERS = 3
AXES = ("gx", "gy", "gz")
OFF = 8
CHUNK = 32
LOG2E = 1.4426950408889634
F32 = jnp.float32


def harmonic(left, right):
    total = left + right
    return 2.0 * left * right / jnp.where(total > 0, total, 1.0)


def sides_of(size):
    return 0 if size < 2 else 1 if size == 2 else 2


def swaps(size):
    a = [(i, i ^ 1) for i in range(size) if i ^ 1 < size]
    b = [(i, i + 1) for i in range(1, size - 1, 2)]
    return (a, b + [(j, i) for i, j in b])


def after_of(axis):
    odd = lax.rem(lax.axis_index(axis), 2)
    return (1 - odd, odd)


class Plan:
    def __init__(self, mesh):
        self.sizes = [mesh.shape[a] for a in AXES]
        self.count = self.sizes[0] * self.sizes[1] * self.sizes[2]
        self.swaps = [(d, s) for d in range(3) for s in range(sides_of(self.sizes[d]))]

    def exchange(self, faces):
        out = []
        for (d, s), face in zip(self.swaps, faces):
            out.append(lax.ppermute(face, AXES[d], swaps(self.sizes[d])[s]))
        return out

    def face_shapes(self, shape, lead=()):
        nx, ny, nz = shape
        kinds = ((ny, nz), (nx, 1, nz), (nx, ny))
        return [lead + kinds[d] for d, _ in self.swaps]


def vmem(shape):
    return pltpu.VMEM(tuple(shape), F32)


def call(kernel, out_shapes, args, out_specs=None, aliases=None, cost=(0, 0), name=None):
    vm = pl.BlockSpec(memory_space=pltpu.VMEM)
    return pl.pallas_call(
        kernel,
        out_shape=out_shapes,
        in_specs=[vm] * len(args),
        out_specs=out_specs or [vm] * len(out_shapes),
        input_output_aliases=aliases or {},
        compiler_params=pltpu.CompilerParams(vmem_limit_bytes=16 * 2**20),
        cost_estimate=pl.CostEstimate(flops=cost[0], bytes_accessed=cost[1], transcendentals=0),
        name=name,
    )(*args)


def faces_kernel(plan, phi, eps, *outs):
    nx, ny, nz = phi.shape
    z_faces = []
    for (d, s), out in zip(plan.swaps, outs):
        after = after_of(AXES[d])[s]
        for k, ref in enumerate((phi, eps)):
            if d == 0:
                out[k] = ref[after * (nx - 1)]
            elif d == 1:
                out[k] = ref[:, pl.ds(after * (ny - 1), 1), :]
        if d == 2:
            z_faces.append((after, out))
    if z_faces:
        for k, ref in enumerate((phi, eps)):
            for x in range(nx):
                flipped = ref[x].T
                first, last = flipped[0:1], flipped[nz - 1 : nz]
                for after, out in z_faces:
                    out[k, x : x + 1, :] = jnp.where(after == 1, last, first)


def weights_kernel(phi, eps, pad, wx, wy, wz):
    nx, ny, nz = phi.shape
    lane = lax.broadcasted_iota(jnp.int32, (CHUNK, nz), 1)
    zero = jnp.zeros((ny, nz), F32)
    pad[0] = jnp.zeros(pad.shape[1:], F32)
    pad[nx + 1] = jnp.zeros(pad.shape[1:], F32)
    wx[0] = zero
    wx[nx] = zero

    def plane(x, carry):
        edge = jnp.zeros((OFF, nz), F32)
        pad[x + 1, 0:OFF] = edge
        pad[x + 1, OFF + ny : 2 * OFF + ny] = edge
        wy[x, 0:OFF] = edge
        wy[x, OFF + ny : 2 * OFF + ny] = edge
        for y in range(0, ny, CHUNK):
            here = eps[x, y : y + CHUNK]
            pad[x + 1, OFF + y : OFF + y + CHUNK] = phi[x, y : y + CHUNK]
            right = harmonic(here, pltpu.roll(here, nz - 1, 1))
            wz[x, y : y + CHUNK] = jnp.where(lane == nz - 1, 0.0, right)
            if y + CHUNK < ny:
                wy[x, OFF + y : OFF + y + CHUNK] = harmonic(here, eps[x, y + 1 : y + 1 + CHUNK])
            else:
                wy[x, OFF + y : OFF + y + CHUNK - 1] = harmonic(
                    eps[x, y : y + CHUNK - 1], eps[x, y + 1 : y + CHUNK]
                )
                wy[x, OFF + ny - 1 : OFF + ny] = jnp.zeros((1, nz), F32)
        return carry

    lax.fori_loop(0, nx, plane, 0)

    def deep(x, carry):
        for y in range(0, ny, CHUNK):
            wx[x + 1, y : y + CHUNK] = harmonic(eps[x, y : y + CHUNK], eps[x + 1, y : y + CHUNK])
        return carry

    lax.fori_loop(0, nx - 1, deep, 0)


def spread(scratch, before, after):
    nz = scratch.shape[0]
    nx = before.shape[0]
    for x in range(nx):
        scratch[2 * x : 2 * x + 1] = before[x : x + 1]
        row = (2 * x - 1) % nz
        scratch[row : row + 1] = after[x : x + 1]
    return scratch[...].T


def sweep(plan, refs, z_flux, z_weight):
    pad, wx, wy, wz, diag, scr, src, d, stats, faces, gt, gw, turn = refs
    nx, ny, nz = d.shape
    lane = lax.broadcasted_iota(jnp.int32, (CHUNK, nz), 1)
    edge = (lane == 0) | (lane == nz - 1)
    first = z_weight is not None
    turn[...] = jnp.zeros(turn.shape, F32)
    gt[...] = spread(turn, *z_flux)
    if first:
        gw[...] = spread(turn, *z_weight)
    z_faces = [
        (after_of("gz")[s], out) for (dim, s), out in zip(plan.swaps, faces) if dim == 2
    ]

    def plane(x, sums):
        squares, charges = sums
        shift = lax.rem(nz - 2 * x, nz)
        for y in range(0, ny, CHUNK):
            rows = pl.ds(y, CHUNK)
            c = pad[x + 1, OFF + y : OFF + y + CHUNK]
            w_xp, w_xm = wx[x + 1, rows], wx[x, rows]
            w_yp = wy[x, OFF + y : OFF + y + CHUNK]
            w_ym = wy[x, OFF - 1 + y : OFF - 1 + y + CHUNK]
            w_z = wz[x, rows]
            f_z = w_z * (c - pltpu.roll(c, nz - 1, 1))
            flux = w_xp * (c - pad[x + 2, OFF + y : OFF + y + CHUNK])
            flux += w_xm * (c - pad[x, OFF + y : OFF + y + CHUNK])
            flux += w_yp * (c - pad[x + 1, OFF + 1 + y : OFF + 1 + y + CHUNK])
            flux += w_ym * (c - pad[x + 1, OFF - 1 + y : OFF - 1 + y + CHUNK])
            flux += f_z - pltpu.roll(f_z, 1, 1)
            flux += jnp.where(edge, pltpu.roll(gt[rows], shift, 1), 0.0)
            if first:
                total = (w_xp + w_xm) + (w_yp + w_ym) + (w_z + pltpu.roll(w_z, 1, 1))
                total += jnp.where(edge, pltpu.roll(gw[rows], shift, 1), 0.0)
                diag[x, rows] = total
            else:
                total = diag[x, rows]
            up = jnp.exp2(c * LOG2E)
            down = jnp.exp2(c * -LOG2E)
            c2 = c * c
            series = c * (1.0 + c2 * (1.0 / 6.0 + c2 * (1.0 / 120.0)))
            s = scr[x, rows]
            charge = s * jnp.where(c2 < 0.0625, series, 0.5 * (up - down))
            res = src[x, rows] - flux - charge
            total = total + s * (0.5 * (up + down))
            d[x, rows] = res / jnp.where(total > 0, total, 1.0)
            squares += jnp.sum((res * res).reshape(CHUNK // 8, 8, nz), axis=0)
            charges += jnp.sum(charge.reshape(CHUNK // 8, 8, nz), axis=0)
        if z_faces:
            flipped = d[x].T
            head, tail = flipped[0:1], flipped[nz - 1 : nz]
            for after, out in z_faces:
                out[pl.ds(x, 1), :] = jnp.where(after == 1, tail, head)
        return (squares, charges)

    none = jnp.zeros((8, nz), F32)
    squares, charges = lax.fori_loop(0, nx, plane, (none, none))
    half = nz // 2
    a = jnp.sum(squares, axis=0, keepdims=True)
    b = jnp.sum(charges, axis=0, keepdims=True)
    a = a + pltpu.roll(a, half, 1)
    b = b + pltpu.roll(b, half, 1)
    low = lax.broadcasted_iota(jnp.int32, (1, nz), 1) < half
    stats[...] = jnp.broadcast_to(jnp.where(low, a, b), stats.shape)
    for (dim, s), out in zip(plan.swaps, faces):
        after = after_of(AXES[dim])[s]
        if dim == 0:
            out[...] = d[after * (nx - 1)]
        elif dim == 1:
            out[...] = d[:, pl.ds(after * (ny - 1), 1), :]


def totals(stats, cells):
    rows, nz = stats.shape
    both = jnp.sum(stats[...], axis=0, keepdims=True)
    low = lax.broadcasted_iota(jnp.int32, (1, nz), 1) < nz // 2
    squares = jnp.sum(jnp.where(low, both, 0.0), axis=1, keepdims=True)
    charges = jnp.sum(jnp.where(low, 0.0, both), axis=1, keepdims=True)
    return jnp.sqrt(squares / cells + 1e-06), charges / cells


def z_pair(plan, values, like):
    zero = jnp.zeros(like, F32)
    if not values:
        return (zero, zero)
    one = after_of("gz")[0] == 1
    other = values[1] if len(values) > 1 else zero
    return (jnp.where(one, other, values[0]), jnp.where(one, values[0], other))


def first_kernel(plan, *refs):
    k = len(plan.swaps)
    sent, got = refs[:k], refs[k : 2 * k]
    _, _, _, wz, scr, src = refs[2 * k : 2 * k + 6]
    pad, wx, wy, diag, d, stats, zs = refs[2 * k + 6 : 2 * k + 13]
    faces = refs[2 * k + 13 : 3 * k + 13]
    gt, gw, turn = refs[3 * k + 13 :]
    nx, ny, nz = d.shape
    fluxes, weights = [], []
    for (dim, s), mine, theirs in zip(plan.swaps, sent, got):
        after = after_of(AXES[dim])[s]
        if dim == 0:
            pad[after * (nx + 1), OFF : OFF + ny] = theirs[0]
            wx[after * nx] = harmonic(mine[1], theirs[1])
        elif dim == 1:
            row = OFF - 1 + after * (ny + 1)
            pad[1 : nx + 1, pl.ds(row, 1), :] = theirs[0]
            wy[:, pl.ds(OFF - 1 + after * ny, 1), :] = harmonic(mine[1], theirs[1])
        else:
            w = harmonic(mine[1], theirs[1])
            zs[3 * s] = mine[0]
            zs[3 * s + 1] = theirs[0]
            zs[3 * s + 2] = w
            weights.append(w)
            fluxes.append(w * (mine[0] - theirs[0]))
    like = (nx, ny)
    sweep(
        plan,
        (pad, wx, wy, wz, diag, scr, src, d, stats, faces, gt, gw, turn),
        z_pair(plan, fluxes, like),
        z_pair(plan, weights, like),
    )


def advance(plan, pad, d, omega):
    nx, ny, nz = d.shape

    def plane(x, carry):
        pad[x + 1, OFF : OFF + ny] += omega * d[x]
        return carry

    lax.fori_loop(0, nx, plane, 0)


def next_kernel(plan, cells, *refs):
    k = len(plan.swaps)
    sent, got = refs[:k], refs[k : 2 * k]
    seen, d_old, _, zs_old, wx, wy, wz, diag, scr, src = refs[2 * k : 2 * k + 10]
    pad, d, stats, zs = refs[2 * k + 10 : 2 * k + 14]
    faces = refs[2 * k + 14 : 3 * k + 14]
    gt, turn = refs[3 * k + 14 :]
    nx, ny, nz = d.shape
    rms, _ = totals(seen, cells)
    omega = 1.0 / (1.0 + rms)
    advance(plan, pad, d_old, omega)
    fluxes = []
    for (dim, s), mine, theirs in zip(plan.swaps, sent, got):
        after = after_of(AXES[dim])[s]
        if dim == 0:
            pad[after * (nx + 1), OFF : OFF + ny] += omega * theirs[...]
        elif dim == 1:
            row = OFF - 1 + after * (ny + 1)
            pad[1 : nx + 1, pl.ds(row, 1), :] += omega[:, None] * theirs[...]
        else:
            own = zs_old[3 * s] + omega * mine[...]
            far = zs_old[3 * s + 1] + omega * theirs[...]
            w = zs_old[3 * s + 2]
            zs[3 * s] = own
            zs[3 * s + 1] = far
            zs[3 * s + 2] = w
            fluxes.append(w * (own - far))
    sweep(
        plan,
        (pad, wx, wy, wz, diag, scr, src, d, stats, faces, gt, None, turn),
        z_pair(plan, fluxes, (nx, ny)),
        None,
    )


def last_kernel(cells, *refs):
    seen = refs[:ITERS]
    pad, d, out, norms, charges = refs[ITERS:]
    nx, ny, nz = d.shape
    for t in range(ITERS):
        rms, charge = totals(seen[t], cells)
        norms[t] = rms[0, 0]
        charges[t] = charge[0, 0]
    omega = 1.0 / (1.0 + rms)

    def plane(x, carry):
        out[x] = pad[x + 1, OFF : OFF + ny] + omega * d[x]
        return carry

    lax.fori_loop(0, nx, plane, 0)


def body(plan, phi, eps, scr, src):
    shape = phi.shape
    nx, ny, nz = shape
    cells = float(nx * ny * nz * plan.count)
    k = len(plan.swaps)
    work = 60 * nx * ny * nz
    cost = (200 * work, 4 * nx * ny * nz)
    padded = (nx + 2, ny + 2 * OFF, nz)

    def gather(stats):
        return lax.all_to_all(stats, AXES, 0, 0, tiled=True)

    def like(refs):
        return [vmem(r.shape) for r in refs]

    sent = call(
        functools.partial(faces_kernel, plan),
        [vmem(s) for s in plan.face_shapes(shape, (2,))],
        (phi, eps),
        cost=cost,
        name="faces",
    )
    got = plan.exchange(sent)
    pad, wx, wy, wz = call(
        weights_kernel,
        [vmem(padded), vmem((nx + 1, ny, nz)), vmem((nx, ny + 2 * OFF, nz)), vmem(shape)],
        (phi, eps),
        cost=cost,
        name="weights",
    )
    z_state = vmem((6, nx, ny))
    face_out = [vmem(s) for s in plan.face_shapes(shape)]
    vm = pl.BlockSpec(memory_space=pltpu.VMEM)

    def sweep_call(kernel, outs, args, aliases, scratch, name):
        return pl.pallas_call(
            kernel,
            out_shape=outs,
            in_specs=[vm] * len(args),
            out_specs=[vm] * len(outs),
            scratch_shapes=scratch,
            input_output_aliases=aliases,
            compiler_params=pltpu.CompilerParams(vmem_limit_bytes=16 * 2**20),
            cost_estimate=pl.CostEstimate(flops=cost[0], bytes_accessed=cost[1], transcendentals=0),
            name=name,
        )(*args)

    stats_shape = vmem((plan.count, nz))
    turned, flat = vmem((nz, ny)), vmem((ny, nz))
    outs = sweep_call(
        functools.partial(first_kernel, plan),
        like((pad, wx, wy)) + [vmem(shape), vmem(shape), stats_shape, z_state] + face_out,
        (*sent, *got, pad, wx, wy, wz, scr, src),
        {2 * k: 0, 2 * k + 1: 1, 2 * k + 2: 2},
        [flat, flat, turned],
        "sweep_0",
    )
    pad, wx, wy, diag, d, stats, zs = outs[:7]
    sent = outs[7:]
    seen = []
    for t in range(1, ITERS):
        got = plan.exchange(sent)
        seen.append(gather(stats))
        outs = sweep_call(
            functools.partial(next_kernel, plan, cells),
            [vmem(padded), vmem(shape), stats_shape, z_state] + (face_out if t < ITERS - 1 else face_out),
            (*sent, *got, seen[-1], d, pad, zs, wx, wy, wz, diag, scr, src),
            {2 * k + 2: 0},
            [flat, turned],
            f"sweep_{t}",
        )
        pad, d, stats, zs = outs[:4]
        sent = outs[4:]
    seen.append(gather(stats))
    sm = pl.BlockSpec(memory_space=pltpu.SMEM)
    small = jax.ShapeDtypeStruct((ITERS,), F32)
    return call(
        functools.partial(last_kernel, cells),
        [jax.ShapeDtypeStruct(shape, F32), small, small],
        (*seen, pad, d),
        out_specs=[vm, sm, sm],
        cost=cost,
        name="finish",
    )


def solution(mesh):
    block = P(*AXES)
    return jax.shard_map(
        functools.partial(body, Plan(mesh)),
        mesh=mesh,
        in_specs=(block,) * 4,
        out_specs=(block, P(), P()),
        check_vma=False,
    )
```

time: 299 us -> 96.7 us (0.32)
  blocking collectives: 122 us -> 11.2 us
  other arithmetic: 46.6 us -> 0 us
  starting transfers between devices: 57.9 us -> 30.2 us
  local copies, waits for them, and re-layouts: 48.2 us -> 24.7 us
  Pallas kernels: 0 us -> 18.9 us
  waiting for transfers between devices: 18.1 us -> 10.1 us
  between operations: 5.17 us -> 0.79 us
    psum x3 -> x0, blocking collectives: 122 us -> none  [statistics(): lax.psum((squares, jnp.sum(own_induced)), ('gx', 'gy', 'gz'))]
    ppermute x24 -> x15, starting transfers between devices: 57.9 us -> 17.7 us  [exchange(): out.append(lax.ppermute(face, AXES[d], swaps(self.sizes[d])[s]))]
    reduce_sum x5 -> x0, other arithmetic: 36.7 us -> none  [the longest x3 27.5 us: statistics(): squares = jnp.sum(own_residual * own_residual)]
    slice x16 -> x0, local copies, waits for them, and re-layouts: 29.5 us -> none  [the longest x7 15.9 us: padded_2(): initial = lax.slice_in_dim(array, 0, width, axis=dim)]
    unnamed x10 -> x48, local copies, waits for them, and re-layouts: 1.92 us -> 24.7 us
    pallas_call x0 -> x6, Pallas kernels: none -> 18.9 us  [the longest x3 15.1 us: sweep_call(): pl.pallas_call(kernel, out_shape=outs, in_specs=[vm] * len(args), out_spe...]
    ppermute x8 -> x0, local copies, waits for them, and re-layouts: 16.9 us -> none  [the longest x4 8.47 us: padded_2(): before = lax.ppermute(last, axis, up)]
    ppermute x24 -> x15, waiting for transfers between devices: 18.1 us -> 3.16 us  [exchange(): out.append(lax.ppermute(face, AXES[d], swaps(self.sizes[d])[s]))]
  transfers between devices with their start and end apart: 24 -> 17, of which waited for: 7 -> 5; matrix products, arithmetic and copies ran while one was open for 12% -> 0% of each run, Pallas kernels for 0% -> 2%
where the time goes in v1:
time: 96.7 us; the launch traced here: 95.8 us
  starting transfers between devices  30.2 us (31%)
  local copies, waits for them, and re-layouts  24.7 us (26%)
  Pallas kernels  18.9 us (20%)
  blocking collectives  11.2 us (12%)
  waiting for transfers between devices  10.1 us (10%)
    unnamed x48, local copies, waits for them, and re-layouts  24.7 us
    ppermute x15, starting transfers between devices, exchange(): out.append(lax.ppermute(face, AXES[d], swaps(self.sizes[d])[s]))  17.7 us
    pallas_call x3, Pallas kernels, sweep_call(): pl.pallas_call(kernel, out_shape=outs, in_specs=[vm] * len(args), out_spe...  15.1 us
    all_to_all x2, starting transfers between devices, gather(): return lax.all_to_all(stats, AXES, 0, 0, tiled=True)  12.5 us
    all_to_all x1, blocking collectives, gather(): return lax.all_to_all(stats, AXES, 0, 0, tiled=True)  11.2 us
    all_to_all x2, waiting for transfers between devices, gather(): return lax.all_to_all(stats, AXES, 0, 0, tiled=True)  6.91 us
    pallas_call x3, Pallas kernels, call(): pl.pallas_call(kernel, out_shape=out_shapes, in_specs=[vm] * len(args), o...  3.74 us
    ppermute x15, waiting for transfers between devices, exchange(): out.append(lax.ppermute(face, AXES[d], swaps(self.sizes[d])[s]))  3.16 us
  transfers between devices with their start and end apart: 17, of which 5 were waited for; matrix products, arithmetic and copies ran while one was open for 0% of the time, Pallas kernels for 2%

profile of v1, /device:TPU:0, one launch (start us, length us, event | category | flops | bytes accessed | tf_op | source)
XLA Modules:
  0.0 95.8 jit_solution(3342978196976359911)
XLA Ops:
  0.6 1.2 %copy-done = f32[16,128,128]{2,1,0:T(8,128)S(1)} copy-done((f32[16,128,128]{2,1,0:T(8,128)S(1)}, f32[16,128,128]{2,1,0:T(8,128)}, u32[]{:S(2)}) %copy-start) | copy-done | bytes 1048600
  1.9 1.2 %copy-done.1 = f32[16,128,128]{2,1,0:T(8,128)S(1)} copy-done((f32[16,128,128]{2,1,0:T(8,128)S(1)}, f32[16,128,128]{2,1,0:T(8,128)}, u32[]{:S(2)}) %copy-start.1) | copy-done | bytes 1048600
  3.7 3.0 %collective-permute-start.2 = (f32[2,16,1,128]{3,2,1,0:T(1,128)S(1)}, f32[2,16,1,128]{3,2,1,0:T(1,128)S(1)}, u32[]{:S(2)}, u32[]{:S(2)}) collective-permute-start(f32[2,16,1,128]{3,2,1,0:T(1,128)S(1)} %get-tuple-element.38.refs_2_), channel_id=1, source_target_pairs={{0,4},{4,0},{1,5},{5,1},{2,6},{6,2},{3,7},{7,3},{8,12},{12,8},{9,1... | collective-permute-start | bytes 49160 | tf_op jit(solution)/shard_map/ppermute | solution.py:46
  7.4 1.6 %collective-permute-start = (f32[2,128,128]{2,1,0:T(8,128)S(1)}, f32[2,128,128]{2,1,0:T(8,128)S(1)}, u32[]{:S(2)}, u32[]{:S(2)}) collective-permute-start(f32[2,128,128]{2,1,0:T(8,128)S(1)} %get-tuple-element.36.refs_0_), channel_id=1, source_target_pairs={{0,8},{8,0},{16,24},{24,16},{1,9},{9,1},{17,25},{25,17},{2,10},{10... | collective-permute-start | bytes 393224 | tf_op jit(solution)/shard_map/ppermute | solution.py:46
  9.8 1.9 %weights.1 = (f32[18,144,128]{2,1,0:T(8,128)S(1)}, f32[17,128,128]{2,1,0:T(8,128)S(1)}, f32[16,144,128]{2,1,0:T(8,128)S(1)}, f32[16,128,128]{2,1,0:T(8,128)S(1)}) custom-call(f32[16,128,128]{2,1,0:T(8,128)S(1)} %copy-done, f32[16,128,128]{2,1,0:T(8,128)S(1)} %copy-done.1), custom_call_target="tpu_custom_call" | custom-call | flops 3145728000 | bytes 1048576 | tf_op jit(solution)/shard_map/weights/pallas_call | solution.py:61
  12.4 4.9 %sweep_0.1 = (f32[18,144,128]{2,1,0:T(8,128)S(1)}, f32[17,128,128]{2,1,0:T(8,128)S(1)}, f32[16,144,128]{2,1,0:T(8,128)S(1)}, f32[16,128,128]{2,1,0:T(8,128)S(1)}...) custom-call(f32[2,128,128]{2,1,0:T(8,128)S(1)} %get-tuple-element.36, ...), custom_call_target="tpu_custom_call", output_to_operand_aliasing={{0}: (10, {}), {1}: (11, {}), {2}: (12, {})} | custom-call | flops 3145728000 | bytes 1048576 | tf_op jit(solution)/shard_map/sweep_0/pallas_call | solution.py:364
  17.3 1.1 %copy-done.4 = f32[18,144,128]{2,1,0:T(8,128)} copy-done((f32[18,144,128]{2,1,0:T(8,128)}, f32[18,144,128]{2,1,0:T(8,128)S(1)}, u32[]{:S(2)}) %copy-start.4) | copy-done | bytes 1327128
  22.5 4.7 %collective-permute-start.5 = (f32[128,128]{1,0:T(8,128)S(1)}, f32[128,128]{1,0:T(8,128)S(1)}, u32[]{:S(2)}, u32[]{:S(2)}) collective-permute-start(f32[128,128]{1,0:T(8,128)S(1)} %get-tuple-element.46.refs_0_), channel_id=1, source_target_pairs={{0,8},{8,0},{16,24},{24,16},{1,9},{9,1},{17,25},{25,17},{2,10},{10... | collective-permute-start | bytes 196616 | tf_op jit(solution)/shard_map/ppermute | solution.py:46
  27.8 6.5 %all-to-all-start = ((f32[32,1,128]{2,1,0:T(1,128)}), f32[32,1,128]{2,1,0:T(1,128)S(1)}, u32[]{:S(2)}, u32[]{:S(2)}) async-start(f32[32,1,128]{2,1,0:T(1,128)} %bitcast.1), calls=%async_computation | async-start | bytes 32768 | tf_op jit(solution)/shard_map/all_to_all | solution.py:339
  34.3 1.8 %collective-permute-start.7 = (f32[16,1,128]{2,1,0:T(1,128)S(1)}, f32[16,1,128]{2,1,0:T(1,128)S(1)}, u32[]{:S(2)}, u32[]{:S(2)}) collective-permute-start(f32[16,1,128]{2,1,0:T(1,128)S(1)} %get-tuple-element.48.refs_2_), channel_id=1, source_target_pairs={{0,4},{4,0},{1,5},{5,1},{2,6},{6,2},{3,7},{7,3},{8,12},{12,8},{9,1... | collective-permute-start | bytes 24584 | tf_op jit(solution)/shard_map/ppermute | solution.py:46
  36.8 1.2 %collective-permute-done.7.refs_7_ = f32[16,1,128]{2,1,0:T(1,128)S(1)} collective-permute-done((f32[16,1,128]{2,1,0:T(1,128)S(1)}, f32[16,1,128]{2,1,0:T(1,128)S(1)}, u32[]{:S(2)}, u32[]{:S(2)}) %collective-permute-start.7) | collective-permute-done | bytes 8224 | tf_op jit(solution)/shard_map/ppermute | solution.py:46
  38.0 3.5 %all-to-all-done = f32[32,1,128]{2,1,0:T(1,128)S(1)} async-done(((f32[32,1,128]{2,1,0:T(1,128)}), f32[32,1,128]{2,1,0:T(1,128)S(1)}, u32[]{:S(2)}, u32[]{:S(2)}) %all-to-all-start) | async-done | bytes 16416 | tf_op jit(solution)/shard_map/all_to_all | solution.py:339
  41.5 1.3 %copy-done.5 = f32[18,144,128]{2,1,0:T(8,128)S(1)} copy-done((f32[18,144,128]{2,1,0:T(8,128)S(1)}, f32[18,144,128]{2,1,0:T(8,128)}, u32[]{:S(2)}) %copy-start.5) | copy-done | bytes 1327128
  42.8 1.3 %copy-done.9 = f32[16,144,128]{2,1,0:T(8,128)S(1)} copy-done((f32[16,144,128]{2,1,0:T(8,128)S(1)}, f32[16,144,128]{2,1,0:T(8,128)}, u32[]{:S(2)}) %copy-start.9) | copy-done | bytes 1179672
  44.1 1.2 %copy-done.12 = f32[17,128,128]{2,1,0:T(8,128)S(1)} copy-done((f32[17,128,128]{2,1,0:T(8,128)S(1)}, f32[17,128,128]{2,1,0:T(8,128)}, u32[]{:S(2)}) %copy-start.12) | copy-done | bytes 1114136
  45.3 1.2 %copy-done.15 = f32[16,128,128]{2,1,0:T(8,128)S(1)} copy-done((f32[16,128,128]{2,1,0:T(8,128)S(1)}, f32[16,128,128]{2,1,0:T(8,128)}, u32[]{:S(2)}) %copy-start.15) | copy-done | bytes 1048600
  46.5 1.2 %copy-done.18 = f32[16,128,128]{2,1,0:T(8,128)S(1)} copy-done((f32[16,128,128]{2,1,0:T(8,128)S(1)}, f32[16,128,128]{2,1,0:T(8,128)}, u32[]{:S(2)}) %copy-start.18) | copy-done | bytes 1048600
  47.8 1.2 %copy-done.23 = f32[16,128,128]{2,1,0:T(8,128)S(1)} copy-done((f32[16,128,128]{2,1,0:T(8,128)S(1)}, f32[16,128,128]{2,1,0:T(8,128)}, u32[]{:S(2)}) %copy-start.23) | copy-done | bytes 1048600
  49.0 5.1 %sweep_1.1 = (f32[18,144,128]{2,1,0:T(8,128)S(1)}, f32[16,128,128]{2,1,0:T(8,128)S(1)}, f32[32,128]{1,0:T(8,128)}, f32[6,16,128]{2,1,0:T(8,128)S(1)}, f32[128,12...) custom-call(f32[128,128]{1,0:T(8,128)S(1)} %get-tuple-element.46.ref, ...), custom_call_target="tpu_custom_call", output_to_operand_aliasing={{0}: (12, {})} | custom-call | flops 3145728000 | bytes 1048576 | tf_op jit(solution)/shard_map/sweep_1/pallas_call | solution.py:364
  57.4 6.1 %all-to-all-start.1 = ((f32[32,1,128]{2,1,0:T(1,128)}), f32[32,1,128]{2,1,0:T(1,128)S(1)}, u32[]{:S(2)}, u32[]{:S(2)}) async-start(f32[32,1,128]{2,1,0:T(1,128)} %bitcast.4), calls=%async_computation.1 | async-start | bytes 32768 | tf_op jit(solution)/shard_map/all_to_all | solution.py:339
  63.5 1.8 %collective-permute-start.12 = (f32[16,1,128]{2,1,0:T(1,128)S(1)}, f32[16,1,128]{2,1,0:T(1,128)S(1)}, u32[]{:S(2)}, u32[]{:S(2)}) collective-permute-start(f32[16,1,128]{2,1,0:T(1,128)S(1)} %get-tuple-element.60.refs_2_), channel_id=1, source_target_pairs={{0,4},{4,0},{1,5},{5,1},{2,6},{6,2},{3,7},{7,3},{8,12},{12,8},{9,1... | collective-permute-start | bytes 24584 | tf_op jit(solution)/shard_map/ppermute | solution.py:46
  66.0 1.2 %collective-permute-done.12.refs_7_ = f32[16,1,128]{2,1,0:T(1,128)S(1)} collective-permute-done((f32[16,1,128]{2,1,0:T(1,128)S(1)}, f32[16,1,128]{2,1,0:T(1,128)S(1)}, u32[]{:S(2)}, u32[]{:S(2)}) %collective-permute-start.12) | collective-permute-done | bytes 8224 | tf_op jit(solution)/shard_map/ppermute | solution.py:46
  67.2 3.5 %all-to-all-done.1 = f32[32,1,128]{2,1,0:T(1,128)S(1)} async-done(((f32[32,1,128]{2,1,0:T(1,128)}), f32[32,1,128]{2,1,0:T(1,128)S(1)}, u32[]{:S(2)}, u32[]{:S(2)}) %all-to-all-start.1) | async-done | bytes 16416 | tf_op jit(solution)/shard_map/all_to_all | solution.py:339
  70.6 1.3 %copy-done.7 = f32[18,144,128]{2,1,0:T(8,128)S(1)} copy-done((f32[18,144,128]{2,1,0:T(8,128)S(1)}, f32[18,144,128]{2,1,0:T(8,128)}, u32[]{:S(2)}) %copy-start.7) | copy-done | bytes 1327128
  72.0 1.3 %copy-done.10 = f32[16,144,128]{2,1,0:T(8,128)S(1)} copy-done((f32[16,144,128]{2,1,0:T(8,128)S(1)}, f32[16,144,128]{2,1,0:T(8,128)}, u32[]{:S(2)}) %copy-start.10) | copy-done | bytes 1179672
  73.2 1.2 %copy-done.13 = f32[17,128,128]{2,1,0:T(8,128)S(1)} copy-done((f32[17,128,128]{2,1,0:T(8,128)S(1)}, f32[17,128,128]{2,1,0:T(8,128)}, u32[]{:S(2)}) %copy-start.13) | copy-done | bytes 1114136
  74.5 1.2 %copy-done.16 = f32[16,128,128]{2,1,0:T(8,128)S(1)} copy-done((f32[16,128,128]{2,1,0:T(8,128)S(1)}, f32[16,128,128]{2,1,0:T(8,128)}, u32[]{:S(2)}) %copy-start.16) | copy-done | bytes 1048600
  75.7 1.2 %copy-done.19 = f32[16,128,128]{2,1,0:T(8,128)S(1)} copy-done((f32[16,128,128]{2,1,0:T(8,128)S(1)}, f32[16,128,128]{2,1,0:T(8,128)}, u32[]{:S(2)}) %copy-start.19) | copy-done | bytes 1048600
  76.9 1.2 %copy-done.21 = f32[16,128,128]{2,1,0:T(8,128)S(1)} copy-done((f32[16,128,128]{2,1,0:T(8,128)S(1)}, f32[16,128,128]{2,1,0:T(8,128)}, u32[]{:S(2)}) %copy-start.21) | copy-done | bytes 1048600
  78.2 5.1 %sweep_2.1 = (f32[18,144,128]{2,1,0:T(8,128)S(1)}, f32[16,128,128]{2,1,0:T(8,128)S(1)}, f32[32,128]{1,0:T(8,128)S(1)}, f32[6,16,128]{2,1,0:T(8,128)}, f32[128,12...) custom-call(f32[128,128]{1,0:T(8,128)S(1)} %get-tuple-element.58.ref, ...), custom_call_target="tpu_custom_call", output_to_operand_aliasing={{0}: (12, {})} | custom-call | flops 3145728000 | bytes 1048576 | tf_op jit(solution)/shard_map/sweep_2/pallas_call | solution.py:364
  83.3 11.2 %all_to_all.33 = f32[32,1,128]{2,1,0:T(1,128)S(1)} all-to-all(f32[32,1,128]{2,1,0:T(1,128)S(1)} %bitcast.16), channel_id=1, replica_groups=mesh['gx'=4,'gy'=2,'gz'=4] {'gx','gy','gz'}, dimensions={0} | all-to-all | bytes 32768 | tf_op jit(solution)/shard_map/all_to_all | solution.py:339
  94.5 1.3 %finish.1 = (f32[16,128,128]{2,1,0:T(8,128)}, f32[3]{0:T(128)}, f32[3]{0:T(128)}) custom-call(f32[32,128]{1,0:T(8,128)S(1)} %bitcast.13, f32[32,128]{1,0:T(8,128)S(1)} %bitcast.15, f32[32,128]{1,0:T(8,128)S(1)} %bitcast.17, f32[18,144,128]{2,1,0:T(8,128)S(1)} %get-tuple-element.67.refs_3_, f32[16,128,128]{2,1,0:T(8,128)S(1)} %get-tuple-element.68.refs_4_), custom_call_target="tpu_custom_call" | custom-call | flops 3145728000 | bytes 1048576 | tf_op jit(solution)/shard_map/finish/pallas_call | solution.py:61
  (57 shorter events, 12.1 us)
Async XLA Ops:
  0.6 1.2 %copy-start = (f32[16,128,128]{2,1,0:T(8,128)S(1)}, f32[16,128,128]{2,1,0:T(8,128)}, u32[]{:S(2)}) copy-start(f32[16,128,128]{2,1,0:T(8,128)} %phi.3) | copy-start | bytes 3145732
  1.9 1.2 %copy-start.1 = (f32[16,128,128]{2,1,0:T(8,128)S(1)}, f32[16,128,128]{2,1,0:T(8,128)}, u32[]{:S(2)}) copy-start(f32[16,128,128]{2,1,0:T(8,128)} %eps.3) | copy-start | bytes 3145732
  3.7 8.0 %collective-permute-start.2 = (f32[2,16,1,128]{3,2,1,0:T(1,128)S(1)}, f32[2,16,1,128]{3,2,1,0:T(1,128)S(1)}, u32[]{:S(2)}, u32[]{:S(2)}) collective-permute-start(f32[2,16,1,128]{3,2,1,0:T(1,128)S(1)} %get-tuple-element.38.refs_2_), channel_id=1, source_target_pairs={{0,4},{4,0},{1,5},{5,1},{2,6},{6,2},{3,7},{7,3},{8,12},{12,8},{9,1... | collective-permute-start | bytes 49160 | tf_op jit(solution)/shard_map/ppermute | solution.py:46
  6.7 5.0 %collective-permute-start.3 = (f32[2,16,128]{2,1,0:T(8,128)S(1)}, f32[2,16,128]{2,1,0:T(8,128)S(1)}, u32[]{:S(2)}, u32[]{:S(2)}) collective-permute-start(f32[2,16,128]{2,1,0:T(8,128)S(1)} %get-tuple-element.39.refs_3_), channel_id=1, source_target_pairs={{0,1},{1,0},{2,3},{3,2},{4,5},{5,4},{6,7},{7,6},{8,9},{9,8},{10,11... | collective-permute-start | bytes 49160 | tf_op jit(solution)/shard_map/ppermute | solution.py:46
  6.7 5.0 %collective-permute-start.4 = (f32[2,16,128]{2,1,0:T(8,128)S(1)}, f32[2,16,128]{2,1,0:T(8,128)S(1)}, u32[]{:S(2)}, u32[]{:S(2)}) collective-permute-start(f32[2,16,128]{2,1,0:T(8,128)S(1)} %get-tuple-element.40.refs_4_), channel_id=1, source_target_pairs={{1,2},{2,1},{5,6},{6,5},{9,10},{10,9},{13,14},{14,13},{17,18},{18,... | collective-permute-start | bytes 49160 | tf_op jit(solution)/shard_map/ppermute | solution.py:46
  7.4 5.0 %collective-permute-start = (f32[2,128,128]{2,1,0:T(8,128)S(1)}, f32[2,128,128]{2,1,0:T(8,128)S(1)}, u32[]{:S(2)}, u32[]{:S(2)}) collective-permute-start(f32[2,128,128]{2,1,0:T(8,128)S(1)} %get-tuple-element.36.refs_0_), channel_id=1, source_target_pairs={{0,8},{8,0},{16,24},{24,16},{1,9},{9,1},{17,25},{25,17},{2,10},{10... | collective-permute-start | bytes 393224 | tf_op jit(solution)/shard_map/ppermute | solution.py:46
  9.0 3.4 %copy-start.2 = (f32[16,128,128]{2,1,0:T(8,128)S(1)}, f32[16,128,128]{2,1,0:T(8,128)}, u32[]{:S(2)}) copy-start(f32[16,128,128]{2,1,0:T(8,128)} %refs_18_.3) | copy-start | bytes 3145732
  9.0 3.4 %copy-start.3 = (f32[16,128,128]{2,1,0:T(8,128)S(1)}, f32[16,128,128]{2,1,0:T(8,128)}, u32[]{:S(2)}) copy-start(f32[16,128,128]{2,1,0:T(8,128)} %refs_19_.3) | copy-start | bytes 3145732
  9.0 3.4 %collective-permute-start.1 = (f32[2,128,128]{2,1,0:T(8,128)S(1)}, f32[2,128,128]{2,1,0:T(8,128)S(1)}, u32[]{:S(2)}, u32[]{:S(2)}) collective-permute-start(f32[2,128,128]{2,1,0:T(8,128)S(1)} %get-tuple-element.37.refs_1_), channel_id=1, source_target_pairs={{8,16},{16,8},{9,17},{17,9},{10,18},{18,10},{11,19},{19,11},{12,20... | collective-permute-start | bytes 393224 | tf_op jit(solution)/shard_map/ppermute | solution.py:46
  11.7 5.6 %copy-start.14 = (f32[16,128,128]{2,1,0:T(8,128)}, f32[16,128,128]{2,1,0:T(8,128)S(1)}, u32[]{:S(2)}) copy-start(f32[16,128,128]{2,1,0:T(8,128)S(1)} %get-tuple-element.44.refs_13_.refs_16_) | copy-start | bytes 3145732
  22.5 19.0 %collective-permute-start.5 = (f32[128,128]{1,0:T(8,128)S(1)}, f32[128,128]{1,0:T(8,128)S(1)}, u32[]{:S(2)}, u32[]{:S(2)}) collective-permute-start(f32[128,128]{1,0:T(8,128)S(1)} %get-tuple-element.46.refs_0_), channel_id=1, source_target_pairs={{0,8},{8,0},{16,24},{24,16},{1,9},{9,1},{17,25},{25,17},{2,10},{10... | collective-permute-start | bytes 196616 | tf_op jit(solution)/shard_map/ppermute | solution.py:46
  27.2 14.3 %collective-permute-start.6 = (f32[128,128]{1,0:T(8,128)S(1)}, f32[128,128]{1,0:T(8,128)S(1)}, u32[]{:S(2)}, u32[]{:S(2)}) collective-permute-start(f32[128,128]{1,0:T(8,128)S(1)} %get-tuple-element.47.refs_1_), channel_id=1, source_target_pairs={{8,16},{16,8},{9,17},{17,9},{10,18},{18,10},{11,19},{19,11},{12,20... | collective-permute-start | bytes 196616 | tf_op jit(solution)/shard_map/ppermute | solution.py:46
  27.8 13.6 %all-to-all-start = ((f32[32,1,128]{2,1,0:T(1,128)}), f32[32,1,128]{2,1,0:T(1,128)S(1)}, u32[]{:S(2)}, u32[]{:S(2)}) async-start(f32[32,1,128]{2,1,0:T(1,128)} %bitcast.1), calls=%async_computation | async-start | bytes 32768 | tf_op jit(solution)/shard_map/all_to_all | solution.py:339
  34.3 3.7 %collective-permute-start.7 = (f32[16,1,128]{2,1,0:T(1,128)S(1)}, f32[16,1,128]{2,1,0:T(1,128)S(1)}, u32[]{:S(2)}, u32[]{:S(2)}) collective-permute-start(f32[16,1,128]{2,1,0:T(1,128)S(1)} %get-tuple-element.48.refs_2_), channel_id=1, source_target_pairs={{0,4},{4,0},{1,5},{5,1},{2,6},{6,2},{3,7},{7,3},{8,12},{12,8},{9,1... | collective-permute-start | bytes 24584 | tf_op jit(solution)/shard_map/ppermute | solution.py:46
  36.1 1.9 %collective-permute-start.8 = (f32[16,128]{1,0:T(8,128)S(1)}, f32[16,128]{1,0:T(8,128)S(1)}, u32[]{:S(2)}, u32[]{:S(2)}) collective-permute-start(f32[16,128]{1,0:T(8,128)S(1)} %get-tuple-element.49.refs_3_), channel_id=1, source_target_pairs={{0,1},{1,0},{2,3},{3,2},{4,5},{5,4},{6,7},{7,6},{8,9},{9,8},{10,11... | collective-permute-start | bytes 24584 | tf_op jit(solution)/shard_map/ppermute | solution.py:46
  36.1 1.9 %collective-permute-start.9 = (f32[16,128]{1,0:T(8,128)S(1)}, f32[16,128]{1,0:T(8,128)S(1)}, u32[]{:S(2)}, u32[]{:S(2)}) collective-permute-start(f32[16,128]{1,0:T(8,128)S(1)} %get-tuple-element.50.refs_4_), channel_id=1, source_target_pairs={{1,2},{2,1},{5,6},{6,5},{9,10},{10,9},{13,14},{14,13},{17,18},{18,... | collective-permute-start | bytes 24584 | tf_op jit(solution)/shard_map/ppermute | solution.py:46
  41.5 1.3 %copy-start.5 = (f32[18,144,128]{2,1,0:T(8,128)S(1)}, f32[18,144,128]{2,1,0:T(8,128)}, u32[]{:S(2)}) copy-start(f32[18,144,128]{2,1,0:T(8,128)} %copy-done.4) | copy-start | bytes 3981316
  42.8 1.3 %copy-start.9 = (f32[16,144,128]{2,1,0:T(8,128)S(1)}, f32[16,144,128]{2,1,0:T(8,128)}, u32[]{:S(2)}) copy-start(f32[16,144,128]{2,1,0:T(8,128)} %copy-done.8) | copy-start | bytes 3538948
  44.1 1.2 %copy-start.12 = (f32[17,128,128]{2,1,0:T(8,128)S(1)}, f32[17,128,128]{2,1,0:T(8,128)}, u32[]{:S(2)}) copy-start(f32[17,128,128]{2,1,0:T(8,128)} %copy-done.11) | copy-start | bytes 3342340
  45.3 1.2 %copy-start.15 = (f32[16,128,128]{2,1,0:T(8,128)S(1)}, f32[16,128,128]{2,1,0:T(8,128)}, u32[]{:S(2)}) copy-start(f32[16,128,128]{2,1,0:T(8,128)} %copy-done.14) | copy-start | bytes 3145732
  46.5 1.2 %copy-start.18 = (f32[16,128,128]{2,1,0:T(8,128)S(1)}, f32[16,128,128]{2,1,0:T(8,128)}, u32[]{:S(2)}) copy-start(f32[16,128,128]{2,1,0:T(8,128)} %copy-done.17) | copy-start | bytes 3145732
  47.8 1.2 %copy-start.23 = (f32[16,128,128]{2,1,0:T(8,128)S(1)}, f32[16,128,128]{2,1,0:T(8,128)}, u32[]{:S(2)}) copy-start(f32[16,128,128]{2,1,0:T(8,128)} %copy-done.22) | copy-start | bytes 3145732
  56.2 14.5 %collective-permute-start.10 = (f32[128,128]{1,0:T(8,128)S(1)}, f32[128,128]{1,0:T(8,128)S(1)}, u32[]{:S(2)}, u32[]{:S(2)}) collective-permute-start(f32[128,128]{1,0:T(8,128)S(1)} %get-tuple-element.58.refs_0_), channel_id=1, source_target_pairs={{0,8},{8,0},{16,24},{24,16},{1,9},{9,1},{17,25},{25,17},{2,10},{10... | collective-permute-start | bytes 196616 | tf_op jit(solution)/shard_map/ppermute | solution.py:46
  56.7 13.9 %collective-permute-start.11 = (f32[128,128]{1,0:T(8,128)S(1)}, f32[128,128]{1,0:T(8,128)S(1)}, u32[]{:S(2)}, u32[]{:S(2)}) collective-permute-start(f32[128,128]{1,0:T(8,128)S(1)} %get-tuple-element.59.refs_1_), channel_id=1, source_target_pairs={{8,16},{16,8},{9,17},{17,9},{10,18},{18,10},{11,19},{19,11},{12,20... | collective-permute-start | bytes 196616 | tf_op jit(solution)/shard_map/ppermute | solution.py:46
  57.4 13.2 %all-to-all-start.1 = ((f32[32,1,128]{2,1,0:T(1,128)}), f32[32,1,128]{2,1,0:T(1,128)S(1)}, u32[]{:S(2)}, u32[]{:S(2)}) async-start(f32[32,1,128]{2,1,0:T(1,128)} %bitcast.4), calls=%async_computation.1 | async-start | bytes 32768 | tf_op jit(solution)/shard_map/all_to_all | solution.py:339
  63.5 3.7 %collective-permute-start.12 = (f32[16,1,128]{2,1,0:T(1,128)S(1)}, f32[16,1,128]{2,1,0:T(1,128)S(1)}, u32[]{:S(2)}, u32[]{:S(2)}) collective-permute-start(f32[16,1,128]{2,1,0:T(1,128)S(1)} %get-tuple-element.60.refs_2_), channel_id=1, source_target_pairs={{0,4},{4,0},{1,5},{5,1},{2,6},{6,2},{3,7},{7,3},{8,12},{12,8},{9,1... | collective-permute-start | bytes 24584 | tf_op jit(solution)/shard_map/ppermute | solution.py:46
  65.3 1.9 %collective-permute-start.13 = (f32[16,128]{1,0:T(8,128)S(1)}, f32[16,128]{1,0:T(8,128)S(1)}, u32[]{:S(2)}, u32[]{:S(2)}) collective-permute-start(f32[16,128]{1,0:T(8,128)S(1)} %get-tuple-element.61.refs_3_), channel_id=1, source_target_pairs={{0,1},{1,0},{2,3},{3,2},{4,5},{5,4},{6,7},{7,6},{8,9},{9,8},{10,11... | collective-permute-start | bytes 24584 | tf_op jit(solution)/shard_map/ppermute | solution.py:46
  65.3 1.9 %collective-permute-start.14 = (f32[16,128]{1,0:T(8,128)S(1)}, f32[16,128]{1,0:T(8,128)S(1)}, u32[]{:S(2)}, u32[]{:S(2)}) collective-permute-start(f32[16,128]{1,0:T(8,128)S(1)} %get-tuple-element.62.refs_4_), channel_id=1, source_target_pairs={{1,2},{2,1},{5,6},{6,5},{9,10},{10,9},{13,14},{14,13},{17,18},{18,... | collective-permute-start | bytes 24584 | tf_op jit(solution)/shard_map/ppermute | solution.py:46
  70.6 1.3 %copy-start.7 = (f32[18,144,128]{2,1,0:T(8,128)S(1)}, f32[18,144,128]{2,1,0:T(8,128)}, u32[]{:S(2)}) copy-start(f32[18,144,128]{2,1,0:T(8,128)} %copy-done.6) | copy-start | bytes 3981316
  72.0 1.3 %copy-start.10 = (f32[16,144,128]{2,1,0:T(8,128)S(1)}, f32[16,144,128]{2,1,0:T(8,128)}, u32[]{:S(2)}) copy-start(f32[16,144,128]{2,1,0:T(8,128)} %copy-done.8) | copy-start | bytes 3538948
  73.2 1.2 %copy-start.13 = (f32[17,128,128]{2,1,0:T(8,128)S(1)}, f32[17,128,128]{2,1,0:T(8,128)}, u32[]{:S(2)}) copy-start(f32[17,128,128]{2,1,0:T(8,128)} %copy-done.11) | copy-start | bytes 3342340
  74.5 1.2 %copy-start.16 = (f32[16,128,128]{2,1,0:T(8,128)S(1)}, f32[16,128,128]{2,1,0:T(8,128)}, u32[]{:S(2)}) copy-start(f32[16,128,128]{2,1,0:T(8,128)} %copy-done.14) | copy-start | bytes 3145732
  (9 other events, 9.7 us)

commit v2 on v1

--- a/solution.py
+++ b/solution.py
@@ -6,6 +6,7 @@
 from jax.experimental.pallas import tpu as pltpu
 from jax.sharding import PartitionSpec as P
 
+
 ITERS = 3
 AXES = ("gx", "gy", "gz")
 OFF = 8
@@ -56,7 +57,7 @@
     return pltpu.VMEM(tuple(shape), F32)
 
 
-def call(kernel, out_shapes, args, out_specs=None, aliases=None, cost=(0, 0), name=None):
+def call(kernel, out_shapes, args, out_specs=None, aliases=None, cost=(0, 0)):
     vm = pl.BlockSpec(memory_space=pltpu.VMEM)
     return pl.pallas_call(
         kernel,
@@ -66,7 +67,6 @@
         input_output_aliases=aliases or {},
         compiler_params=pltpu.CompilerParams(vmem_limit_bytes=16 * 2**20),
         cost_estimate=pl.CostEstimate(flops=cost[0], bytes_accessed=cost[1], transcendentals=0),
-        name=name,
     )(*args)
 
 
@@ -213,7 +213,7 @@
 
 
 def totals(stats, cells):
-    rows, nz = stats.shape
+    _, nz = stats.shape
     both = jnp.sum(stats[...], axis=0, keepdims=True)
     low = lax.broadcasted_iota(jnp.int32, (1, nz), 1) < nz // 2
     squares = jnp.sum(jnp.where(low, both, 0.0), axis=1, keepdims=True)
@@ -221,7 +221,7 @@
     return jnp.sqrt(squares / cells + 1e-06), charges / cells
 
 
-def z_pair(plan, values, like):
+def z_pair(values, like):
     zero = jnp.zeros(like, F32)
     if not values:
         return (zero, zero)
@@ -237,7 +237,7 @@
     pad, wx, wy, diag, d, stats, zs = refs[2 * k + 6 : 2 * k + 13]
     faces = refs[2 * k + 13 : 3 * k + 13]
     gt, gw, turn = refs[3 * k + 13 :]
-    nx, ny, nz = d.shape
+    nx, ny, _ = d.shape
     fluxes, weights = [], []
     for (dim, s), mine, theirs in zip(plan.swaps, sent, got):
         after = after_of(AXES[dim])[s]
@@ -259,13 +259,13 @@
     sweep(
         plan,
         (pad, wx, wy, wz, diag, scr, src, d, stats, faces, gt, gw, turn),
-        z_pair(plan, fluxes, like),
-        z_pair(plan, weights, like),
-    )
-
-
-def advance(plan, pad, d, omega):
-    nx, ny, nz = d.shape
+        z_pair(fluxes, like),
+        z_pair(weights, like),
+    )
+
+
+def advance(pad, d, omega):
+    nx, ny, _ = d.shape
 
     def plane(x, carry):
         pad[x + 1, OFF : OFF + ny] += omega * d[x]
@@ -281,10 +281,10 @@
     pad, d, stats, zs = refs[2 * k + 10 : 2 * k + 14]
     faces = refs[2 * k + 14 : 3 * k + 14]
     gt, turn = refs[3 * k + 14 :]
-    nx, ny, nz = d.shape
+    nx, ny, _ = d.shape
     rms, _ = totals(seen, cells)
     omega = 1.0 / (1.0 + rms)
-    advance(plan, pad, d_old, omega)
+    advance(pad, d_old, omega)
     fluxes = []
     for (dim, s), mine, theirs in zip(plan.swaps, sent, got):
         after = after_of(AXES[dim])[s]
@@ -304,7 +304,7 @@
     sweep(
         plan,
         (pad, wx, wy, wz, diag, scr, src, d, stats, faces, gt, None, turn),
-        z_pair(plan, fluxes, (nx, ny)),
+        z_pair(fluxes, (nx, ny)),
         None,
     )
 
@@ -312,7 +312,7 @@
 def last_kernel(cells, *refs):
     seen = refs[:ITERS]
     pad, d, out, norms, charges = refs[ITERS:]
-    nx, ny, nz = d.shape
+    nx, ny, _ = d.shape
     for t in range(ITERS):
         rms, charge = totals(seen[t], cells)
         norms[t] = rms[0, 0]
@@ -346,7 +346,6 @@
         [vmem(s) for s in plan.face_shapes(shape, (2,))],
         (phi, eps),
         cost=cost,
-        name="faces",
     )
     got = plan.exchange(sent)
     pad, wx, wy, wz = call(
@@ -354,13 +353,12 @@
         [vmem(padded), vmem((nx + 1, ny, nz)), vmem((nx, ny + 2 * OFF, nz)), vmem(shape)],
         (phi, eps),
         cost=cost,
-        name="weights",
     )
     z_state = vmem((6, nx, ny))
     face_out = [vmem(s) for s in plan.face_shapes(shape)]
     vm = pl.BlockSpec(memory_space=pltpu.VMEM)
 
-    def sweep_call(kernel, outs, args, aliases, scratch, name):
+    def sweep_call(kernel, outs, args, aliases, scratch):
         return pl.pallas_call(
             kernel,
             out_shape=outs,
@@ -370,7 +368,6 @@
             input_output_aliases=aliases,
             compiler_params=pltpu.CompilerParams(vmem_limit_bytes=16 * 2**20),
             cost_estimate=pl.CostEstimate(flops=cost[0], bytes_accessed=cost[1], transcendentals=0),
-            name=name,
         )(*args)
 
     stats_shape = vmem((plan.count, nz))
@@ -381,21 +378,19 @@
         (*sent, *got, pad, wx, wy, wz, scr, src),
         {2 * k: 0, 2 * k + 1: 1, 2 * k + 2: 2},
         [flat, flat, turned],
-        "sweep_0",
     )
     pad, wx, wy, diag, d, stats, zs = outs[:7]
     sent = outs[7:]
     seen = []
-    for t in range(1, ITERS):
+    for _ in range(1, ITERS):
         got = plan.exchange(sent)
         seen.append(gather(stats))
         outs = sweep_call(
             functools.partial(next_kernel, plan, cells),
-            [vmem(padded), vmem(shape), stats_shape, z_state] + (face_out if t < ITERS - 1 else face_out),
+            [vmem(padded), vmem(shape), stats_shape, z_state] + face_out,
             (*sent, *got, seen[-1], d, pad, zs, wx, wy, wz, diag, scr, src),
             {2 * k + 2: 0},
             [flat, turned],
-            f"sweep_{t}",
         )
         pad, d, stats, zs = outs[:4]
         sent = outs[4:]
@@ -408,7 +403,6 @@
         (*seen, pad, d),
         out_specs=[vm, sm, sm],
         cost=cost,
-        name="finish",
     )
 
 

time: 96.7 us -> 96.7 us (level)
  no operation moved by 1% of the time
where the time goes in v2:
time: 96.7 us; the launch traced here: 95.8 us
  starting transfers between devices  30.2 us (31%)
  local copies, waits for them, and re-layouts  24.7 us (26%)
  Pallas kernels  18.9 us (20%)
  blocking collectives  11.2 us (12%)
  waiting for transfers between devices  10.1 us (10%)
    unnamed x48, local copies, waits for them, and re-layouts  24.7 us
    ppermute x15, starting transfers between devices, exchange(): out.append(lax.ppermute(face, AXES[d], swaps(self.sizes[d])[s]))  17.7 us
    pallas_call x3, Pallas kernels, sweep_call(): pl.pallas_call(kernel, out_shape=outs, in_specs=[vm] * len(args), out_spe...  15.1 us
    all_to_all x2, starting transfers between devices, gather(): return lax.all_to_all(stats, AXES, 0, 0, tiled=True)  12.5 us
    all_to_all x1, blocking collectives, gather(): return lax.all_to_all(stats, AXES, 0, 0, tiled=True)  11.2 us
    all_to_all x2, waiting for transfers between devices, gather(): return lax.all_to_all(stats, AXES, 0, 0, tiled=True)  6.91 us
    pallas_call x3, Pallas kernels, call(): pl.pallas_call(kernel, out_shape=out_shapes, in_specs=[vm] * len(args), o...  3.74 us
    ppermute x15, waiting for transfers between devices, exchange(): out.append(lax.ppermute(face, AXES[d], swaps(self.sizes[d])[s]))  3.16 us
  transfers between devices with their start and end apart: 17, of which 5 were waited for; matrix products, arithmetic and copies ran while one was open for 0% of the time, Pallas kernels for 2%

profile of v2, /device:TPU:0, one launch (start us, length us, event | category | flops | bytes accessed | tf_op | source)
XLA Modules:
  0.0 95.8 jit_solution(3342978196976359911)
XLA Ops:
  0.6 1.2 %copy-done = f32[16,128,128]{2,1,0:T(8,128)S(1)} copy-done((f32[16,128,128]{2,1,0:T(8,128)S(1)}, f32[16,128,128]{2,1,0:T(8,128)}, u32[]{:S(2)}) %copy-start) | copy-done | bytes 1048600
  1.9 1.2 %copy-done.1 = f32[16,128,128]{2,1,0:T(8,128)S(1)} copy-done((f32[16,128,128]{2,1,0:T(8,128)S(1)}, f32[16,128,128]{2,1,0:T(8,128)}, u32[]{:S(2)}) %copy-start.1) | copy-done | bytes 1048600
  3.7 3.0 %collective-permute-start.2 = (f32[2,16,1,128]{3,2,1,0:T(1,128)S(1)}, f32[2,16,1,128]{3,2,1,0:T(1,128)S(1)}, u32[]{:S(2)}, u32[]{:S(2)}) collective-permute-start(f32[2,16,1,128]{3,2,1,0:T(1,128)S(1)} %get-tuple-element.38.refs_2_), channel_id=1, source_target_pairs={{0,4},{4,0},{1,5},{5,1},{2,6},{6,2},{3,7},{7,3},{8,12},{12,8},{9,1... | collective-permute-start | bytes 49160 | tf_op jit(solution)/shard_map/ppermute | solution.py:47
  7.4 1.6 %collective-permute-start = (f32[2,128,128]{2,1,0:T(8,128)S(1)}, f32[2,128,128]{2,1,0:T(8,128)S(1)}, u32[]{:S(2)}, u32[]{:S(2)}) collective-permute-start(f32[2,128,128]{2,1,0:T(8,128)S(1)} %get-tuple-element.36.refs_0_), channel_id=1, source_target_pairs={{0,8},{8,0},{16,24},{24,16},{1,9},{9,1},{17,25},{25,17},{2,10},{10... | collective-permute-start | bytes 393224 | tf_op jit(solution)/shard_map/ppermute | solution.py:47
  9.8 1.9 %shard_map.68 = (f32[18,144,128]{2,1,0:T(8,128)S(1)}, f32[17,128,128]{2,1,0:T(8,128)S(1)}, f32[16,144,128]{2,1,0:T(8,128)S(1)}, f32[16,128,128]{2,1,0:T(8,128)S(1)}) custom-call(f32[16,128,128]{2,1,0:T(8,128)S(1)} %copy-done, f32[16,128,128]{2,1,0:T(8,128)S(1)} %copy-done.1), custom_call_target="tpu_custom_call" | custom-call | flops 3145728000 | bytes 1048576 | tf_op jit(solution)/shard_map/pallas_call | solution.py:62
  12.4 4.9 %shard_map.69 = (f32[18,144,128]{2,1,0:T(8,128)S(1)}, f32[17,128,128]{2,1,0:T(8,128)S(1)}, f32[16,144,128]{2,1,0:T(8,128)S(1)}, f32[16,128,128]{2,1,0:T(8,128)S(...) custom-call(f32[2,128,128]{2,1,0:T(8,128)S(1)} %get-tuple-element.36, ...), custom_call_target="tpu_custom_call", output_to_operand_aliasing={{0}: (10, {}), {1}: (11, {}), {2}: (12, {})} | custom-call | flops 3145728000 | bytes 1048576 | tf_op jit(solution)/shard_map/pallas_call | solution.py:362
  17.3 1.1 %copy-done.4 = f32[18,144,128]{2,1,0:T(8,128)} copy-done((f32[18,144,128]{2,1,0:T(8,128)}, f32[18,144,128]{2,1,0:T(8,128)S(1)}, u32[]{:S(2)}) %copy-start.4) | copy-done | bytes 1327128
  22.5 4.7 %collective-permute-start.5 = (f32[128,128]{1,0:T(8,128)S(1)}, f32[128,128]{1,0:T(8,128)S(1)}, u32[]{:S(2)}, u32[]{:S(2)}) collective-permute-start(f32[128,128]{1,0:T(8,128)S(1)} %get-tuple-element.46.refs_0_), channel_id=1, source_target_pairs={{0,8},{8,0},{16,24},{24,16},{1,9},{9,1},{17,25},{25,17},{2,10},{10... | collective-permute-start | bytes 196616 | tf_op jit(solution)/shard_map/ppermute | solution.py:47
  27.8 6.5 %all-to-all-start = ((f32[32,1,128]{2,1,0:T(1,128)}), f32[32,1,128]{2,1,0:T(1,128)S(1)}, u32[]{:S(2)}, u32[]{:S(2)}) async-start(f32[32,1,128]{2,1,0:T(1,128)} %bitcast.1), calls=%async_computation | async-start | bytes 32768 | tf_op jit(solution)/shard_map/all_to_all | solution.py:339
  34.3 1.8 %collective-permute-start.7 = (f32[16,1,128]{2,1,0:T(1,128)S(1)}, f32[16,1,128]{2,1,0:T(1,128)S(1)}, u32[]{:S(2)}, u32[]{:S(2)}) collective-permute-start(f32[16,1,128]{2,1,0:T(1,128)S(1)} %get-tuple-element.48.refs_2_), channel_id=1, source_target_pairs={{0,4},{4,0},{1,5},{5,1},{2,6},{6,2},{3,7},{7,3},{8,12},{12,8},{9,1... | collective-permute-start | bytes 24584 | tf_op jit(solution)/shard_map/ppermute | solution.py:47
  36.8 1.2 %collective-permute-done.7.refs_7_ = f32[16,1,128]{2,1,0:T(1,128)S(1)} collective-permute-done((f32[16,1,128]{2,1,0:T(1,128)S(1)}, f32[16,1,128]{2,1,0:T(1,128)S(1)}, u32[]{:S(2)}, u32[]{:S(2)}) %collective-permute-start.7) | collective-permute-done | bytes 8224 | tf_op jit(solution)/shard_map/ppermute | solution.py:47
  38.0 3.5 %all-to-all-done = f32[32,1,128]{2,1,0:T(1,128)S(1)} async-done(((f32[32,1,128]{2,1,0:T(1,128)}), f32[32,1,128]{2,1,0:T(1,128)S(1)}, u32[]{:S(2)}, u32[]{:S(2)}) %all-to-all-start) | async-done | bytes 16416 | tf_op jit(solution)/shard_map/all_to_all | solution.py:339
  41.5 1.3 %copy-done.5 = f32[18,144,128]{2,1,0:T(8,128)S(1)} copy-done((f32[18,144,128]{2,1,0:T(8,128)S(1)}, f32[18,144,128]{2,1,0:T(8,128)}, u32[]{:S(2)}) %copy-start.5) | copy-done | bytes 1327128
  42.8 1.3 %copy-done.9 = f32[16,144,128]{2,1,0:T(8,128)S(1)} copy-done((f32[16,144,128]{2,1,0:T(8,128)S(1)}, f32[16,144,128]{2,1,0:T(8,128)}, u32[]{:S(2)}) %copy-start.9) | copy-done | bytes 1179672
  44.1 1.2 %copy-done.12 = f32[17,128,128]{2,1,0:T(8,128)S(1)} copy-done((f32[17,128,128]{2,1,0:T(8,128)S(1)}, f32[17,128,128]{2,1,0:T(8,128)}, u32[]{:S(2)}) %copy-start.12) | copy-done | bytes 1114136
  45.3 1.2 %copy-done.15 = f32[16,128,128]{2,1,0:T(8,128)S(1)} copy-done((f32[16,128,128]{2,1,0:T(8,128)S(1)}, f32[16,128,128]{2,1,0:T(8,128)}, u32[]{:S(2)}) %copy-start.15) | copy-done | bytes 1048600
  46.5 1.2 %copy-done.18 = f32[16,128,128]{2,1,0:T(8,128)S(1)} copy-done((f32[16,128,128]{2,1,0:T(8,128)S(1)}, f32[16,128,128]{2,1,0:T(8,128)}, u32[]{:S(2)}) %copy-start.18) | copy-done | bytes 1048600
  47.8 1.2 %copy-done.23 = f32[16,128,128]{2,1,0:T(8,128)S(1)} copy-done((f32[16,128,128]{2,1,0:T(8,128)S(1)}, f32[16,128,128]{2,1,0:T(8,128)}, u32[]{:S(2)}) %copy-start.23) | copy-done | bytes 1048600
  49.0 5.1 %shard_map.70 = (f32[18,144,128]{2,1,0:T(8,128)S(1)}, f32[16,128,128]{2,1,0:T(8,128)S(1)}, f32[32,128]{1,0:T(8,128)}, f32[6,16,128]{2,1,0:T(8,128)S(1)}, f32[128...) custom-call(f32[128,128]{1,0:T(8,128)S(1)} %get-tuple-element.46.ref, ...), custom_call_target="tpu_custom_call", output_to_operand_aliasing={{0}: (12, {})} | custom-call | flops 3145728000 | bytes 1048576 | tf_op jit(solution)/shard_map/pallas_call | solution.py:362
  57.4 6.1 %all-to-all-start.1 = ((f32[32,1,128]{2,1,0:T(1,128)}), f32[32,1,128]{2,1,0:T(1,128)S(1)}, u32[]{:S(2)}, u32[]{:S(2)}) async-start(f32[32,1,128]{2,1,0:T(1,128)} %bitcast.4), calls=%async_computation.1 | async-start | bytes 32768 | tf_op jit(solution)/shard_map/all_to_all | solution.py:339
  63.5 1.8 %collective-permute-start.12 = (f32[16,1,128]{2,1,0:T(1,128)S(1)}, f32[16,1,128]{2,1,0:T(1,128)S(1)}, u32[]{:S(2)}, u32[]{:S(2)}) collective-permute-start(f32[16,1,128]{2,1,0:T(1,128)S(1)} %get-tuple-element.60.refs_2_), channel_id=1, source_target_pairs={{0,4},{4,0},{1,5},{5,1},{2,6},{6,2},{3,7},{7,3},{8,12},{12,8},{9,1... | collective-permute-start | bytes 24584 | tf_op jit(solution)/shard_map/ppermute | solution.py:47
  66.0 1.2 %collective-permute-done.12.refs_7_ = f32[16,1,128]{2,1,0:T(1,128)S(1)} collective-permute-done((f32[16,1,128]{2,1,0:T(1,128)S(1)}, f32[16,1,128]{2,1,0:T(1,128)S(1)}, u32[]{:S(2)}, u32[]{:S(2)}) %collective-permute-start.12) | collective-permute-done | bytes 8224 | tf_op jit(solution)/shard_map/ppermute | solution.py:47
  67.2 3.5 %all-to-all-done.1 = f32[32,1,128]{2,1,0:T(1,128)S(1)} async-done(((f32[32,1,128]{2,1,0:T(1,128)}), f32[32,1,128]{2,1,0:T(1,128)S(1)}, u32[]{:S(2)}, u32[]{:S(2)}) %all-to-all-start.1) | async-done | bytes 16416 | tf_op jit(solution)/shard_map/all_to_all | solution.py:339
  70.6 1.3 %copy-done.7 = f32[18,144,128]{2,1,0:T(8,128)S(1)} copy-done((f32[18,144,128]{2,1,0:T(8,128)S(1)}, f32[18,144,128]{2,1,0:T(8,128)}, u32[]{:S(2)}) %copy-start.7) | copy-done | bytes 1327128
  72.0 1.3 %copy-done.10 = f32[16,144,128]{2,1,0:T(8,128)S(1)} copy-done((f32[16,144,128]{2,1,0:T(8,128)S(1)}, f32[16,144,128]{2,1,0:T(8,128)}, u32[]{:S(2)}) %copy-start.10) | copy-done | bytes 1179672
  73.2 1.2 %copy-done.13 = f32[17,128,128]{2,1,0:T(8,128)S(1)} copy-done((f32[17,128,128]{2,1,0:T(8,128)S(1)}, f32[17,128,128]{2,1,0:T(8,128)}, u32[]{:S(2)}) %copy-start.13) | copy-done | bytes 1114136
  74.5 1.2 %copy-done.16 = f32[16,128,128]{2,1,0:T(8,128)S(1)} copy-done((f32[16,128,128]{2,1,0:T(8,128)S(1)}, f32[16,128,128]{2,1,0:T(8,128)}, u32[]{:S(2)}) %copy-start.16) | copy-done | bytes 1048600
  75.7 1.2 %copy-done.19 = f32[16,128,128]{2,1,0:T(8,128)S(1)} copy-done((f32[16,128,128]{2,1,0:T(8,128)S(1)}, f32[16,128,128]{2,1,0:T(8,128)}, u32[]{:S(2)}) %copy-start.19) | copy-done | bytes 1048600
  76.9 1.2 %copy-done.21 = f32[16,128,128]{2,1,0:T(8,128)S(1)} copy-done((f32[16,128,128]{2,1,0:T(8,128)S(1)}, f32[16,128,128]{2,1,0:T(8,128)}, u32[]{:S(2)}) %copy-start.21) | copy-done | bytes 1048600
  78.2 5.1 %shard_map.71 = (f32[18,144,128]{2,1,0:T(8,128)S(1)}, f32[16,128,128]{2,1,0:T(8,128)S(1)}, f32[32,128]{1,0:T(8,128)S(1)}, f32[6,16,128]{2,1,0:T(8,128)}, f32[128...) custom-call(f32[128,128]{1,0:T(8,128)S(1)} %get-tuple-element.58.ref, ...), custom_call_target="tpu_custom_call", output_to_operand_aliasing={{0}: (12, {})} | custom-call | flops 3145728000 | bytes 1048576 | tf_op jit(solution)/shard_map/pallas_call | solution.py:362
  83.3 11.2 %all_to_all.33 = f32[32,1,128]{2,1,0:T(1,128)S(1)} all-to-all(f32[32,1,128]{2,1,0:T(1,128)S(1)} %bitcast.16), channel_id=1, replica_groups=mesh['gx'=4,'gy'=2,'gz'=4] {'gx','gy','gz'}, dimensions={0} | all-to-all | bytes 32768 | tf_op jit(solution)/shard_map/all_to_all | solution.py:339
  94.5 1.3 %shard_map.72 = (f32[16,128,128]{2,1,0:T(8,128)}, f32[3]{0:T(128)}, f32[3]{0:T(128)}) custom-call(f32[32,128]{1,0:T(8,128)S(1)} %bitcast.13, f32[32,128]{1,0:T(8,128)S(1)} %bitcast.15, f32[32,128]{1,0:T(8,128)S(1)} %bitcast.17, f32[18,144,128]{2,1,0:T(8,128)S(1)} %get-tuple-element.67.refs_3_, f32[16,128,128]{2,1,0:T(8,128)S(1)} %get-tuple-element.68.refs_4_), custom_call_target="tpu_custom_call" | custom-call | flops 3145728000 | bytes 1048576 | tf_op jit(solution)/shard_map/pallas_call | solution.py:62
  (57 shorter events, 12.1 us)
Async XLA Ops:
  0.6 1.2 %copy-start = (f32[16,128,128]{2,1,0:T(8,128)S(1)}, f32[16,128,128]{2,1,0:T(8,128)}, u32[]{:S(2)}) copy-start(f32[16,128,128]{2,1,0:T(8,128)} %phi.3) | copy-start | bytes 3145732
  3.7 8.0 %collective-permute-start.2 = (f32[2,16,1,128]{3,2,1,0:T(1,128)S(1)}, f32[2,16,1,128]{3,2,1,0:T(1,128)S(1)}, u32[]{:S(2)}, u32[]{:S(2)}) collective-permute-start(f32[2,16,1,128]{3,2,1,0:T(1,128)S(1)} %get-tuple-element.38.refs_2_), channel_id=1, source_target_pairs={{0,4},{4,0},{1,5},{5,1},{2,6},{6,2},{3,7},{7,3},{8,12},{12,8},{9,1... | collective-permute-start | bytes 49160 | tf_op jit(solution)/shard_map/ppermute | solution.py:47
  6.7 5.0 %collective-permute-start.3 = (f32[2,16,128]{2,1,0:T(8,128)S(1)}, f32[2,16,128]{2,1,0:T(8,128)S(1)}, u32[]{:S(2)}, u32[]{:S(2)}) collective-permute-start(f32[2,16,128]{2,1,0:T(8,128)S(1)} %get-tuple-element.39.refs_3_), channel_id=1, source_target_pairs={{0,1},{1,0},{2,3},{3,2},{4,5},{5,4},{6,7},{7,6},{8,9},{9,8},{10,11... | collective-permute-start | bytes 49160 | tf_op jit(solution)/shard_map/ppermute | solution.py:47
  6.7 5.0 %collective-permute-start.4 = (f32[2,16,128]{2,1,0:T(8,128)S(1)}, f32[2,16,128]{2,1,0:T(8,128)S(1)}, u32[]{:S(2)}, u32[]{:S(2)}) collective-permute-start(f32[2,16,128]{2,1,0:T(8,128)S(1)} %get-tuple-element.40.refs_4_), channel_id=1, source_target_pairs={{1,2},{2,1},{5,6},{6,5},{9,10},{10,9},{13,14},{14,13},{17,18},{18,... | collective-permute-start | bytes 49160 | tf_op jit(solution)/shard_map/ppermute | solution.py:47
  7.4 5.0 %collective-permute-start = (f32[2,128,128]{2,1,0:T(8,128)S(1)}, f32[2,128,128]{2,1,0:T(8,128)S(1)}, u32[]{:S(2)}, u32[]{:S(2)}) collective-permute-start(f32[2,128,128]{2,1,0:T(8,128)S(1)} %get-tuple-element.36.refs_0_), channel_id=1, source_target_pairs={{0,8},{8,0},{16,24},{24,16},{1,9},{9,1},{17,25},{25,17},{2,10},{10... | collective-permute-start | bytes 393224 | tf_op jit(solution)/shard_map/ppermute | solution.py:47
  9.0 3.4 %copy-start.2 = (f32[16,128,128]{2,1,0:T(8,128)S(1)}, f32[16,128,128]{2,1,0:T(8,128)}, u32[]{:S(2)}) copy-start(f32[16,128,128]{2,1,0:T(8,128)} %refs_18_.3) | copy-start | bytes 3145732
  9.0 3.4 %copy-start.3 = (f32[16,128,128]{2,1,0:T(8,128)S(1)}, f32[16,128,128]{2,1,0:T(8,128)}, u32[]{:S(2)}) copy-start(f32[16,128,128]{2,1,0:T(8,128)} %refs_19_.3) | copy-start | bytes 3145732
  9.0 3.4 %collective-permute-start.1 = (f32[2,128,128]{2,1,0:T(8,128)S(1)}, f32[2,128,128]{2,1,0:T(8,128)S(1)}, u32[]{:S(2)}, u32[]{:S(2)}) collective-permute-start(f32[2,128,128]{2,1,0:T(8,128)S(1)} %get-tuple-element.37.refs_1_), channel_id=1, source_target_pairs={{8,16},{16,8},{9,17},{17,9},{10,18},{18,10},{11,19},{19,11},{12,20... | collective-permute-start | bytes 393224 | tf_op jit(solution)/shard_map/ppermute | solution.py:47
  11.7 5.6 %copy-start.14 = (f32[16,128,128]{2,1,0:T(8,128)}, f32[16,128,128]{2,1,0:T(8,128)S(1)}, u32[]{:S(2)}) copy-start(f32[16,128,128]{2,1,0:T(8,128)S(1)} %get-tuple-element.44.refs_13_.refs_16_) | copy-start | bytes 3145732
  22.5 19.0 %collective-permute-start.5 = (f32[128,128]{1,0:T(8,128)S(1)}, f32[128,128]{1,0:T(8,128)S(1)}, u32[]{:S(2)}, u32[]{:S(2)}) collective-permute-start(f32[128,128]{1,0:T(8,128)S(1)} %get-tuple-element.46.refs_0_), channel_id=1, source_target_pairs={{0,8},{8,0},{16,24},{24,16},{1,9},{9,1},{17,25},{25,17},{2,10},{10... | collective-permute-start | bytes 196616 | tf_op jit(solution)/shard_map/ppermute | solution.py:47
  27.2 14.3 %collective-permute-start.6 = (f32[128,128]{1,0:T(8,128)S(1)}, f32[128,128]{1,0:T(8,128)S(1)}, u32[]{:S(2)}, u32[]{:S(2)}) collective-permute-start(f32[128,128]{1,0:T(8,128)S(1)} %get-tuple-element.47.refs_1_), channel_id=1, source_target_pairs={{8,16},{16,8},{9,17},{17,9},{10,18},{18,10},{11,19},{19,11},{12,20... | collective-permute-start | bytes 196616 | tf_op jit(solution)/shard_map/ppermute | solution.py:47
  27.8 13.6 %all-to-all-start = ((f32[32,1,128]{2,1,0:T(1,128)}), f32[32,1,128]{2,1,0:T(1,128)S(1)}, u32[]{:S(2)}, u32[]{:S(2)}) async-start(f32[32,1,128]{2,1,0:T(1,128)} %bitcast.1), calls=%async_computation | async-start | bytes 32768 | tf_op jit(solution)/shard_map/all_to_all | solution.py:339
  34.3 3.7 %collective-permute-start.7 = (f32[16,1,128]{2,1,0:T(1,128)S(1)}, f32[16,1,128]{2,1,0:T(1,128)S(1)}, u32[]{:S(2)}, u32[]{:S(2)}) collective-permute-start(f32[16,1,128]{2,1,0:T(1,128)S(1)} %get-tuple-element.48.refs_2_), channel_id=1, source_target_pairs={{0,4},{4,0},{1,5},{5,1},{2,6},{6,2},{3,7},{7,3},{8,12},{12,8},{9,1... | collective-permute-start | bytes 24584 | tf_op jit(solution)/shard_map/ppermute | solution.py:47
  36.1 1.9 %collective-permute-start.8 = (f32[16,128]{1,0:T(8,128)S(1)}, f32[16,128]{1,0:T(8,128)S(1)}, u32[]{:S(2)}, u32[]{:S(2)}) collective-permute-start(f32[16,128]{1,0:T(8,128)S(1)} %get-tuple-element.49.refs_3_), channel_id=1, source_target_pairs={{0,1},{1,0},{2,3},{3,2},{4,5},{5,4},{6,7},{7,6},{8,9},{9,8},{10,11... | collective-permute-start | bytes 24584 | tf_op jit(solution)/shard_map/ppermute | solution.py:47
  36.1 1.9 %collective-permute-start.9 = (f32[16,128]{1,0:T(8,128)S(1)}, f32[16,128]{1,0:T(8,128)S(1)}, u32[]{:S(2)}, u32[]{:S(2)}) collective-permute-start(f32[16,128]{1,0:T(8,128)S(1)} %get-tuple-element.50.refs_4_), channel_id=1, source_target_pairs={{1,2},{2,1},{5,6},{6,5},{9,10},{10,9},{13,14},{14,13},{17,18},{18,... | collective-permute-start | bytes 24584 | tf_op jit(solution)/shard_map/ppermute | solution.py:47
  41.5 1.3 %copy-start.5 = (f32[18,144,128]{2,1,0:T(8,128)S(1)}, f32[18,144,128]{2,1,0:T(8,128)}, u32[]{:S(2)}) copy-start(f32[18,144,128]{2,1,0:T(8,128)} %copy-done.4) | copy-start | bytes 3981316
  42.8 1.3 %copy-start.9 = (f32[16,144,128]{2,1,0:T(8,128)S(1)}, f32[16,144,128]{2,1,0:T(8,128)}, u32[]{:S(2)}) copy-start(f32[16,144,128]{2,1,0:T(8,128)} %copy-done.8) | copy-start | bytes 3538948
  44.1 1.2 %copy-start.12 = (f32[17,128,128]{2,1,0:T(8,128)S(1)}, f32[17,128,128]{2,1,0:T(8,128)}, u32[]{:S(2)}) copy-start(f32[17,128,128]{2,1,0:T(8,128)} %copy-done.11) | copy-start | bytes 3342340
  45.3 1.2 %copy-start.15 = (f32[16,128,128]{2,1,0:T(8,128)S(1)}, f32[16,128,128]{2,1,0:T(8,128)}, u32[]{:S(2)}) copy-start(f32[16,128,128]{2,1,0:T(8,128)} %copy-done.14) | copy-start | bytes 3145732
  46.5 1.2 %copy-start.18 = (f32[16,128,128]{2,1,0:T(8,128)S(1)}, f32[16,128,128]{2,1,0:T(8,128)}, u32[]{:S(2)}) copy-start(f32[16,128,128]{2,1,0:T(8,128)} %copy-done.17) | copy-start | bytes 3145732
  47.8 1.2 %copy-start.23 = (f32[16,128,128]{2,1,0:T(8,128)S(1)}, f32[16,128,128]{2,1,0:T(8,128)}, u32[]{:S(2)}) copy-start(f32[16,128,128]{2,1,0:T(8,128)} %copy-done.22) | copy-start | bytes 3145732
  56.2 14.5 %collective-permute-start.10 = (f32[128,128]{1,0:T(8,128)S(1)}, f32[128,128]{1,0:T(8,128)S(1)}, u32[]{:S(2)}, u32[]{:S(2)}) collective-permute-start(f32[128,128]{1,0:T(8,128)S(1)} %get-tuple-element.58.refs_0_), channel_id=1, source_target_pairs={{0,8},{8,0},{16,24},{24,16},{1,9},{9,1},{17,25},{25,17},{2,10},{10... | collective-permute-start | bytes 196616 | tf_op jit(solution)/shard_map/ppermute | solution.py:47
  56.7 13.9 %collective-permute-start.11 = (f32[128,128]{1,0:T(8,128)S(1)}, f32[128,128]{1,0:T(8,128)S(1)}, u32[]{:S(2)}, u32[]{:S(2)}) collective-permute-start(f32[128,128]{1,0:T(8,128)S(1)} %get-tuple-element.59.refs_1_), channel_id=1, source_target_pairs={{8,16},{16,8},{9,17},{17,9},{10,18},{18,10},{11,19},{19,11},{12,20... | collective-permute-start | bytes 196616 | tf_op jit(solution)/shard_map/ppermute | solution.py:47
  57.4 13.2 %all-to-all-start.1 = ((f32[32,1,128]{2,1,0:T(1,128)}), f32[32,1,128]{2,1,0:T(1,128)S(1)}, u32[]{:S(2)}, u32[]{:S(2)}) async-start(f32[32,1,128]{2,1,0:T(1,128)} %bitcast.4), calls=%async_computation.1 | async-start | bytes 32768 | tf_op jit(solution)/shard_map/all_to_all | solution.py:339
  63.5 3.7 %collective-permute-start.12 = (f32[16,1,128]{2,1,0:T(1,128)S(1)}, f32[16,1,128]{2,1,0:T(1,128)S(1)}, u32[]{:S(2)}, u32[]{:S(2)}) collective-permute-start(f32[16,1,128]{2,1,0:T(1,128)S(1)} %get-tuple-element.60.refs_2_), channel_id=1, source_target_pairs={{0,4},{4,0},{1,5},{5,1},{2,6},{6,2},{3,7},{7,3},{8,12},{12,8},{9,1... | collective-permute-start | bytes 24584 | tf_op jit(solution)/shard_map/ppermute | solution.py:47
  65.3 1.9 %collective-permute-start.13 = (f32[16,128]{1,0:T(8,128)S(1)}, f32[16,128]{1,0:T(8,128)S(1)}, u32[]{:S(2)}, u32[]{:S(2)}) collective-permute-start(f32[16,128]{1,0:T(8,128)S(1)} %get-tuple-element.61.refs_3_), channel_id=1, source_target_pairs={{0,1},{1,0},{2,3},{3,2},{4,5},{5,4},{6,7},{7,6},{8,9},{9,8},{10,11... | collective-permute-start | bytes 24584 | tf_op jit(solution)/shard_map/ppermute | solution.py:47
  65.3 1.9 %collective-permute-start.14 = (f32[16,128]{1,0:T(8,128)S(1)}, f32[16,128]{1,0:T(8,128)S(1)}, u32[]{:S(2)}, u32[]{:S(2)}) collective-permute-start(f32[16,128]{1,0:T(8,128)S(1)} %get-tuple-element.62.refs_4_), channel_id=1, source_target_pairs={{1,2},{2,1},{5,6},{6,5},{9,10},{10,9},{13,14},{14,13},{17,18},{18,... | collective-permute-start | bytes 24584 | tf_op jit(solution)/shard_map/ppermute | solution.py:47
  70.6 1.3 %copy-start.7 = (f32[18,144,128]{2,1,0:T(8,128)S(1)}, f32[18,144,128]{2,1,0:T(8,128)}, u32[]{:S(2)}) copy-start(f32[18,144,128]{2,1,0:T(8,128)} %copy-done.6) | copy-start | bytes 3981316
  72.0 1.3 %copy-start.10 = (f32[16,144,128]{2,1,0:T(8,128)S(1)}, f32[16,144,128]{2,1,0:T(8,128)}, u32[]{:S(2)}) copy-start(f32[16,144,128]{2,1,0:T(8,128)} %copy-done.8) | copy-start | bytes 3538948
  73.2 1.2 %copy-start.13 = (f32[17,128,128]{2,1,0:T(8,128)S(1)}, f32[17,128,128]{2,1,0:T(8,128)}, u32[]{:S(2)}) copy-start(f32[17,128,128]{2,1,0:T(8,128)} %copy-done.11) | copy-start | bytes 3342340
  75.7 1.2 %copy-start.19 = (f32[16,128,128]{2,1,0:T(8,128)S(1)}, f32[16,128,128]{2,1,0:T(8,128)}, u32[]{:S(2)}) copy-start(f32[16,128,128]{2,1,0:T(8,128)} %copy-done.17) | copy-start | bytes 3145732
  76.9 1.2 %copy-start.21 = (f32[16,128,128]{2,1,0:T(8,128)S(1)}, f32[16,128,128]{2,1,0:T(8,128)}, u32[]{:S(2)}) copy-start(f32[16,128,128]{2,1,0:T(8,128)} %copy-done.20) | copy-start | bytes 3145732
  (9 other events, 9.7 us)

commit v3 on v2

v3 whole, which is shorter than its diff:
```python
import functools
import jax
import jax.numpy as jnp
from jax import lax
from jax.experimental import pallas as pl
from jax.experimental.pallas import tpu as pltpu
from jax.sharding import PartitionSpec as P


ITERS = 3
AXES = ("gx", "gy", "gz")
OFF = 8
CHUNK = 32
LOG2E = 1.4426950408889634
F32 = jnp.float32


def harmonic(left, right):
    total = left + right
    return 2.0 * left * right / jnp.where(total > 0, total, 1.0)


def sides_of(size):
    return 0 if size < 2 else 1 if size == 2 else 2


def swaps(size):
    a = [(i, i ^ 1) for i in range(size) if i ^ 1 < size]
    b = [(i, i + 1) for i in range(1, size - 1, 2)]
    return (a, b + [(j, i) for i, j in b])


def after_of(axis):
    odd = lax.rem(lax.axis_index(axis), 2)
    return (1 - odd, odd)


class Plan:
    def __init__(self, mesh):
        self.sizes = [mesh.shape[a] for a in AXES]
        self.count = self.sizes[0] * self.sizes[1] * self.sizes[2]
        self.swaps = [(d, s) for d in range(3) for s in range(sides_of(self.sizes[d]))]

    def exchange(self, faces):
        out = []
        for (d, s), face in zip(self.swaps, faces):
            out.append(lax.ppermute(face, AXES[d], swaps(self.sizes[d])[s]))
        return out

    def face_shapes(self, shape, lead=()):
        nx, ny, nz = shape
        kinds = ((ny, nz), (nx, 1, nz), (nx, ny))
        return [lead + kinds[d] for d, _ in self.swaps]


def vmem(shape):
    return pltpu.VMEM(tuple(shape), F32)


def faces_kernel(plan, phi_in, eps_in, *refs):
    outs, (phi, eps, sems) = refs[:-3], refs[-3:]
    copies = [
        pltpu.make_async_copy(phi_in, phi, sems.at[0]),
        pltpu.make_async_copy(eps_in, eps, sems.at[1]),
    ]
    for copy in copies:
        copy.start()
    nx, ny, nz = phi.shape
    z_faces = [(after_of("gz")[s], o) for (d, s), o in zip(plan.swaps, outs) if d == 2]
    for k, ref in enumerate((phi, eps)):
        copies[k].wait()
        for (d, s), out in zip(plan.swaps, outs):
            after = after_of(AXES[d])[s]
            if d == 0:
                out[k] = ref[after * (nx - 1)]
            elif d == 1:
                out[k] = ref[:, pl.ds(after * (ny - 1), 1), :]
        if z_faces:
            for x in range(nx):
                flipped = ref[x].T
                first, last = flipped[0:1], flipped[nz - 1 : nz]
                for after, out in z_faces:
                    out[k, x : x + 1, :] = jnp.where(after == 1, last, first)


def weights_kernel(phi, eps, pad, wx, wy, wz, wz_low):
    nx, ny, nz = phi.shape
    lane = lax.broadcasted_iota(jnp.int32, (CHUNK, nz), 1)
    zero = jnp.zeros((ny, nz), F32)
    pad[0] = jnp.zeros(pad.shape[1:], F32)
    pad[nx + 1] = jnp.zeros(pad.shape[1:], F32)
    wx[0] = zero
    wx[nx] = zero

    def plane(x, carry):
        edge = jnp.zeros((OFF, nz), F32)
        pad[x + 1, 0:OFF] = edge
        pad[x + 1, OFF + ny : 2 * OFF + ny] = edge
        wy[x, 0:OFF] = edge
        wy[x, OFF + ny : 2 * OFF + ny] = edge
        for y in range(0, ny, CHUNK):
            rows = pl.ds(y, CHUNK)
            here = eps[x, rows]
            pad[x + 1, OFF + y : OFF + y + CHUNK] = phi[x, rows]
            high = harmonic(here, pltpu.roll(here, nz - 1, 1))
            low = harmonic(here, pltpu.roll(here, 1, 1))
            wz[x, rows] = jnp.where(lane == nz - 1, 0.0, high)
            wz_low[x, rows] = jnp.where(lane == 0, 0.0, low)
            if y + CHUNK < ny:
                wy[x, OFF + y : OFF + y + CHUNK] = harmonic(here, eps[x, y + 1 : y + 1 + CHUNK])
            else:
                wy[x, OFF + y : OFF + y + CHUNK - 1] = harmonic(
                    eps[x, y : y + CHUNK - 1], eps[x, y + 1 : y + CHUNK]
                )
                wy[x, OFF + ny - 1 : OFF + ny] = jnp.zeros((1, nz), F32)
        return carry

    lax.fori_loop(0, nx, plane, 0)

    def deep(x, carry):
        for y in range(0, ny, CHUNK):
            wx[x + 1, y : y + CHUNK] = harmonic(eps[x, y : y + CHUNK], eps[x + 1, y : y + CHUNK])
        return carry

    lax.fori_loop(0, nx - 1, deep, 0)


def spread(scratch, before, after):
    nz = scratch.shape[0]
    nx = before.shape[0]
    for x in range(nx):
        scratch[2 * x : 2 * x + 1] = before[x : x + 1]
        row = (2 * x - 1) % nz
        scratch[row : row + 1] = after[x : x + 1]
    return scratch[...].T


def sweep(plan, refs, z_flux, z_weight, step):
    pad, wx, wy, wz, wz_low, diag, scr, src, d, stats, faces, scratch = refs
    gt, gw, turn, z_high, z_low, z_rows = scratch
    nx, ny, nz = src.shape
    lane = lax.broadcasted_iota(jnp.int32, (CHUNK, nz), 1)
    edge = (lane == 0) | (lane == nz - 1)
    first = z_weight is not None
    turn[...] = jnp.zeros(turn.shape, F32)
    gt[...] = spread(turn, *z_flux)
    if first:
        gw[...] = spread(turn, *z_weight)
    z_faces = [(after_of("gz")[s], o) for (dim, s), o in zip(plan.swaps, faces) if dim == 2]

    def ready(x):
        for y in range(0, ny, CHUNK):
            rows = pl.ds(y, CHUNK)
            mine = pl.ds(OFF + y, CHUNK)
            if step is None:
                c = pad[x + 1, mine]
            else:
                old, change, omega = step
                c = old[x + 1, mine] + omega * change[x + 1, rows]
                pad[x + 1, mine] = c
            z_high[x, rows] = pltpu.roll(c, nz - 1, 1)
            z_low[x, rows] = pltpu.roll(c, 1, 1)

    def turned(x):
        flipped = d[x + 1].T
        head, tail = flipped[0:1], flipped[nz - 1 : nz]
        for k, (after, _) in enumerate(z_faces):
            z_rows[k, pl.ds(x + 8, 1), :] = jnp.where(after == 1, tail, head)

    def solve(x, sums):
        squares, charges = sums
        shift = lax.rem(nz - 2 * x, nz)
        for y in range(0, ny, CHUNK):
            rows = pl.ds(y, CHUNK)
            c = pad[x + 1, OFF + y : OFF + y + CHUNK]
            w_xp, w_xm = wx[x + 1, rows], wx[x, rows]
            w_yp = wy[x, OFF + y : OFF + y + CHUNK]
            w_ym = wy[x, OFF - 1 + y : OFF - 1 + y + CHUNK]
            w_zp, w_zm = wz[x, rows], wz_low[x, rows]
            flux = w_xp * (c - pad[x + 2, OFF + y : OFF + y + CHUNK])
            flux += w_xm * (c - pad[x, OFF + y : OFF + y + CHUNK])
            flux += w_yp * (c - pad[x + 1, OFF + 1 + y : OFF + 1 + y + CHUNK])
            flux += w_ym * (c - pad[x + 1, OFF - 1 + y : OFF - 1 + y + CHUNK])
            flux += w_zp * (c - z_high[x, rows])
            flux += w_zm * (c - z_low[x, rows])
            flux += jnp.where(edge, pltpu.roll(gt[rows], shift, 1), 0.0)
            if first:
                total = (w_xp + w_xm) + (w_yp + w_ym) + (w_zp + w_zm)
                total += jnp.where(edge, pltpu.roll(gw[rows], shift, 1), 0.0)
                diag[x, rows] = total
            else:
                total = diag[x, rows]
            up = jnp.exp2(c * LOG2E)
            down = jnp.exp2(c * -LOG2E)
            c2 = c * c
            series = c * (1.0 + c2 * (1.0 / 6.0 + c2 * (1.0 / 120.0)))
            s = scr[x, rows]
            charge = s * jnp.where(c2 < 0.0625, series, 0.5 * (up - down))
            res = src[x, rows] - flux - charge
            total = total + s * (0.5 * (up + down))
            d[x + 1, rows] = res / jnp.where(total > 0, total, 1.0)
            squares += jnp.sum((res * res).reshape(CHUNK // 8, 8, nz), axis=0)
            charges += jnp.sum(charge.reshape(CHUNK // 8, 8, nz), axis=0)
        return (squares, charges)

    def full(x, sums):
        if z_faces:
            turned(x - 1)
        ready(x + 2)
        return solve(x, sums)

    def tail(x, sums):
        if z_faces:
            turned(x - 1)
        return solve(x, sums)

    ahead = min(2, nx)
    for x in range(ahead):
        ready(x)
    if z_faces:
        d[0] = jnp.zeros((ny, nz), F32)
    none = jnp.zeros((8, nz), F32)
    sums = lax.fori_loop(0, nx - ahead, full, (none, none))
    squares, charges = lax.fori_loop(nx - ahead, nx, tail, sums)
    half = nz // 2
    a = jnp.sum(squares, axis=0, keepdims=True)
    b = jnp.sum(charges, axis=0, keepdims=True)
    a = a + pltpu.roll(a, half, 1)
    b = b + pltpu.roll(b, half, 1)
    low = lax.broadcasted_iota(jnp.int32, (1, nz), 1) < half
    stats[...] = jnp.broadcast_to(jnp.where(low, a, b), stats.shape)
    if z_faces:
        turned(nx - 1)
        for k, (_, out) in enumerate(z_faces):
            out[...] = z_rows[k, 8 : 8 + nx]
    if faces:
        for (dim, s), out in zip(plan.swaps, faces):
            after = after_of(AXES[dim])[s]
            if dim == 0:
                out[...] = d[1 + after * (nx - 1)]
            elif dim == 1:
                out[...] = d[1 : nx + 1, pl.ds(after * (ny - 1), 1), :]


def totals(stats, cells):
    _, nz = stats.shape
    both = jnp.sum(stats[...], axis=0, keepdims=True)
    low = lax.broadcasted_iota(jnp.int32, (1, nz), 1) < nz // 2
    squares = jnp.sum(jnp.where(low, both, 0.0), axis=1, keepdims=True)
    charges = jnp.sum(jnp.where(low, 0.0, both), axis=1, keepdims=True)
    return jnp.sqrt(squares / cells + 1e-06), charges / cells


def z_pair(values, like):
    zero = jnp.zeros(like, F32)
    if not values:
        return (zero, zero)
    one = after_of("gz")[0] == 1
    other = values[1] if len(values) > 1 else zero
    return (jnp.where(one, other, values[0]), jnp.where(one, values[0], other))


def first_kernel(plan, *refs):
    k = len(plan.swaps)
    sent, got = refs[:k], refs[k : 2 * k]
    _, _, _, wz, wz_low, scr, src = refs[2 * k : 2 * k + 7]
    pad, wx, wy, diag, d, stats, zs = refs[2 * k + 7 : 2 * k + 14]
    faces = refs[2 * k + 14 : 3 * k + 14]
    scratch = refs[3 * k + 14 :]
    nx, ny, _ = src.shape
    fluxes, weights = [], []
    for (dim, s), mine, theirs in zip(plan.swaps, sent, got):
        after = after_of(AXES[dim])[s]
        if dim == 0:
            pad[after * (nx + 1), OFF : OFF + ny] = theirs[0]
            wx[after * nx] = harmonic(mine[1], theirs[1])
        elif dim == 1:
            row = OFF - 1 + after * (ny + 1)
            pad[1 : nx + 1, pl.ds(row, 1), :] = theirs[0]
            wy[:, pl.ds(OFF - 1 + after * ny, 1), :] = harmonic(mine[1], theirs[1])
        else:
            w = harmonic(mine[1], theirs[1])
            zs[3 * s] = mine[0]
            zs[3 * s + 1] = theirs[0]
            zs[3 * s + 2] = w
            weights.append(w)
            fluxes.append(w * (mine[0] - theirs[0]))
    like = (nx, ny)
    sweep(
        plan,
        (pad, wx, wy, wz, wz_low, diag, scr, src, d, stats, faces, scratch),
        z_pair(fluxes, like),
        z_pair(weights, like),
        None,
    )


def next_kernel(plan, cells, final, *refs):
    k = len(plan.swaps)
    sent, got = refs[:k], refs[k : 2 * k]
    seen, d_old, old, zs_old, wx, wy, wz, wz_low, diag, scr, src = refs[2 * k : 2 * k + 11]
    pad, d, stats = refs[2 * k + 11 : 2 * k + 14]
    rest = refs[2 * k + 14 :]
    zs, faces, scratch = (None, (), rest) if final else (rest[0], rest[1 : k + 1], rest[k + 1 :])
    nx, ny, _ = src.shape
    rms, _ = totals(seen, cells)
    omega = 1.0 / (1.0 + rms)
    pad[0, OFF : OFF + ny] = old[0, OFF : OFF + ny]
    pad[nx + 1, OFF : OFF + ny] = old[nx + 1, OFF : OFF + ny]
    for row in (OFF - 1, OFF + ny):
        pad[1 : nx + 1, row : row + 1, :] = old[1 : nx + 1, row : row + 1, :]
    fluxes = []
    for (dim, s), mine, theirs in zip(plan.swaps, sent, got):
        after = after_of(AXES[dim])[s]
        if dim == 0:
            pad[after * (nx + 1), OFF : OFF + ny] += omega * theirs[...]
        elif dim == 1:
            row = OFF - 1 + after * (ny + 1)
            pad[1 : nx + 1, pl.ds(row, 1), :] += omega[:, None] * theirs[...]
        else:
            own = zs_old[3 * s] + omega * mine[...]
            far = zs_old[3 * s + 1] + omega * theirs[...]
            w = zs_old[3 * s + 2]
            if not final:
                zs[3 * s] = own
                zs[3 * s + 1] = far
                zs[3 * s + 2] = w
            fluxes.append(w * (own - far))
    sweep(
        plan,
        (pad, wx, wy, wz, wz_low, diag, scr, src, d, stats, faces, scratch),
        z_pair(fluxes, (nx, ny)),
        None,
        (old, d_old, omega),
    )


def last_kernel(cells, *refs):
    seen = refs[:ITERS]
    pad, d, out, norms, charges = refs[ITERS:]
    nx, ny, _ = out.shape
    for t in range(ITERS):
        rms, charge = totals(seen[t], cells)
        norms[t] = rms[0, 0]
        charges[t] = charge[0, 0]
    omega = 1.0 / (1.0 + rms)

    def plane(x, carry):
        out[x] = pad[x + 1, OFF : OFF + ny] + omega * d[x + 1]
        return carry

    lax.fori_loop(0, nx, plane, 0)


def body(plan, phi, eps, scr, src):
    shape = phi.shape
    nx, ny, nz = shape
    cells = float(nx * ny * nz * plan.count)
    k = len(plan.swaps)
    cost = pl.CostEstimate(flops=12000 * nx * ny * nz, bytes_accessed=4 * nx * ny * nz, transcendentals=0)
    padded = vmem((nx + 2, ny + 2 * OFF, nz))
    block, shifted = vmem(shape), vmem((nx + 1, ny, nz))
    wide_x, wide_y = shifted, vmem((nx, ny + 2 * OFF, nz))
    vm = pl.BlockSpec(memory_space=pltpu.VMEM)

    def call(kernel, outs, args, in_specs=None, out_specs=None, aliases=None, scratch=()):
        return pl.pallas_call(
            kernel,
            out_shape=outs,
            in_specs=in_specs or [vm] * len(args),
            out_specs=out_specs or [vm] * len(outs),
            scratch_shapes=scratch,
            input_output_aliases=aliases or {},
            compiler_params=pltpu.CompilerParams(vmem_limit_bytes=16 * 2**20),
            cost_estimate=cost,
        )(*args)

    def gather(stats):
        return lax.all_to_all(stats, AXES, 0, 0, tiled=True)

    *sent, phi_v, eps_v = call(
        functools.partial(faces_kernel, plan),
        [vmem(s) for s in plan.face_shapes(shape, (2,))] + [block, block],
        (phi, eps),
        in_specs=[pl.BlockSpec(memory_space=pl.ANY)] * 2,
        scratch=[pltpu.SemaphoreType.DMA((2,))],
    )
    got = plan.exchange(sent)
    pad, wx, wy, wz, wz_low = call(
        weights_kernel, [padded, wide_x, wide_y, block, block], (phi_v, eps_v)
    )
    z_state = vmem((6, nx, ny))
    face_out = [vmem(s) for s in plan.face_shapes(shape)]
    stats_shape = vmem((plan.count, nz))
    flat = vmem((ny, nz))
    scratch = [flat, flat, vmem((nz, ny)), block, block, vmem((2, nx + 8, ny))]
    pad, wx, wy, diag, d, stats, zs, *sent = call(
        functools.partial(first_kernel, plan),
        [padded, wide_x, wide_y, block, shifted, stats_shape, z_state] + face_out,
        (*sent, *got, pad, wx, wy, wz, wz_low, scr, src),
        aliases={2 * k: 0, 2 * k + 1: 1, 2 * k + 2: 2},
        scratch=scratch,
    )
    seen = []
    for t in range(1, ITERS):
        final = t == ITERS - 1
        got = plan.exchange(sent)
        seen.append(gather(stats))
        pad, d, stats, *more = call(
            functools.partial(next_kernel, plan, cells, final),
            [padded, shifted, stats_shape] + ([] if final else [z_state] + face_out),
            (*sent, *got, seen[-1], d, pad, zs, wx, wy, wz, wz_low, diag, scr, src),
            scratch=scratch,
        )
        if not final:
            zs, *sent = more
    seen.append(gather(stats))
    sm = pl.BlockSpec(memory_space=pltpu.SMEM)
    small = jax.ShapeDtypeStruct((ITERS,), F32)
    return call(
        functools.partial(last_kernel, cells),
        [jax.ShapeDtypeStruct(shape, F32), small, small],
        (*seen, pad, d),
        out_specs=[vm, sm, sm],
    )


def solution(mesh):
    block = P(*AXES)
    return jax.shard_map(
        functools.partial(body, Plan(mesh)),
        mesh=mesh,
        in_specs=(block,) * 4,
        out_specs=(block, P(), P()),
        check_vma=False,
    )
```

time: 96.7 us -> 93.8 us (0.970)
  Pallas kernels: 18.9 us -> 13.8 us
  local copies, waits for them, and re-layouts: 24.7 us -> 27.2 us
    pallas_call x6, Pallas kernels: 18.9 us -> 13.8 us  [call(): pl.pallas_call(kernel, out_shape=outs, in_specs=in_specs or [vm] * len(ar...]
    unnamed x48 -> x54, local copies, waits for them, and re-layouts: 24.7 us -> 27.2 us
where the time goes in v3:
time: 93.8 us; the launch traced here: 92.9 us
  starting transfers between devices  29.9 us (32%)
  local copies, waits for them, and re-layouts  27.2 us (29%)
  Pallas kernels  13.8 us (15%)
  blocking collectives  11.2 us (12%)
  waiting for transfers between devices  9.91 us (11%)
    unnamed x54, local copies, waits for them, and re-layouts  27.2 us
    ppermute x15, starting transfers between devices, exchange(): out.append(lax.ppermute(face, AXES[d], swaps(self.sizes[d])[s]))  17.4 us
    pallas_call x6, Pallas kernels, call(): pl.pallas_call(kernel, out_shape=outs, in_specs=in_specs or [vm] * len(ar...  13.8 us
    all_to_all x2, starting transfers between devices, gather(): return lax.all_to_all(stats, AXES, 0, 0, tiled=True)  12.5 us
    all_to_all x1, blocking collectives, gather(): return lax.all_to_all(stats, AXES, 0, 0, tiled=True)  11.2 us
    all_to_all x2, waiting for transfers between devices, gather(): return lax.all_to_all(stats, AXES, 0, 0, tiled=True)  6.91 us
    ppermute x15, waiting for transfers between devices, exchange(): out.append(lax.ppermute(face, AXES[d], swaps(self.sizes[d])[s]))  3 us
  transfers between devices with their start and end apart: 17, of which 5 were waited for; matrix products, arithmetic and copies ran while one was open for 0% of the time, Pallas kernels for 2%

profile of v3, /device:TPU:0, one launch (start us, length us, event | category | flops | bytes accessed | tf_op | source)
XLA Modules:
  0.0 92.9 jit_solution(5537889977776816331)
XLA Ops:
  1.9 1.2 %copy-done.1 = f32[16,128,128]{2,1,0:T(8,128)S(1)} copy-done((f32[16,128,128]{2,1,0:T(8,128)S(1)}, f32[16,128,128]{2,1,0:T(8,128)}, u32[]{:S(2)}) %copy-start.1) | copy-done | bytes 1048600
  4.0 3.0 %collective-permute-start.2 = (f32[2,16,1,128]{3,2,1,0:T(1,128)S(1)}, f32[2,16,1,128]{3,2,1,0:T(1,128)S(1)}, u32[]{:S(2)}, u32[]{:S(2)}) collective-permute-start(f32[2,16,1,128]{3,2,1,0:T(1,128)S(1)} %get-tuple-element.41.refs_2_), channel_id=1, source_target_pairs={{0,4},{4,0},{1,5},{5,1},{2,6},{6,2},{3,7},{7,3},{8,12},{12,8},{9,1... | collective-permute-start | bytes 49160 | tf_op jit(solution)/shard_map/ppermute | solution.py:47
  7.6 1.6 %collective-permute-start = (f32[2,128,128]{2,1,0:T(8,128)S(1)}, f32[2,128,128]{2,1,0:T(8,128)S(1)}, u32[]{:S(2)}, u32[]{:S(2)}) collective-permute-start(f32[2,128,128]{2,1,0:T(8,128)S(1)} %get-tuple-element.39.refs_0_), channel_id=1, source_target_pairs={{0,8},{8,0},{16,24},{24,16},{1,9},{9,1},{17,25},{25,17},{2,10},{10... | collective-permute-start | bytes 393224 | tf_op jit(solution)/shard_map/ppermute | solution.py:47
  10.0 2.1 %shard_map.68 = (f32[18,144,128]{2,1,0:T(8,128)S(1)}, f32[17,128,128]{2,1,0:T(8,128)S(1)}, f32[16,144,128]{2,1,0:T(8,128)S(1)}, f32[16,128,128]{2,1,0:T(8,128)S(1)}, f32[16,128,128]{2,1,0:T(8,128)S(1)}) custom-call(f32[16,128,128]{2,1,0:T(8,128)S(1)} %get-tuple-element.44.phi, f32[16,128,128]{2,1,0:T(8,128)S(1)} %get-tuple-element.45.eps), custom_call_target="tpu_custom_call" | custom-call | flops 3145728000 | bytes 1048576 | tf_op jit(solution)/shard_map/pallas_call | solution.py:367
  12.7 3.7 %shard_map.69 = (f32[18,144,128]{2,1,0:T(8,128)S(1)}, f32[17,128,128]{2,1,0:T(8,128)S(1)}, f32[16,144,128]{2,1,0:T(8,128)S(1)}, f32[16,128,128]{2,1,0:T(8,128)S(...) custom-call(f32[2,128,128]{2,1,0:T(8,128)S(1)} %get-tuple-element.39, ...), custom_call_target="tpu_custom_call", output_to_operand_aliasing={{0}: (10, {}), {1}: (11, {}), {2}: (12, {})} | custom-call | flops 3145728000 | bytes 1048576 | tf_op jit(solution)/shard_map/pallas_call | solution.py:367
  21.5 4.6 %collective-permute-start.5 = (f32[128,128]{1,0:T(8,128)S(1)}, f32[128,128]{1,0:T(8,128)S(1)}, u32[]{:S(2)}, u32[]{:S(2)}) collective-permute-start(f32[128,128]{1,0:T(8,128)S(1)} %get-tuple-element.52.refs_0_), channel_id=1, source_target_pairs={{0,8},{8,0},{16,24},{24,16},{1,9},{9,1},{17,25},{25,17},{2,10},{10... | collective-permute-start | bytes 196616 | tf_op jit(solution)/shard_map/ppermute | solution.py:47
  26.8 6.5 %all-to-all-start = ((f32[32,1,128]{2,1,0:T(1,128)}), f32[32,1,128]{2,1,0:T(1,128)S(1)}, u32[]{:S(2)}, u32[]{:S(2)}) async-start(f32[32,1,128]{2,1,0:T(1,128)} %bitcast.1), calls=%async_computation | async-start | bytes 32768 | tf_op jit(solution)/shard_map/all_to_all | solution.py:379
  33.2 1.8 %collective-permute-start.7 = (f32[16,1,128]{2,1,0:T(1,128)S(1)}, f32[16,1,128]{2,1,0:T(1,128)S(1)}, u32[]{:S(2)}, u32[]{:S(2)}) collective-permute-start(f32[16,1,128]{2,1,0:T(1,128)S(1)} %get-tuple-element.54.refs_2_), channel_id=1, source_target_pairs={{0,4},{4,0},{1,5},{5,1},{2,6},{6,2},{3,7},{7,3},{8,12},{12,8},{9,1... | collective-permute-start | bytes 24584 | tf_op jit(solution)/shard_map/ppermute | solution.py:47
  35.7 1.2 %collective-permute-done.7.refs_7_ = f32[16,1,128]{2,1,0:T(1,128)S(1)} collective-permute-done((f32[16,1,128]{2,1,0:T(1,128)S(1)}, f32[16,1,128]{2,1,0:T(1,128)S(1)}, u32[]{:S(2)}, u32[]{:S(2)}) %collective-permute-start.7) | collective-permute-done | bytes 8224 | tf_op jit(solution)/shard_map/ppermute | solution.py:47
  36.9 3.5 %all-to-all-done = f32[32,1,128]{2,1,0:T(1,128)S(1)} async-done(((f32[32,1,128]{2,1,0:T(1,128)}), f32[32,1,128]{2,1,0:T(1,128)S(1)}, u32[]{:S(2)}, u32[]{:S(2)}) %all-to-all-start) | async-done | bytes 16416 | tf_op jit(solution)/shard_map/all_to_all | solution.py:379
  40.4 1.3 %copy-done.7 = f32[18,144,128]{2,1,0:T(8,128)S(1)} copy-done((f32[18,144,128]{2,1,0:T(8,128)S(1)}, f32[18,144,128]{2,1,0:T(8,128)}, u32[]{:S(2)}) %copy-start.7) | copy-done | bytes 1327128
  41.7 1.3 %copy-done.9 = f32[16,144,128]{2,1,0:T(8,128)S(1)} copy-done((f32[16,144,128]{2,1,0:T(8,128)S(1)}, f32[16,144,128]{2,1,0:T(8,128)}, u32[]{:S(2)}) %copy-start.9) | copy-done | bytes 1179672
  43.0 1.2 %copy-done.12 = f32[17,128,128]{2,1,0:T(8,128)S(1)} copy-done((f32[17,128,128]{2,1,0:T(8,128)S(1)}, f32[17,128,128]{2,1,0:T(8,128)}, u32[]{:S(2)}) %copy-start.12) | copy-done | bytes 1114136
  44.3 1.2 %copy-done.16 = f32[17,128,128]{2,1,0:T(8,128)S(1)} copy-done((f32[17,128,128]{2,1,0:T(8,128)S(1)}, f32[17,128,128]{2,1,0:T(8,128)}, u32[]{:S(2)}) %copy-start.16) | copy-done | bytes 1114136
  45.5 1.2 %copy-done.19 = f32[16,128,128]{2,1,0:T(8,128)S(1)} copy-done((f32[16,128,128]{2,1,0:T(8,128)S(1)}, f32[16,128,128]{2,1,0:T(8,128)}, u32[]{:S(2)}) %copy-start.19) | copy-done | bytes 1048600
  46.7 1.2 %copy-done.22 = f32[16,128,128]{2,1,0:T(8,128)S(1)} copy-done((f32[16,128,128]{2,1,0:T(8,128)S(1)}, f32[16,128,128]{2,1,0:T(8,128)}, u32[]{:S(2)}) %copy-start.22) | copy-done | bytes 1048600
  48.0 1.2 %copy-done.25 = f32[16,128,128]{2,1,0:T(8,128)S(1)} copy-done((f32[16,128,128]{2,1,0:T(8,128)S(1)}, f32[16,128,128]{2,1,0:T(8,128)}, u32[]{:S(2)}) %copy-start.25) | copy-done | bytes 1048600
  49.2 3.4 %shard_map.70 = (f32[18,144,128]{2,1,0:T(8,128)S(1)}, f32[17,128,128]{2,1,0:T(8,128)S(1)}, f32[32,128]{1,0:T(8,128)}, f32[6,16,128]{2,1,0:T(8,128)S(1)}, f32[128...) custom-call(f32[128,128]{1,0:T(8,128)S(1)} %get-tuple-element.52.ref, ...), custom_call_target="tpu_custom_call" | custom-call | flops 3145728000 | bytes 1048576 | tf_op jit(solution)/shard_map/pallas_call | solution.py:367
  55.9 6.1 %all-to-all-start.1 = ((f32[32,1,128]{2,1,0:T(1,128)}), f32[32,1,128]{2,1,0:T(1,128)S(1)}, u32[]{:S(2)}, u32[]{:S(2)}) async-start(f32[32,1,128]{2,1,0:T(1,128)} %bitcast.4), calls=%async_computation.1 | async-start | bytes 32768 | tf_op jit(solution)/shard_map/all_to_all | solution.py:379
  62.0 1.8 %collective-permute-start.12 = (f32[16,1,128]{2,1,0:T(1,128)S(1)}, f32[16,1,128]{2,1,0:T(1,128)S(1)}, u32[]{:S(2)}, u32[]{:S(2)}) collective-permute-start(f32[16,1,128]{2,1,0:T(1,128)S(1)} %get-tuple-element.66.refs_2_), channel_id=1, source_target_pairs={{0,4},{4,0},{1,5},{5,1},{2,6},{6,2},{3,7},{7,3},{8,12},{12,8},{9,1... | collective-permute-start | bytes 24584 | tf_op jit(solution)/shard_map/ppermute | solution.py:47
  64.5 1.2 %collective-permute-done.12.refs_7_ = f32[16,1,128]{2,1,0:T(1,128)S(1)} collective-permute-done((f32[16,1,128]{2,1,0:T(1,128)S(1)}, f32[16,1,128]{2,1,0:T(1,128)S(1)}, u32[]{:S(2)}, u32[]{:S(2)}) %collective-permute-start.12) | collective-permute-done | bytes 8224 | tf_op jit(solution)/shard_map/ppermute | solution.py:47
  65.7 3.5 %all-to-all-done.1 = f32[32,1,128]{2,1,0:T(1,128)S(1)} async-done(((f32[32,1,128]{2,1,0:T(1,128)}), f32[32,1,128]{2,1,0:T(1,128)S(1)}, u32[]{:S(2)}, u32[]{:S(2)}) %all-to-all-start.1) | async-done | bytes 16416 | tf_op jit(solution)/shard_map/all_to_all | solution.py:379
  69.2 1.3 %copy-done.5 = f32[18,144,128]{2,1,0:T(8,128)S(1)} copy-done((f32[18,144,128]{2,1,0:T(8,128)S(1)}, f32[18,144,128]{2,1,0:T(8,128)}, u32[]{:S(2)}) %copy-start.5) | copy-done | bytes 1327128
  70.5 1.3 %copy-done.10 = f32[16,144,128]{2,1,0:T(8,128)S(1)} copy-done((f32[16,144,128]{2,1,0:T(8,128)S(1)}, f32[16,144,128]{2,1,0:T(8,128)}, u32[]{:S(2)}) %copy-start.10) | copy-done | bytes 1179672
  71.8 1.2 %copy-done.14 = f32[17,128,128]{2,1,0:T(8,128)S(1)} copy-done((f32[17,128,128]{2,1,0:T(8,128)S(1)}, f32[17,128,128]{2,1,0:T(8,128)}, u32[]{:S(2)}) %copy-start.14) | copy-done | bytes 1114136
  73.0 1.2 %copy-done.17 = f32[17,128,128]{2,1,0:T(8,128)S(1)} copy-done((f32[17,128,128]{2,1,0:T(8,128)S(1)}, f32[17,128,128]{2,1,0:T(8,128)}, u32[]{:S(2)}) %copy-start.17) | copy-done | bytes 1114136
  74.3 1.2 %copy-done.20 = f32[16,128,128]{2,1,0:T(8,128)S(1)} copy-done((f32[16,128,128]{2,1,0:T(8,128)S(1)}, f32[16,128,128]{2,1,0:T(8,128)}, u32[]{:S(2)}) %copy-start.20) | copy-done | bytes 1048600
  75.5 1.2 %copy-done.23 = f32[16,128,128]{2,1,0:T(8,128)S(1)} copy-done((f32[16,128,128]{2,1,0:T(8,128)S(1)}, f32[16,128,128]{2,1,0:T(8,128)}, u32[]{:S(2)}) %copy-start.23) | copy-done | bytes 1048600
  76.7 1.2 %copy-done.26 = f32[16,128,128]{2,1,0:T(8,128)S(1)} copy-done((f32[16,128,128]{2,1,0:T(8,128)S(1)}, f32[16,128,128]{2,1,0:T(8,128)}, u32[]{:S(2)}) %copy-start.26) | copy-done | bytes 1048600
  78.0 2.4 %shard_map.71 = (f32[18,144,128]{2,1,0:T(8,128)S(1)}, f32[17,128,128]{2,1,0:T(8,128)S(1)}, f32[32,128]{1,0:T(8,128)S(1)}) custom-call(f32[128,128]{1,0:T(8,128)S(1)} %get-tuple-element.64.refs_0_, f32[128,128]{1,0:T(8,128)S(1)} %get-tuple-element.65.refs_1_, f32[16,1,128]{2,1,0:T(1,128)S(1)} %get-tuple-element.66.refs_2_, ...), custom_call_target="tpu_custom_call" | custom-call | flops 3145728000 | bytes 1048576 | tf_op jit(solution)/shard_map/pallas_call | solution.py:367
  80.4 11.2 %all_to_all.33 = f32[32,1,128]{2,1,0:T(1,128)S(1)} all-to-all(f32[32,1,128]{2,1,0:T(1,128)S(1)} %bitcast.16), channel_id=1, replica_groups=mesh['gx'=4,'gy'=2,'gz'=4] {'gx','gy','gz'}, dimensions={0} | all-to-all | bytes 32768 | tf_op jit(solution)/shard_map/all_to_all | solution.py:379
  91.6 1.3 %shard_map.72 = (f32[16,128,128]{2,1,0:T(8,128)}, f32[3]{0:T(128)}, f32[3]{0:T(128)}) custom-call(f32[32,128]{1,0:T(8,128)S(1)} %bitcast.13, f32[32,128]{1,0:T(8,128)S(1)} %bitcast.15, f32[32,128]{1,0:T(8,128)S(1)} %bitcast.17, f32[18,144,128]{2,1,0:T(8,128)S(1)} %get-tuple-element.73.refs_3_, f32[17,128,128]{2,1,0:T(8,128)S(1)} %get-tuple-element.74.refs_4_), custom_call_target="tpu_custom_call" | custom-call | flops 3145728000 | bytes 1048576 | tf_op jit(solution)/shard_map/pallas_call | solution.py:367
  (63 shorter events, 14.4 us)
Async XLA Ops:
  0.6 1.2 %copy-start = (f32[16,128,128]{2,1,0:T(8,128)S(1)}, f32[16,128,128]{2,1,0:T(8,128)}, u32[]{:S(2)}) copy-start(f32[16,128,128]{2,1,0:T(8,128)} %phi_in.1) | copy-start | bytes 3145732
  4.0 8.2 %collective-permute-start.2 = (f32[2,16,1,128]{3,2,1,0:T(1,128)S(1)}, f32[2,16,1,128]{3,2,1,0:T(1,128)S(1)}, u32[]{:S(2)}, u32[]{:S(2)}) collective-permute-start(f32[2,16,1,128]{3,2,1,0:T(1,128)S(1)} %get-tuple-element.41.refs_2_), channel_id=1, source_target_pairs={{0,4},{4,0},{1,5},{5,1},{2,6},{6,2},{3,7},{7,3},{8,12},{12,8},{9,1... | collective-permute-start | bytes 49160 | tf_op jit(solution)/shard_map/ppermute | solution.py:47
  7.0 5.2 %collective-permute-start.3 = (f32[2,16,128]{2,1,0:T(8,128)S(1)}, f32[2,16,128]{2,1,0:T(8,128)S(1)}, u32[]{:S(2)}, u32[]{:S(2)}) collective-permute-start(f32[2,16,128]{2,1,0:T(8,128)S(1)} %get-tuple-element.42.refs_3_), channel_id=1, source_target_pairs={{0,1},{1,0},{2,3},{3,2},{4,5},{5,4},{6,7},{7,6},{8,9},{9,8},{10,11... | collective-permute-start | bytes 49160 | tf_op jit(solution)/shard_map/ppermute | solution.py:47
  7.0 5.2 %collective-permute-start.4 = (f32[2,16,128]{2,1,0:T(8,128)S(1)}, f32[2,16,128]{2,1,0:T(8,128)S(1)}, u32[]{:S(2)}, u32[]{:S(2)}) collective-permute-start(f32[2,16,128]{2,1,0:T(8,128)S(1)} %get-tuple-element.43.refs_4_), channel_id=1, source_target_pairs={{1,2},{2,1},{5,6},{6,5},{9,10},{10,9},{13,14},{14,13},{17,18},{18,... | collective-permute-start | bytes 49160 | tf_op jit(solution)/shard_map/ppermute | solution.py:47
  7.6 5.0 %collective-permute-start = (f32[2,128,128]{2,1,0:T(8,128)S(1)}, f32[2,128,128]{2,1,0:T(8,128)S(1)}, u32[]{:S(2)}, u32[]{:S(2)}) collective-permute-start(f32[2,128,128]{2,1,0:T(8,128)S(1)} %get-tuple-element.39.refs_0_), channel_id=1, source_target_pairs={{0,8},{8,0},{16,24},{24,16},{1,9},{9,1},{17,25},{25,17},{2,10},{10... | collective-permute-start | bytes 393224 | tf_op jit(solution)/shard_map/ppermute | solution.py:47
  9.3 3.4 %collective-permute-start.1 = (f32[2,128,128]{2,1,0:T(8,128)S(1)}, f32[2,128,128]{2,1,0:T(8,128)S(1)}, u32[]{:S(2)}, u32[]{:S(2)}) collective-permute-start(f32[2,128,128]{2,1,0:T(8,128)S(1)} %get-tuple-element.40.refs_1_), channel_id=1, source_target_pairs={{8,16},{16,8},{9,17},{17,9},{10,18},{18,10},{11,19},{19,11},{12,20... | collective-permute-start | bytes 393224 | tf_op jit(solution)/shard_map/ppermute | solution.py:47
  9.9 2.7 %copy-start.2 = (f32[16,128,128]{2,1,0:T(8,128)S(1)}, f32[16,128,128]{2,1,0:T(8,128)}, u32[]{:S(2)}) copy-start(f32[16,128,128]{2,1,0:T(8,128)} %refs_19_.3) | copy-start | bytes 3145732
  10.0 2.7 %copy-start.3 = (f32[16,128,128]{2,1,0:T(8,128)S(1)}, f32[16,128,128]{2,1,0:T(8,128)}, u32[]{:S(2)}) copy-start(f32[16,128,128]{2,1,0:T(8,128)} %refs_20_.3) | copy-start | bytes 3145732
  12.1 4.3 %copy-start.18 = (f32[16,128,128]{2,1,0:T(8,128)}, f32[16,128,128]{2,1,0:T(8,128)S(1)}, u32[]{:S(2)}) copy-start(f32[16,128,128]{2,1,0:T(8,128)S(1)} %get-tuple-element.49.refs_13_.refs_16_) | copy-start | bytes 3145732
  12.1 4.3 %copy-start.21 = (f32[16,128,128]{2,1,0:T(8,128)}, f32[16,128,128]{2,1,0:T(8,128)S(1)}, u32[]{:S(2)}) copy-start(f32[16,128,128]{2,1,0:T(8,128)S(1)} %get-tuple-element.50.refs_14_.refs_17_) | copy-start | bytes 3145732
  21.5 18.9 %collective-permute-start.5 = (f32[128,128]{1,0:T(8,128)S(1)}, f32[128,128]{1,0:T(8,128)S(1)}, u32[]{:S(2)}, u32[]{:S(2)}) collective-permute-start(f32[128,128]{1,0:T(8,128)S(1)} %get-tuple-element.52.refs_0_), channel_id=1, source_target_pairs={{0,8},{8,0},{16,24},{24,16},{1,9},{9,1},{17,25},{25,17},{2,10},{10... | collective-permute-start | bytes 196616 | tf_op jit(solution)/shard_map/ppermute | solution.py:47
  26.1 14.3 %collective-permute-start.6 = (f32[128,128]{1,0:T(8,128)S(1)}, f32[128,128]{1,0:T(8,128)S(1)}, u32[]{:S(2)}, u32[]{:S(2)}) collective-permute-start(f32[128,128]{1,0:T(8,128)S(1)} %get-tuple-element.53.refs_1_), channel_id=1, source_target_pairs={{8,16},{16,8},{9,17},{17,9},{10,18},{18,10},{11,19},{19,11},{12,20... | collective-permute-start | bytes 196616 | tf_op jit(solution)/shard_map/ppermute | solution.py:47
  26.8 13.6 %all-to-all-start = ((f32[32,1,128]{2,1,0:T(1,128)}), f32[32,1,128]{2,1,0:T(1,128)S(1)}, u32[]{:S(2)}, u32[]{:S(2)}) async-start(f32[32,1,128]{2,1,0:T(1,128)} %bitcast.1), calls=%async_computation | async-start | bytes 32768 | tf_op jit(solution)/shard_map/all_to_all | solution.py:379
  33.2 3.7 %collective-permute-start.7 = (f32[16,1,128]{2,1,0:T(1,128)S(1)}, f32[16,1,128]{2,1,0:T(1,128)S(1)}, u32[]{:S(2)}, u32[]{:S(2)}) collective-permute-start(f32[16,1,128]{2,1,0:T(1,128)S(1)} %get-tuple-element.54.refs_2_), channel_id=1, source_target_pairs={{0,4},{4,0},{1,5},{5,1},{2,6},{6,2},{3,7},{7,3},{8,12},{12,8},{9,1... | collective-permute-start | bytes 24584 | tf_op jit(solution)/shard_map/ppermute | solution.py:47
  35.1 1.9 %collective-permute-start.8 = (f32[16,128]{1,0:T(8,128)S(1)}, f32[16,128]{1,0:T(8,128)S(1)}, u32[]{:S(2)}, u32[]{:S(2)}) collective-permute-start(f32[16,128]{1,0:T(8,128)S(1)} %get-tuple-element.55.refs_3_), channel_id=1, source_target_pairs={{0,1},{1,0},{2,3},{3,2},{4,5},{5,4},{6,7},{7,6},{8,9},{9,8},{10,11... | collective-permute-start | bytes 24584 | tf_op jit(solution)/shard_map/ppermute | solution.py:47
  35.1 1.9 %collective-permute-start.9 = (f32[16,128]{1,0:T(8,128)S(1)}, f32[16,128]{1,0:T(8,128)S(1)}, u32[]{:S(2)}, u32[]{:S(2)}) collective-permute-start(f32[16,128]{1,0:T(8,128)S(1)} %get-tuple-element.56.refs_4_), channel_id=1, source_target_pairs={{1,2},{2,1},{5,6},{6,5},{9,10},{10,9},{13,14},{14,13},{17,18},{18,... | collective-permute-start | bytes 24584 | tf_op jit(solution)/shard_map/ppermute | solution.py:47
  40.4 1.3 %copy-start.7 = (f32[18,144,128]{2,1,0:T(8,128)S(1)}, f32[18,144,128]{2,1,0:T(8,128)}, u32[]{:S(2)}) copy-start(f32[18,144,128]{2,1,0:T(8,128)} %copy-done.6) | copy-start | bytes 3981316
  41.7 1.3 %copy-start.9 = (f32[16,144,128]{2,1,0:T(8,128)S(1)}, f32[16,144,128]{2,1,0:T(8,128)}, u32[]{:S(2)}) copy-start(f32[16,144,128]{2,1,0:T(8,128)} %copy-done.8) | copy-start | bytes 3538948
  43.0 1.2 %copy-start.12 = (f32[17,128,128]{2,1,0:T(8,128)S(1)}, f32[17,128,128]{2,1,0:T(8,128)}, u32[]{:S(2)}) copy-start(f32[17,128,128]{2,1,0:T(8,128)} %copy-done.11) | copy-start | bytes 3342340
  44.3 1.2 %copy-start.16 = (f32[17,128,128]{2,1,0:T(8,128)S(1)}, f32[17,128,128]{2,1,0:T(8,128)}, u32[]{:S(2)}) copy-start(f32[17,128,128]{2,1,0:T(8,128)} %copy-done.15) | copy-start | bytes 3342340
  45.5 1.2 %copy-start.19 = (f32[16,128,128]{2,1,0:T(8,128)S(1)}, f32[16,128,128]{2,1,0:T(8,128)}, u32[]{:S(2)}) copy-start(f32[16,128,128]{2,1,0:T(8,128)} %copy-done.18) | copy-start | bytes 3145732
  46.7 1.2 %copy-start.22 = (f32[16,128,128]{2,1,0:T(8,128)S(1)}, f32[16,128,128]{2,1,0:T(8,128)}, u32[]{:S(2)}) copy-start(f32[16,128,128]{2,1,0:T(8,128)} %copy-done.21) | copy-start | bytes 3145732
  54.7 14.5 %collective-permute-start.10 = (f32[128,128]{1,0:T(8,128)S(1)}, f32[128,128]{1,0:T(8,128)S(1)}, u32[]{:S(2)}, u32[]{:S(2)}) collective-permute-start(f32[128,128]{1,0:T(8,128)S(1)} %get-tuple-element.64.refs_0_), channel_id=1, source_target_pairs={{0,8},{8,0},{16,24},{24,16},{1,9},{9,1},{17,25},{25,17},{2,10},{10... | collective-permute-start | bytes 196616 | tf_op jit(solution)/shard_map/ppermute | solution.py:47
  55.3 13.9 %collective-permute-start.11 = (f32[128,128]{1,0:T(8,128)S(1)}, f32[128,128]{1,0:T(8,128)S(1)}, u32[]{:S(2)}, u32[]{:S(2)}) collective-permute-start(f32[128,128]{1,0:T(8,128)S(1)} %get-tuple-element.65.refs_1_), channel_id=1, source_target_pairs={{8,16},{16,8},{9,17},{17,9},{10,18},{18,10},{11,19},{19,11},{12,20... | collective-permute-start | bytes 196616 | tf_op jit(solution)/shard_map/ppermute | solution.py:47
  55.9 13.2 %all-to-all-start.1 = ((f32[32,1,128]{2,1,0:T(1,128)}), f32[32,1,128]{2,1,0:T(1,128)S(1)}, u32[]{:S(2)}, u32[]{:S(2)}) async-start(f32[32,1,128]{2,1,0:T(1,128)} %bitcast.4), calls=%async_computation.1 | async-start | bytes 32768 | tf_op jit(solution)/shard_map/all_to_all | solution.py:379
  62.0 3.7 %collective-permute-start.12 = (f32[16,1,128]{2,1,0:T(1,128)S(1)}, f32[16,1,128]{2,1,0:T(1,128)S(1)}, u32[]{:S(2)}, u32[]{:S(2)}) collective-permute-start(f32[16,1,128]{2,1,0:T(1,128)S(1)} %get-tuple-element.66.refs_2_), channel_id=1, source_target_pairs={{0,4},{4,0},{1,5},{5,1},{2,6},{6,2},{3,7},{7,3},{8,12},{12,8},{9,1... | collective-permute-start | bytes 24584 | tf_op jit(solution)/shard_map/ppermute | solution.py:47
  63.8 1.9 %collective-permute-start.13 = (f32[16,128]{1,0:T(8,128)S(1)}, f32[16,128]{1,0:T(8,128)S(1)}, u32[]{:S(2)}, u32[]{:S(2)}) collective-permute-start(f32[16,128]{1,0:T(8,128)S(1)} %get-tuple-element.67.refs_3_), channel_id=1, source_target_pairs={{0,1},{1,0},{2,3},{3,2},{4,5},{5,4},{6,7},{7,6},{8,9},{9,8},{10,11... | collective-permute-start | bytes 24584 | tf_op jit(solution)/shard_map/ppermute | solution.py:47
  63.8 1.9 %collective-permute-start.14 = (f32[16,128]{1,0:T(8,128)S(1)}, f32[16,128]{1,0:T(8,128)S(1)}, u32[]{:S(2)}, u32[]{:S(2)}) collective-permute-start(f32[16,128]{1,0:T(8,128)S(1)} %get-tuple-element.68.refs_4_), channel_id=1, source_target_pairs={{1,2},{2,1},{5,6},{6,5},{9,10},{10,9},{13,14},{14,13},{17,18},{18,... | collective-permute-start | bytes 24584 | tf_op jit(solution)/shard_map/ppermute | solution.py:47
  69.2 1.3 %copy-start.5 = (f32[18,144,128]{2,1,0:T(8,128)S(1)}, f32[18,144,128]{2,1,0:T(8,128)}, u32[]{:S(2)}) copy-start(f32[18,144,128]{2,1,0:T(8,128)} %copy-done.4) | copy-start | bytes 3981316
  70.5 1.3 %copy-start.10 = (f32[16,144,128]{2,1,0:T(8,128)S(1)}, f32[16,144,128]{2,1,0:T(8,128)}, u32[]{:S(2)}) copy-start(f32[16,144,128]{2,1,0:T(8,128)} %copy-done.8) | copy-start | bytes 3538948
  71.8 1.2 %copy-start.14 = (f32[17,128,128]{2,1,0:T(8,128)S(1)}, f32[17,128,128]{2,1,0:T(8,128)}, u32[]{:S(2)}) copy-start(f32[17,128,128]{2,1,0:T(8,128)} %copy-done.13) | copy-start | bytes 3342340
  73.0 1.2 %copy-start.17 = (f32[17,128,128]{2,1,0:T(8,128)S(1)}, f32[17,128,128]{2,1,0:T(8,128)}, u32[]{:S(2)}) copy-start(f32[17,128,128]{2,1,0:T(8,128)} %copy-done.15) | copy-start | bytes 3342340
  (12 other events, 13.3 us)

commit v4 on v3

--- a/solution.py
+++ b/solution.py
@@ -10,6 +10,7 @@
 ITERS = 3
 AXES = ("gx", "gy", "gz")
 OFF = 8
+VMEM_BYTES = 67043328
 CHUNK = 32
 LOG2E = 1.4426950408889634
 F32 = jnp.float32
@@ -363,7 +364,7 @@
     wide_x, wide_y = shifted, vmem((nx, ny + 2 * OFF, nz))
     vm = pl.BlockSpec(memory_space=pltpu.VMEM)
 
-    def call(kernel, outs, args, in_specs=None, out_specs=None, aliases=None, scratch=()):
+    def call(kernel, outs, args, in_specs=None, out_specs=None, aliases=None, scratch=(), room=16 * 2**20):
         return pl.pallas_call(
             kernel,
             out_shape=outs,
@@ -371,7 +372,7 @@
             out_specs=out_specs or [vm] * len(outs),
             scratch_shapes=scratch,
             input_output_aliases=aliases or {},
-            compiler_params=pltpu.CompilerParams(vmem_limit_bytes=16 * 2**20),
+            compiler_params=pltpu.CompilerParams(vmem_limit_bytes=room),
             cost_estimate=cost,
         )(*args)
 
@@ -382,8 +383,9 @@
         functools.partial(faces_kernel, plan),
         [vmem(s) for s in plan.face_shapes(shape, (2,))] + [block, block],
         (phi, eps),
-        in_specs=[pl.BlockSpec(memory_space=pl.ANY)] * 2,
+        in_specs=[pl.BlockSpec(memory_space=pltpu.HBM)] * 2,
         scratch=[pltpu.SemaphoreType.DMA((2,))],
+        room=VMEM_BYTES - 4 * (2 * nx * ny * nz + 8 * (ny * nz + nx * nz + nx * ny)) - 2**19,
     )
     got = plan.exchange(sent)
     pad, wx, wy, wz, wz_low = call(

time: 93.8 us -> 95.6 us (1.019)
  local copies, waits for them, and re-layouts: 27.2 us -> 29.2 us
  Pallas kernels: 13.8 us -> 14.9 us
    unnamed x54 -> x58, local copies, waits for them, and re-layouts: 27.2 us -> 29.2 us
    pallas_call x6, Pallas kernels: 13.8 us -> 14.9 us  [call(): pl.pallas_call(kernel, out_shape=outs, in_specs=in_specs or [vm] * len(ar...]
  transfers between devices with their start and end apart: 17 -> 17, of which waited for: 5 -> 4; matrix products, arithmetic and copies ran while one was open for 0% -> 0% of each run, Pallas kernels for 2% -> 2%
where the time goes in v4:
time: 95.6 us; the launch traced here: 94.7 us
  local copies, waits for them, and re-layouts  29.2 us (31%)
  starting transfers between devices  29.1 us (30%)
  Pallas kernels  14.9 us (16%)
  blocking collectives  11.2 us (12%)
  waiting for transfers between devices  9.39 us (10%)
    unnamed x58, local copies, waits for them, and re-layouts  29.2 us
    ppermute x15, starting transfers between devices, exchange(): out.append(lax.ppermute(face, AXES[d], swaps(self.sizes[d])[s]))  17.2 us
    pallas_call x6, Pallas kernels, call(): pl.pallas_call(kernel, out_shape=outs, in_specs=in_specs or [vm] * len(ar...  14.9 us
    all_to_all x2, starting transfers between devices, gather(): return lax.all_to_all(stats, AXES, 0, 0, tiled=True)  12 us
    all_to_all x1, blocking collectives, gather(): return lax.all_to_all(stats, AXES, 0, 0, tiled=True)  11.2 us
    all_to_all x2, waiting for transfers between devices, gather(): return lax.all_to_all(stats, AXES, 0, 0, tiled=True)  6.91 us
    ppermute x15, waiting for transfers between devices, exchange(): out.append(lax.ppermute(face, AXES[d], swaps(self.sizes[d])[s]))  2.48 us
  transfers between devices with their start and end apart: 17, of which 4 were waited for; matrix products, arithmetic and copies ran while one was open for 0% of the time, Pallas kernels for 2%

profile of v4, /device:TPU:0, one launch (start us, length us, event | category | flops | bytes accessed | tf_op | source)
XLA Modules:
  0.0 94.7 jit_solution(8605510058609577382)
XLA Ops:
  0.6 1.9 %shard_map.67 = (f32[2,128,128]{2,1,0:T(8,128)S(1)}, f32[2,128,128]{2,1,0:T(8,128)S(1)}, f32[2,16,1,128]{3,2,1,0:T(1,128)S(1)}, f32[2,16,128]{2,1,0:T(8,128)S(1)...) custom-call(f32[16,128,128]{2,1,0:T(8,128)} %phi_in.1, f32[16,128,128]{2,1,0:T(8,128)} %eps_in.1), custom_call_target="tpu_custom_call" | custom-call | flops 3145728000 | bytes 1048576 | tf_op jit(solution)/shard_map/pallas_call | solution.py:368
  4.6 3.0 %collective-permute-start.2 = (f32[2,16,1,128]{3,2,1,0:T(1,128)S(1)}, f32[2,16,1,128]{3,2,1,0:T(1,128)S(1)}, u32[]{:S(2)}, u32[]{:S(2)}) collective-permute-start(f32[2,16,1,128]{3,2,1,0:T(1,128)S(1)} %get-tuple-element.41.refs_2_), channel_id=1, source_target_pairs={{0,4},{4,0},{1,5},{5,1},{2,6},{6,2},{3,7},{7,3},{8,12},{12,8},{9,1... | collective-permute-start | bytes 49160 | tf_op jit(solution)/shard_map/ppermute | solution.py:48
  8.2 1.6 %collective-permute-start = (f32[2,128,128]{2,1,0:T(8,128)S(1)}, f32[2,128,128]{2,1,0:T(8,128)S(1)}, u32[]{:S(2)}, u32[]{:S(2)}) collective-permute-start(f32[2,128,128]{2,1,0:T(8,128)S(1)} %get-tuple-element.39.refs_0_), channel_id=1, source_target_pairs={{0,8},{8,0},{16,24},{24,16},{1,9},{9,1},{17,25},{25,17},{2,10},{10... | collective-permute-start | bytes 393224 | tf_op jit(solution)/shard_map/ppermute | solution.py:48
  11.7 1.2 %copy-done.28 = f32[16,128,128]{2,1,0:T(8,128)S(1)} copy-done((f32[16,128,128]{2,1,0:T(8,128)S(1)}, f32[16,128,128]{2,1,0:T(8,128)}, u32[]{:S(2)}) %copy-start.28) | copy-done | bytes 1048600
  12.9 2.1 %shard_map.68 = (f32[18,144,128]{2,1,0:T(8,128)S(1)}, f32[17,128,128]{2,1,0:T(8,128)S(1)}, f32[16,144,128]{2,1,0:T(8,128)S(1)}, f32[16,128,128]{2,1,0:T(8,128)S(1)}, f32[16,128,128]{2,1,0:T(8,128)S(1)}) custom-call(f32[16,128,128]{2,1,0:T(8,128)S(1)} %copy-done.26, f32[16,128,128]{2,1,0:T(8,128)S(1)} %copy-done.28), custom_call_target="tpu_custom_call" | custom-call | flops 3145728000 | bytes 1048576 | tf_op jit(solution)/shard_map/pallas_call | solution.py:368
  15.2 3.7 %shard_map.69 = (f32[18,144,128]{2,1,0:T(8,128)S(1)}, f32[17,128,128]{2,1,0:T(8,128)S(1)}, f32[16,144,128]{2,1,0:T(8,128)S(1)}, f32[16,128,128]{2,1,0:T(8,128)S(...) custom-call(f32[2,128,128]{2,1,0:T(8,128)S(1)} %get-tuple-element.39, ...), custom_call_target="tpu_custom_call", output_to_operand_aliasing={{0}: (10, {}), {1}: (11, {}), {2}: (12, {})} | custom-call | flops 3145728000 | bytes 1048576 | tf_op jit(solution)/shard_map/pallas_call | solution.py:368
  24.0 4.4 %collective-permute-start.5 = (f32[128,128]{1,0:T(8,128)S(1)}, f32[128,128]{1,0:T(8,128)S(1)}, u32[]{:S(2)}, u32[]{:S(2)}) collective-permute-start(f32[128,128]{1,0:T(8,128)S(1)} %get-tuple-element.52.refs_0_), channel_id=1, source_target_pairs={{0,8},{8,0},{16,24},{24,16},{1,9},{9,1},{17,25},{25,17},{2,10},{10... | collective-permute-start | bytes 196616 | tf_op jit(solution)/shard_map/ppermute | solution.py:48
  29.1 5.9 %all-to-all-start = ((f32[32,1,128]{2,1,0:T(1,128)}), f32[32,1,128]{2,1,0:T(1,128)S(1)}, u32[]{:S(2)}, u32[]{:S(2)}) async-start(f32[32,1,128]{2,1,0:T(1,128)} %bitcast.1), calls=%async_computation | async-start | bytes 32768 | tf_op jit(solution)/shard_map/all_to_all | solution.py:380
  35.0 1.8 %collective-permute-start.7 = (f32[16,1,128]{2,1,0:T(1,128)S(1)}, f32[16,1,128]{2,1,0:T(1,128)S(1)}, u32[]{:S(2)}, u32[]{:S(2)}) collective-permute-start(f32[16,1,128]{2,1,0:T(1,128)S(1)} %get-tuple-element.54.refs_2_), channel_id=1, source_target_pairs={{0,4},{4,0},{1,5},{5,1},{2,6},{6,2},{3,7},{7,3},{8,12},{12,8},{9,1... | collective-permute-start | bytes 24584 | tf_op jit(solution)/shard_map/ppermute | solution.py:48
  38.7 3.5 %all-to-all-done = f32[32,1,128]{2,1,0:T(1,128)S(1)} async-done(((f32[32,1,128]{2,1,0:T(1,128)}), f32[32,1,128]{2,1,0:T(1,128)S(1)}, u32[]{:S(2)}, u32[]{:S(2)}) %all-to-all-start) | async-done | bytes 16416 | tf_op jit(solution)/shard_map/all_to_all | solution.py:380
  42.2 1.3 %copy-done.5 = f32[18,144,128]{2,1,0:T(8,128)S(1)} copy-done((f32[18,144,128]{2,1,0:T(8,128)S(1)}, f32[18,144,128]{2,1,0:T(8,128)}, u32[]{:S(2)}) %copy-start.5) | copy-done | bytes 1327128
  43.5 1.3 %copy-done.7 = f32[16,144,128]{2,1,0:T(8,128)S(1)} copy-done((f32[16,144,128]{2,1,0:T(8,128)S(1)}, f32[16,144,128]{2,1,0:T(8,128)}, u32[]{:S(2)}) %copy-start.7) | copy-done | bytes 1179672
  44.8 1.2 %copy-done.10 = f32[17,128,128]{2,1,0:T(8,128)S(1)} copy-done((f32[17,128,128]{2,1,0:T(8,128)S(1)}, f32[17,128,128]{2,1,0:T(8,128)}, u32[]{:S(2)}) %copy-start.10) | copy-done | bytes 1114136
  46.0 1.2 %copy-done.14 = f32[17,128,128]{2,1,0:T(8,128)S(1)} copy-done((f32[17,128,128]{2,1,0:T(8,128)S(1)}, f32[17,128,128]{2,1,0:T(8,128)}, u32[]{:S(2)}) %copy-start.14) | copy-done | bytes 1114136
  47.3 1.2 %copy-done.17 = f32[16,128,128]{2,1,0:T(8,128)S(1)} copy-done((f32[16,128,128]{2,1,0:T(8,128)S(1)}, f32[16,128,128]{2,1,0:T(8,128)}, u32[]{:S(2)}) %copy-start.17) | copy-done | bytes 1048600
  48.5 1.2 %copy-done.20 = f32[16,128,128]{2,1,0:T(8,128)S(1)} copy-done((f32[16,128,128]{2,1,0:T(8,128)S(1)}, f32[16,128,128]{2,1,0:T(8,128)}, u32[]{:S(2)}) %copy-start.20) | copy-done | bytes 1048600
  49.7 1.2 %copy-done.23 = f32[16,128,128]{2,1,0:T(8,128)S(1)} copy-done((f32[16,128,128]{2,1,0:T(8,128)S(1)}, f32[16,128,128]{2,1,0:T(8,128)}, u32[]{:S(2)}) %copy-start.23) | copy-done | bytes 1048600
  50.9 3.4 %shard_map.70 = (f32[18,144,128]{2,1,0:T(8,128)S(1)}, f32[17,128,128]{2,1,0:T(8,128)S(1)}, f32[32,128]{1,0:T(8,128)}, f32[6,16,128]{2,1,0:T(8,128)S(1)}, f32[128...) custom-call(f32[128,128]{1,0:T(8,128)S(1)} %get-tuple-element.52.ref, ...), custom_call_target="tpu_custom_call" | custom-call | flops 3145728000 | bytes 1048576 | tf_op jit(solution)/shard_map/pallas_call | solution.py:368
  57.7 6.1 %all-to-all-start.1 = ((f32[32,1,128]{2,1,0:T(1,128)}), f32[32,1,128]{2,1,0:T(1,128)S(1)}, u32[]{:S(2)}, u32[]{:S(2)}) async-start(f32[32,1,128]{2,1,0:T(1,128)} %bitcast.4), calls=%async_computation.1 | async-start | bytes 32768 | tf_op jit(solution)/shard_map/all_to_all | solution.py:380
  63.8 1.8 %collective-permute-start.12 = (f32[16,1,128]{2,1,0:T(1,128)S(1)}, f32[16,1,128]{2,1,0:T(1,128)S(1)}, u32[]{:S(2)}, u32[]{:S(2)}) collective-permute-start(f32[16,1,128]{2,1,0:T(1,128)S(1)} %get-tuple-element.66.refs_2_), channel_id=1, source_target_pairs={{0,4},{4,0},{1,5},{5,1},{2,6},{6,2},{3,7},{7,3},{8,12},{12,8},{9,1... | collective-permute-start | bytes 24584 | tf_op jit(solution)/shard_map/ppermute | solution.py:48
  66.3 1.2 %collective-permute-done.12.refs_7_ = f32[16,1,128]{2,1,0:T(1,128)S(1)} collective-permute-done((f32[16,1,128]{2,1,0:T(1,128)S(1)}, f32[16,1,128]{2,1,0:T(1,128)S(1)}, u32[]{:S(2)}, u32[]{:S(2)}) %collective-permute-start.12) | collective-permute-done | bytes 8224 | tf_op jit(solution)/shard_map/ppermute | solution.py:48
  67.5 3.5 %all-to-all-done.1 = f32[32,1,128]{2,1,0:T(1,128)S(1)} async-done(((f32[32,1,128]{2,1,0:T(1,128)}), f32[32,1,128]{2,1,0:T(1,128)S(1)}, u32[]{:S(2)}, u32[]{:S(2)}) %all-to-all-start.1) | async-done | bytes 16416 | tf_op jit(solution)/shard_map/all_to_all | solution.py:380
  71.0 1.3 %copy-done.3 = f32[18,144,128]{2,1,0:T(8,128)S(1)} copy-done((f32[18,144,128]{2,1,0:T(8,128)S(1)}, f32[18,144,128]{2,1,0:T(8,128)}, u32[]{:S(2)}) %copy-start.3) | copy-done | bytes 1327128
  72.3 1.3 %copy-done.8 = f32[16,144,128]{2,1,0:T(8,128)S(1)} copy-done((f32[16,144,128]{2,1,0:T(8,128)S(1)}, f32[16,144,128]{2,1,0:T(8,128)}, u32[]{:S(2)}) %copy-start.8) | copy-done | bytes 1179672
  73.6 1.2 %copy-done.12 = f32[17,128,128]{2,1,0:T(8,128)S(1)} copy-done((f32[17,128,128]{2,1,0:T(8,128)S(1)}, f32[17,128,128]{2,1,0:T(8,128)}, u32[]{:S(2)}) %copy-start.12) | copy-done | bytes 1114136
  74.8 1.2 %copy-done.15 = f32[17,128,128]{2,1,0:T(8,128)S(1)} copy-done((f32[17,128,128]{2,1,0:T(8,128)S(1)}, f32[17,128,128]{2,1,0:T(8,128)}, u32[]{:S(2)}) %copy-start.15) | copy-done | bytes 1114136
  76.1 1.2 %copy-done.18 = f32[16,128,128]{2,1,0:T(8,128)S(1)} copy-done((f32[16,128,128]{2,1,0:T(8,128)S(1)}, f32[16,128,128]{2,1,0:T(8,128)}, u32[]{:S(2)}) %copy-start.18) | copy-done | bytes 1048600
  77.3 1.2 %copy-done.21 = f32[16,128,128]{2,1,0:T(8,128)S(1)} copy-done((f32[16,128,128]{2,1,0:T(8,128)S(1)}, f32[16,128,128]{2,1,0:T(8,128)}, u32[]{:S(2)}) %copy-start.21) | copy-done | bytes 1048600
  78.5 1.2 %copy-done.24 = f32[16,128,128]{2,1,0:T(8,128)S(1)} copy-done((f32[16,128,128]{2,1,0:T(8,128)S(1)}, f32[16,128,128]{2,1,0:T(8,128)}, u32[]{:S(2)}) %copy-start.24) | copy-done | bytes 1048600
  79.7 2.4 %shard_map.71 = (f32[18,144,128]{2,1,0:T(8,128)S(1)}, f32[17,128,128]{2,1,0:T(8,128)S(1)}, f32[32,128]{1,0:T(8,128)S(1)}) custom-call(f32[128,128]{1,0:T(8,128)S(1)} %get-tuple-element.64.refs_0_, f32[128,128]{1,0:T(8,128)S(1)} %get-tuple-element.65.refs_1_, f32[16,1,128]{2,1,0:T(1,128)S(1)} %get-tuple-element.66.refs_2_, ...), custom_call_target="tpu_custom_call" | custom-call | flops 3145728000 | bytes 1048576 | tf_op jit(solution)/shard_map/pallas_call | solution.py:368
  82.2 11.2 %all_to_all.33 = f32[32,1,128]{2,1,0:T(1,128)S(1)} all-to-all(f32[32,1,128]{2,1,0:T(1,128)S(1)} %bitcast.16), channel_id=1, replica_groups=mesh['gx'=4,'gy'=2,'gz'=4] {'gx','gy','gz'}, dimensions={0} | all-to-all | bytes 32768 | tf_op jit(solution)/shard_map/all_to_all | solution.py:380
  93.4 1.3 %shard_map.72 = (f32[16,128,128]{2,1,0:T(8,128)}, f32[3]{0:T(128)}, f32[3]{0:T(128)}) custom-call(f32[32,128]{1,0:T(8,128)S(1)} %bitcast.13, f32[32,128]{1,0:T(8,128)S(1)} %bitcast.15, f32[32,128]{1,0:T(8,128)S(1)} %bitcast.17, f32[18,144,128]{2,1,0:T(8,128)S(1)} %get-tuple-element.73.refs_3_, f32[17,128,128]{2,1,0:T(8,128)S(1)} %get-tuple-element.74.refs_4_), custom_call_target="tpu_custom_call" | custom-call | flops 3145728000 | bytes 1048576 | tf_op jit(solution)/shard_map/pallas_call | solution.py:368
  (67 shorter events, 16.2 us)
Async XLA Ops:
  4.6 10.5 %collective-permute-start.2 = (f32[2,16,1,128]{3,2,1,0:T(1,128)S(1)}, f32[2,16,1,128]{3,2,1,0:T(1,128)S(1)}, u32[]{:S(2)}, u32[]{:S(2)}) collective-permute-start(f32[2,16,1,128]{3,2,1,0:T(1,128)S(1)} %get-tuple-element.41.refs_2_), channel_id=1, source_target_pairs={{0,4},{4,0},{1,5},{5,1},{2,6},{6,2},{3,7},{7,3},{8,12},{12,8},{9,1... | collective-permute-start | bytes 49160 | tf_op jit(solution)/shard_map/ppermute | solution.py:48
  7.5 7.6 %collective-permute-start.3 = (f32[2,16,128]{2,1,0:T(8,128)S(1)}, f32[2,16,128]{2,1,0:T(8,128)S(1)}, u32[]{:S(2)}, u32[]{:S(2)}) collective-permute-start(f32[2,16,128]{2,1,0:T(8,128)S(1)} %get-tuple-element.42.refs_3_), channel_id=1, source_target_pairs={{0,1},{1,0},{2,3},{3,2},{4,5},{5,4},{6,7},{7,6},{8,9},{9,8},{10,11... | collective-permute-start | bytes 49160 | tf_op jit(solution)/shard_map/ppermute | solution.py:48
  7.5 7.6 %collective-permute-start.4 = (f32[2,16,128]{2,1,0:T(8,128)S(1)}, f32[2,16,128]{2,1,0:T(8,128)S(1)}, u32[]{:S(2)}, u32[]{:S(2)}) collective-permute-start(f32[2,16,128]{2,1,0:T(8,128)S(1)} %get-tuple-element.43.refs_4_), channel_id=1, source_target_pairs={{1,2},{2,1},{5,6},{6,5},{9,10},{10,9},{13,14},{14,13},{17,18},{18,... | collective-permute-start | bytes 49160 | tf_op jit(solution)/shard_map/ppermute | solution.py:48
  8.2 6.9 %collective-permute-start = (f32[2,128,128]{2,1,0:T(8,128)S(1)}, f32[2,128,128]{2,1,0:T(8,128)S(1)}, u32[]{:S(2)}, u32[]{:S(2)}) collective-permute-start(f32[2,128,128]{2,1,0:T(8,128)S(1)} %get-tuple-element.39.refs_0_), channel_id=1, source_target_pairs={{0,8},{8,0},{16,24},{24,16},{1,9},{9,1},{17,25},{25,17},{2,10},{10... | collective-permute-start | bytes 393224 | tf_op jit(solution)/shard_map/ppermute | solution.py:48
  9.8 5.3 %collective-permute-start.1 = (f32[2,128,128]{2,1,0:T(8,128)S(1)}, f32[2,128,128]{2,1,0:T(8,128)S(1)}, u32[]{:S(2)}, u32[]{:S(2)}) collective-permute-start(f32[2,128,128]{2,1,0:T(8,128)S(1)} %get-tuple-element.40.refs_1_), channel_id=1, source_target_pairs={{8,16},{16,8},{9,17},{17,9},{10,18},{18,10},{11,19},{19,11},{12,20... | collective-permute-start | bytes 393224 | tf_op jit(solution)/shard_map/ppermute | solution.py:48
  10.5 1.2 %copy-start.26 = (f32[16,128,128]{2,1,0:T(8,128)S(1)}, f32[16,128,128]{2,1,0:T(8,128)}, u32[]{:S(2)}) copy-start(f32[16,128,128]{2,1,0:T(8,128)} %copy-done.25) | copy-start | bytes 3145732
  11.7 1.2 %copy-start.28 = (f32[16,128,128]{2,1,0:T(8,128)S(1)}, f32[16,128,128]{2,1,0:T(8,128)}, u32[]{:S(2)}) copy-start(f32[16,128,128]{2,1,0:T(8,128)} %copy-done.27) | copy-start | bytes 3145732
  12.9 2.2 %copy-start = (f32[16,128,128]{2,1,0:T(8,128)S(1)}, f32[16,128,128]{2,1,0:T(8,128)}, u32[]{:S(2)}) copy-start(f32[16,128,128]{2,1,0:T(8,128)} %refs_19_.3) | copy-start | bytes 3145732
  12.9 2.2 %copy-start.1 = (f32[16,128,128]{2,1,0:T(8,128)S(1)}, f32[16,128,128]{2,1,0:T(8,128)}, u32[]{:S(2)}) copy-start(f32[16,128,128]{2,1,0:T(8,128)} %refs_20_.3) | copy-start | bytes 3145732
  15.1 3.8 %copy-start.16 = (f32[16,128,128]{2,1,0:T(8,128)}, f32[16,128,128]{2,1,0:T(8,128)S(1)}, u32[]{:S(2)}) copy-start(f32[16,128,128]{2,1,0:T(8,128)S(1)} %get-tuple-element.49.refs_13_.refs_16_) | copy-start | bytes 3145732
  15.1 3.8 %copy-start.19 = (f32[16,128,128]{2,1,0:T(8,128)}, f32[16,128,128]{2,1,0:T(8,128)S(1)}, u32[]{:S(2)}) copy-start(f32[16,128,128]{2,1,0:T(8,128)S(1)} %get-tuple-element.50.refs_14_.refs_17_) | copy-start | bytes 3145732
  24.0 18.1 %collective-permute-start.5 = (f32[128,128]{1,0:T(8,128)S(1)}, f32[128,128]{1,0:T(8,128)S(1)}, u32[]{:S(2)}, u32[]{:S(2)}) collective-permute-start(f32[128,128]{1,0:T(8,128)S(1)} %get-tuple-element.52.refs_0_), channel_id=1, source_target_pairs={{0,8},{8,0},{16,24},{24,16},{1,9},{9,1},{17,25},{25,17},{2,10},{10... | collective-permute-start | bytes 196616 | tf_op jit(solution)/shard_map/ppermute | solution.py:48
  28.4 13.8 %collective-permute-start.6 = (f32[128,128]{1,0:T(8,128)S(1)}, f32[128,128]{1,0:T(8,128)S(1)}, u32[]{:S(2)}, u32[]{:S(2)}) collective-permute-start(f32[128,128]{1,0:T(8,128)S(1)} %get-tuple-element.53.refs_1_), channel_id=1, source_target_pairs={{8,16},{16,8},{9,17},{17,9},{10,18},{18,10},{11,19},{19,11},{12,20... | collective-permute-start | bytes 196616 | tf_op jit(solution)/shard_map/ppermute | solution.py:48
  29.1 13.1 %all-to-all-start = ((f32[32,1,128]{2,1,0:T(1,128)}), f32[32,1,128]{2,1,0:T(1,128)S(1)}, u32[]{:S(2)}, u32[]{:S(2)}) async-start(f32[32,1,128]{2,1,0:T(1,128)} %bitcast.1), calls=%async_computation | async-start | bytes 32768 | tf_op jit(solution)/shard_map/all_to_all | solution.py:380
  35.0 3.7 %collective-permute-start.7 = (f32[16,1,128]{2,1,0:T(1,128)S(1)}, f32[16,1,128]{2,1,0:T(1,128)S(1)}, u32[]{:S(2)}, u32[]{:S(2)}) collective-permute-start(f32[16,1,128]{2,1,0:T(1,128)S(1)} %get-tuple-element.54.refs_2_), channel_id=1, source_target_pairs={{0,4},{4,0},{1,5},{5,1},{2,6},{6,2},{3,7},{7,3},{8,12},{12,8},{9,1... | collective-permute-start | bytes 24584 | tf_op jit(solution)/shard_map/ppermute | solution.py:48
  36.8 1.9 %collective-permute-start.8 = (f32[16,128]{1,0:T(8,128)S(1)}, f32[16,128]{1,0:T(8,128)S(1)}, u32[]{:S(2)}, u32[]{:S(2)}) collective-permute-start(f32[16,128]{1,0:T(8,128)S(1)} %get-tuple-element.55.refs_3_), channel_id=1, source_target_pairs={{0,1},{1,0},{2,3},{3,2},{4,5},{5,4},{6,7},{7,6},{8,9},{9,8},{10,11... | collective-permute-start | bytes 24584 | tf_op jit(solution)/shard_map/ppermute | solution.py:48
  36.8 1.9 %collective-permute-start.9 = (f32[16,128]{1,0:T(8,128)S(1)}, f32[16,128]{1,0:T(8,128)S(1)}, u32[]{:S(2)}, u32[]{:S(2)}) collective-permute-start(f32[16,128]{1,0:T(8,128)S(1)} %get-tuple-element.56.refs_4_), channel_id=1, source_target_pairs={{1,2},{2,1},{5,6},{6,5},{9,10},{10,9},{13,14},{14,13},{17,18},{18,... | collective-permute-start | bytes 24584 | tf_op jit(solution)/shard_map/ppermute | solution.py:48
  42.2 1.3 %copy-start.5 = (f32[18,144,128]{2,1,0:T(8,128)S(1)}, f32[18,144,128]{2,1,0:T(8,128)}, u32[]{:S(2)}) copy-start(f32[18,144,128]{2,1,0:T(8,128)} %copy-done.4) | copy-start | bytes 3981316
  43.5 1.3 %copy-start.7 = (f32[16,144,128]{2,1,0:T(8,128)S(1)}, f32[16,144,128]{2,1,0:T(8,128)}, u32[]{:S(2)}) copy-start(f32[16,144,128]{2,1,0:T(8,128)} %copy-done.6) | copy-start | bytes 3538948
  44.8 1.2 %copy-start.10 = (f32[17,128,128]{2,1,0:T(8,128)S(1)}, f32[17,128,128]{2,1,0:T(8,128)}, u32[]{:S(2)}) copy-start(f32[17,128,128]{2,1,0:T(8,128)} %copy-done.9) | copy-start | bytes 3342340
  46.0 1.2 %copy-start.14 = (f32[17,128,128]{2,1,0:T(8,128)S(1)}, f32[17,128,128]{2,1,0:T(8,128)}, u32[]{:S(2)}) copy-start(f32[17,128,128]{2,1,0:T(8,128)} %copy-done.13) | copy-start | bytes 3342340
  47.3 1.2 %copy-start.17 = (f32[16,128,128]{2,1,0:T(8,128)S(1)}, f32[16,128,128]{2,1,0:T(8,128)}, u32[]{:S(2)}) copy-start(f32[16,128,128]{2,1,0:T(8,128)} %copy-done.16) | copy-start | bytes 3145732
  56.5 14.5 %collective-permute-start.10 = (f32[128,128]{1,0:T(8,128)S(1)}, f32[128,128]{1,0:T(8,128)S(1)}, u32[]{:S(2)}, u32[]{:S(2)}) collective-permute-start(f32[128,128]{1,0:T(8,128)S(1)} %get-tuple-element.64.refs_0_), channel_id=1, source_target_pairs={{0,8},{8,0},{16,24},{24,16},{1,9},{9,1},{17,25},{25,17},{2,10},{10... | collective-permute-start | bytes 196616 | tf_op jit(solution)/shard_map/ppermute | solution.py:48
  57.1 13.9 %collective-permute-start.11 = (f32[128,128]{1,0:T(8,128)S(1)}, f32[128,128]{1,0:T(8,128)S(1)}, u32[]{:S(2)}, u32[]{:S(2)}) collective-permute-start(f32[128,128]{1,0:T(8,128)S(1)} %get-tuple-element.65.refs_1_), channel_id=1, source_target_pairs={{8,16},{16,8},{9,17},{17,9},{10,18},{18,10},{11,19},{19,11},{12,20... | collective-permute-start | bytes 196616 | tf_op jit(solution)/shard_map/ppermute | solution.py:48
  57.7 13.2 %all-to-all-start.1 = ((f32[32,1,128]{2,1,0:T(1,128)}), f32[32,1,128]{2,1,0:T(1,128)S(1)}, u32[]{:S(2)}, u32[]{:S(2)}) async-start(f32[32,1,128]{2,1,0:T(1,128)} %bitcast.4), calls=%async_computation.1 | async-start | bytes 32768 | tf_op jit(solution)/shard_map/all_to_all | solution.py:380
  63.8 3.7 %collective-permute-start.12 = (f32[16,1,128]{2,1,0:T(1,128)S(1)}, f32[16,1,128]{2,1,0:T(1,128)S(1)}, u32[]{:S(2)}, u32[]{:S(2)}) collective-permute-start(f32[16,1,128]{2,1,0:T(1,128)S(1)} %get-tuple-element.66.refs_2_), channel_id=1, source_target_pairs={{0,4},{4,0},{1,5},{5,1},{2,6},{6,2},{3,7},{7,3},{8,12},{12,8},{9,1... | collective-permute-start | bytes 24584 | tf_op jit(solution)/shard_map/ppermute | solution.py:48
  65.6 1.9 %collective-permute-start.13 = (f32[16,128]{1,0:T(8,128)S(1)}, f32[16,128]{1,0:T(8,128)S(1)}, u32[]{:S(2)}, u32[]{:S(2)}) collective-permute-start(f32[16,128]{1,0:T(8,128)S(1)} %get-tuple-element.67.refs_3_), channel_id=1, source_target_pairs={{0,1},{1,0},{2,3},{3,2},{4,5},{5,4},{6,7},{7,6},{8,9},{9,8},{10,11... | collective-permute-start | bytes 24584 | tf_op jit(solution)/shard_map/ppermute | solution.py:48
  65.6 1.9 %collective-permute-start.14 = (f32[16,128]{1,0:T(8,128)S(1)}, f32[16,128]{1,0:T(8,128)S(1)}, u32[]{:S(2)}, u32[]{:S(2)}) collective-permute-start(f32[16,128]{1,0:T(8,128)S(1)} %get-tuple-element.68.refs_4_), channel_id=1, source_target_pairs={{1,2},{2,1},{5,6},{6,5},{9,10},{10,9},{13,14},{14,13},{17,18},{18,... | collective-permute-start | bytes 24584 | tf_op jit(solution)/shard_map/ppermute | solution.py:48
  71.0 1.3 %copy-start.3 = (f32[18,144,128]{2,1,0:T(8,128)S(1)}, f32[18,144,128]{2,1,0:T(8,128)}, u32[]{:S(2)}) copy-start(f32[18,144,128]{2,1,0:T(8,128)} %copy-done.2) | copy-start | bytes 3981316
  72.3 1.3 %copy-start.8 = (f32[16,144,128]{2,1,0:T(8,128)S(1)}, f32[16,144,128]{2,1,0:T(8,128)}, u32[]{:S(2)}) copy-start(f32[16,144,128]{2,1,0:T(8,128)} %copy-done.6) | copy-start | bytes 3538948
  73.6 1.2 %copy-start.12 = (f32[17,128,128]{2,1,0:T(8,128)S(1)}, f32[17,128,128]{2,1,0:T(8,128)}, u32[]{:S(2)}) copy-start(f32[17,128,128]{2,1,0:T(8,128)} %copy-done.11) | copy-start | bytes 3342340
  74.8 1.2 %copy-start.15 = (f32[17,128,128]{2,1,0:T(8,128)S(1)}, f32[17,128,128]{2,1,0:T(8,128)}, u32[]{:S(2)}) copy-start(f32[17,128,128]{2,1,0:T(8,128)} %copy-done.13) | copy-start | bytes 3342340
  (14 other events, 15.3 us)
